TPU v7x, 256 devices: a whole 4x4x8 slice. The times are simulated.
256 devices in a mesh: hi: 8 (over y, core), lo: 32 (over z, x).
Axes of the slice: x: 4, y: 4, z: 8, core: 2. Of those that a mesh axis runs over, the one named last changes fastest.
Arguments:
- grm: bfloat16 [8, 32, 64, 8, 2048], P(None, 'lo', None, 'hi'), as said below
- right_sides: float32 [16384, 512], P(('hi', 'lo')), may hold values from -6 to 6
- inv_diag: float32 [16384], P(('hi', 'lo')), may hold values from 0.3 to 1
- bases: float32 [16384, 576], P(('hi', 'lo')), may hold values from -0.75 to 0.75
- couplings: float32 [9, 64, 64], replicated, as said below
- level_map: int32 [8], replicated, may hold values from 0 to 7, each once
- variance: float32 [2], replicated, may hold values from 0.3 to 1.5
- iters_per_column: int32 [512], replicated, may hold values from 1 to 3
Outputs:
- solution: float32 [16384, 512], P(('hi', 'lo'))
- residual: float32 [16384, 512], P(('hi', 'lo'))
Inputs may be any that keep to these rules, and one draw needn't show every extreme that they name: `grm`: G is symmetric and positive definite. `couplings`: each of the 9 matrices is symmetric and positive definite. `level_map`: a permutation of the levels.
All inputs are finite; a program needn't handle non-finite values.
Results may differ from a plain program's by a relative error of at most 0.0055.
Values may be sent and summed in bfloat16 or wider, within the bound.
No kernel may reach another device: no remote copies, remote signals or barrier semaphores. Data moves between devices by JAX's collectives and lax.ppermute only.
A program may use at most 64 MiB of HBM per device.

v0:
```python
import functools

import jax
import jax.numpy as jnp
from jax import lax
from jax.experimental import pallas as pl
from jax.experimental.pallas import tpu as pltpu
from jax.sharding import Mesh
from jax.sharding import PartitionSpec as P


HI = ("y", "c")
LO = ("z", "x")
HI_LO = ("y", "c", "z", "x")
COLUMNS = ("c", "z")
ROWS = ("y", "x")
BF16 = jnp.bfloat16
F32 = jnp.float32
EXACT = lax.Precision.HIGHEST
STEPS = 3
INTERPRET = False
PARTS = 1


def mm(left, right):
    return jnp.dot(left, right, precision=EXACT)


def mm3(left, right):
    return jnp.dot(left, right, precision=lax.Precision.HIGH)


def from_everyone(array, axes):
    copies = jnp.broadcast_to(array, (lax.axis_size(axes), *array.shape))
    return lax.all_to_all(copies, axes, split_axis=0, concat_axis=0, tiled=True)


def exchanged(array, axes):
    return lax.all_to_all(array, axes, split_axis=0, concat_axis=0, tiled=True)


def shifted(value, axis, step):
    size = lax.axis_size(axis)
    return lax.ppermute(value, axis, [(i, (i + step) % size) for i in range(size)])


def from_partner(value, axis, distance):
    return lax.ppermute(value, axis, [(i, i ^ distance) for i in range(lax.axis_size(axis))])


def two_terms(values):
    top = lax.reduce_precision(values, 8, 7)
    return jnp.concatenate([top, values - top], axis=0).astype(BF16)


def by_x_kernel(n_x, n_z, me_ref, grm_ref, *out_refs):
    rows = grm_ref.shape[1]
    whole = grm_ref[0]
    for x in range(n_x):
        starts = [(z * n_x + x) * rows for z in range(n_z)]
        columns = jnp.concatenate([whole[:, at : at + rows] for at in starts], axis=1)
        for step, out_ref in enumerate(out_refs):

            @pl.when(lax.rem(x - me_ref[0] + n_x, n_x) == step)
            def _():
                out_ref[0] = columns


def place_kernel(n_x, n_c, me_ref, *refs):
    arrived, (kept_ref, other_ref) = refs[:n_x], refs[n_x:]
    for step, ref in enumerate(arrived):
        x = lax.rem(me_ref[0] - step + n_x, n_x)
        for y in range(ref.shape[0] // n_c):
            kept_ref[y, x] = ref[y * n_c + me_ref[1]]
            other_ref[y, x] = ref[y * n_c + 1 - me_ref[1]]


def cut_by_x(grm):
    n_y, n_c, n_z, n_x = (lax.axis_size(name) for name in HI_LO)
    rows = grm.shape[2]
    me = lax.axis_index("x").astype(jnp.int32)[None]
    depth = n_z * rows
    return pl.pallas_call(
        functools.partial(by_x_kernel, n_x, n_z),
        grid=(n_y * n_c,),
        out_shape=[jax.ShapeDtypeStruct((n_y * n_c, rows, depth), grm.dtype)] * n_x,
        in_specs=[
            pl.BlockSpec(memory_space=pltpu.SMEM),
            pl.BlockSpec((1, rows, n_x * depth), lambda i: (i, 0, 0)),
        ],
        out_specs=[pl.BlockSpec((1, rows, depth), lambda i: (i, 0, 0))] * n_x,
        name="by_x",
        interpret=INTERPRET,
    )(me, grm.reshape(n_y * n_c, rows, n_x * depth))


def rearranged(blocks):
    n_y, n_c, _, n_x = (lax.axis_size(name) for name in HI_LO)
    _, rows, depth = blocks[0].shape
    me = jnp.stack([lax.axis_index("x"), lax.axis_index("c")]).astype(jnp.int32)
    arrived = [shifted(block, "x", k) if k else block for k, block in enumerate(blocks)]
    kept, other = kernel_call(
        functools.partial(place_kernel, n_x, n_c),
        [((n_y, n_x, rows, depth), BF16)] * 2,
        [me, *arrived],
        1,
    )
    return kept.reshape(-1, depth), shifted(other, "c", 1).reshape(-1, depth)


def times_kernel(rows, width, share, rank, me_ref, g_near_ref, g_far_ref, near_ref, far_ref, *refs):
    near_field_ref, far_field_ref, below_ref = refs[-3:]
    out_ref, own_ref = refs[-5:-3]
    step = pl.program_id(0)

    @pl.when(step == 0)
    def _():
        for half, field_ref in ((near_ref, near_field_ref), (far_ref, far_field_ref)):
            for z in range(half.shape[0]):
                field_ref[z * rows : (z + 1) * rows] = half[z, :rows, :width]

    product = jnp.dot(g_near_ref[...], near_field_ref[...], preferred_element_type=F32)
    product += jnp.dot(g_far_ref[...], far_field_ref[...], preferred_element_type=F32)
    per_step = out_ref.shape[0]
    for k in range(per_step):
        block = product[k * rows : (k + 1) * rows]
        out_ref[k, :rows] = block.astype(BF16)

        @pl.when(me_ref[0] == step * per_step + k)
        def _():
            own_ref[...] = block

    if share:

        @pl.when(step == 0)
        def _():
            t_ref, near_k_ref, far_k_ref, near_first_ref, far_first_ref = refs[:5]
            depth = near_ref.shape[0] * rows
            images = [
                half[:, :rows, half.shape[2] - rank :].reshape(depth, rank)
                for half in (near_k_ref, far_k_ref)
            ]
            firsts = [
                half[:, :rows, :width].reshape(depth, width)
                for half in (near_first_ref, far_first_ref)
            ]
            values = [t_ref[...]]
            for others in (firsts, (near_field_ref[...], far_field_ref[...])):
                total = sum(
                    lax.dot_general(
                        image, other, (((0,), (0,)), ((), ())), preferred_element_type=F32
                    )
                    for image, other in zip(images, others)
                )
                mine = jnp.zeros((share, width), F32)
                for i in range(rank // share):
                    mine = jnp.where(me_ref[1] == i, total[i * share : (i + 1) * share], mine)
                values.append(mine)
            below_ref[...] = jnp.concatenate(in_two(jnp.concatenate(values, axis=0)), axis=0)

        for k in range(per_step):
            out_ref[k, rows:] = below_ref[...]
    elif out_ref.shape[1] > rows:
        for k in range(per_step):
            out_ref[k, rows:] = refs[0][k]


def in_two(values):
    top = values.astype(BF16)
    return top, (values - top.astype(F32)).astype(BF16)


def send_coefficients(field, basis_ref, sent_refs):
    top, rest = in_two(field)
    terms = jnp.concatenate([top, rest, top], axis=0)
    coefficients = jnp.dot(basis_ref[...], terms, preferred_element_type=F32).astype(BF16)
    rank = sent_refs[0].shape[0]
    for bit, ref in enumerate(sent_refs):
        ref[...] = coefficients[bit * rank : (bit + 1) * rank]


def coefficients_kernel(field_ref, basis_ref, *sent_refs):
    send_coefficients(field_ref[...], basis_ref, sent_refs)


def image_kernel(me_ref, variance_ref, arrived_ref, own_ref, field_ref, *refs):
    rows = own_ref.shape[0]

    def add(d, total):
        part = arrived_ref[d, :rows].astype(F32)
        return total + jnp.where(me_ref[0] == d, jnp.zeros_like(part), part)

    total = lax.fori_loop(0, arrived_ref.shape[0], add, own_ref[...])
    image = variance_ref[0] * total + variance_ref[1] * field_ref[...]
    if len(refs) == 1:
        refs[0][...] = image
    else:
        refs[1][...] = image
        send_coefficients(image, refs[0], refs[2:])


def lift_kernel(levels, cuts, inside, field_ref, own_ref, lift_ref, *refs):
    outs = refs[-2 * len(cuts) :]
    arrived, extra = refs[:levels], refs[levels : -2 * len(cuts)]
    rank = arrived[0].shape[0]
    rows = field_ref.shape[0]
    terms = sum(
        jnp.dot(
            lift_ref[:, bit * rank : (bit + 1) * rank],
            arrived[bit][...],
            preferred_element_type=F32,
        )
        for bit in range(levels)
    )
    field = jnp.dot(own_ref[...], field_ref[...], precision=EXACT, preferred_element_type=F32)
    field = field + (terms[:rows] + terms[rows:])
    beside = [ref for ref in extra if ref.shape[0] == rows]
    below = [ref for ref in extra if ref.shape[0] != rows]
    for k, (start, stop) in enumerate(cuts):
        out_ref, sent_ref = outs[2 * k : 2 * k + 2]
        part = field[:, start:stop]
        whole = part
        if beside and k == 0:
            whole = jnp.concatenate([part, beside[0][...]], axis=1)
        out_ref[...] = whole if inside else part
        whole = whole.astype(BF16)
        for copy in range(sent_ref.shape[0]):
            sent_ref[copy, :rows] = whole
            for ref in below:
                sent_ref[copy, rows:] = ref[...]


def kernel_call(kernel, shapes, operands, scalars=0, scratch=()):
    in_smem = [pl.BlockSpec(memory_space=pltpu.SMEM)] * scalars
    in_vmem = [pl.BlockSpec(memory_space=pltpu.VMEM)] * (len(operands) - scalars)
    return pl.pallas_call(
        kernel,
        out_shape=[jax.ShapeDtypeStruct(shape, dtype) for shape, dtype in shapes],
        in_specs=in_smem + in_vmem,
        out_specs=[pl.BlockSpec(memory_space=pltpu.VMEM)] * len(shapes),
        scratch_shapes=[pltpu.VMEM(shape, dtype) for shape, dtype in scratch],
        interpret=INTERPRET,
    )(*operands)


def local(grm, right_sides, inv_diag, bases, couplings, level_map, variance, iters_per_column):
    rows, rhs = right_sides.shape
    levels = couplings.shape[0] - 1
    rank = couplings.shape[1]
    split_at = levels * rank
    n_rows, n_columns = lax.axis_size(ROWS), lax.axis_size(COLUMNS)
    me_rows, me_columns = lax.axis_index(ROWS), lax.axis_index(COLUMNS)

    old = lax.broadcasted_iota(jnp.int32, (split_at, split_at), 0)
    new = jnp.repeat(level_map, rank) * rank + jnp.arange(split_at, dtype=jnp.int32) % rank
    shuffle = (old == new[None, :]).astype(F32)
    by_bit = mm3(bases[:, :split_at], shuffle)
    coarse_basis = bases[:, split_at:]

    scale = 1.0 / (n_rows * n_columns * jnp.max(jnp.abs(couplings)))
    couplings = couplings * scale
    diag = (inv_diag * scale)[:, None]
    coarse_coupling = couplings[levels]
    column = lax.broadcasted_iota(jnp.int32, (split_at, split_at), 1)
    repeat = (
        lax.broadcasted_iota(jnp.int32, (rank, split_at), 0)
        == lax.broadcasted_iota(jnp.int32, (rank, split_at), 1) % rank
    )
    tiled = mm3(couplings[:levels].reshape(split_at, rank), repeat.astype(F32))
    old_rows = lax.broadcasted_iota(jnp.int32, (split_at, split_at), 0)
    diagonal_blocks = jnp.where(old_rows // rank == column // rank, tiled, 0.0)
    lift = mm3(mm3(bases[:, :split_at], diagonal_blocks), shuffle)
    lift_terms = two_terms(lift)
    eye = lax.broadcasted_iota(jnp.int32, (rows, rows), 0) == jnp.arange(rows)[None]
    own_lift = mm3(lift, by_bit.T) + jnp.where(eye, diag, 0.0)
    basis_top, basis_rest = jnp.split(two_terms(by_bit.T), 2, axis=0)
    basis_terms = jnp.concatenate([basis_top, basis_top, basis_rest], axis=1)

    def coefficient_shapes(columns):
        return [((rank, columns), BF16)] * levels

    def precondition(field, sent, cuts=None, inside=False, beside=None, below=None):
        far = [("x", 1), ("x", 2), ("z", 1), ("z", 2), ("z", 4), ("c", 1), ("y", 1), ("y", 2)]
        order = [5, 0, 6, 2, 1, 7, 3, 4]
        arrived = {bit: from_partner(sent[bit], *far[bit]) for bit in order}
        extra = [array for array in (beside, below) if array is not None]
        more_rows = 0 if below is None else below.shape[0]
        cuts = cuts or [(0, field.shape[1])]
        shapes = []
        for k, (start, stop) in enumerate(cuts):
            more = beside.shape[1] if beside is not None and k == 0 else 0
            shapes.append(((rows, stop - start + (more if inside else 0)), F32))
            copies = (lax.axis_size("z"), rows + more_rows, stop - start + more)
            shapes.append((copies, BF16))
        return kernel_call(
            functools.partial(lift_kernel, levels, cuts, inside),
            shapes,
            [field, own_lift, lift_terms, *[arrived[bit] for bit in range(levels)], *extra],
        )

    places = jnp.stack([me_rows, me_columns]).astype(jnp.int32)
    right_sides, *blocks = lax.optimization_barrier((right_sides, *cut_by_x(grm)))
    sent = kernel_call(coefficients_kernel, coefficient_shapes(rhs), [right_sides, basis_terms])
    g_blocks = rearranged(blocks)

    def gathered(copies):
        near = exchanged(copies, "z")
        return near, shifted(near, "c", 1)

    def products(everyone, width, riders=(), more_rows=0, share=0):
        depth = lax.axis_size("z") * rows
        per_step = n_rows // 4
        height = rows + more_rows

        def whole(array):
            return pl.BlockSpec(array.shape, lambda i: (0,) * array.ndim)

        def some(shape):
            return pl.BlockSpec(shape, lambda i: (i,) + (0,) * (len(shape) - 1))

        rider_specs = [whole(array) for array in riders]
        if riders and not share:
            rider_specs = [some((per_step, *riders[0].shape[1:]))]
        partial, own = pl.pallas_call(
            functools.partial(times_kernel, rows, width, share, rank),
            grid=(4,),
            out_shape=[
                jax.ShapeDtypeStruct((n_rows, height, width), BF16),
                jax.ShapeDtypeStruct((rows, width), F32),
            ],
            in_specs=[
                pl.BlockSpec(memory_space=pltpu.SMEM),
                *[some((per_step * rows, depth))] * 2,
                *[whole(array) for array in everyone],
                *rider_specs,
            ],
            out_specs=[some((per_step, height, width)), pl.BlockSpec((rows, width), lambda i: (0, 0))],
            scratch_shapes=[
                *[pltpu.VMEM((depth, width), BF16)] * 2,
                pltpu.VMEM((more_rows or 8, width), BF16),
            ],
            name="times",
            interpret=INTERPRET,
        )(places, *g_blocks, *everyone, *riders)
        return exchanged(partial, ROWS), own

    def image_of(arrived, own, field, send=True):
        width = field.shape[1]
        shapes = [((rows, width), F32)] + (coefficient_shapes(width) if send else [])
        operands = [places, variance, arrived, own, field] + ([basis_terms] if send else [])
        image, *sent = kernel_call(image_kernel, shapes, operands, 2)
        return image, sent

    def sum_of_terms(terms, axis):
        top, rest = jnp.split(terms.astype(F32), 2, axis=axis)
        return top + rest

    half = rhs // PARTS
    cuts = [(k * half, (k + 1) * half) for k in range(PARTS)]
    widths = [half + (0 if k else rank) for k in range(PARTS)]
    parts = range(len(cuts))

    def padded(array, width):
        more = width - array.shape[-1]
        return jnp.pad(array, [(0, 0)] * (array.ndim - 1) + [(0, more)])

    share = rank // n_columns
    t_share = rank // n_rows
    t_parts = mm3(coarse_basis.T, right_sides).reshape(n_rows, t_share, rhs)
    t_top = lax.reduce_precision(t_parts, 8, 7)
    t_parts = jnp.concatenate([t_top, t_parts - t_top], axis=1).astype(BF16)
    t_parts = [padded(t_parts[:, :, slice(*cuts[k])], widths[k]) for k in parts]

    first = precondition(right_sides, sent, cuts, True, beside=coarse_basis)
    first, copies = first[::2], first[1::2]
    all_first = [gathered(copies[k]) for k in parts]
    sums = [products(all_first[k], widths[k], [t_parts[k]], 2 * t_share) for k in parts]
    first_image, sent = zip(*[image_of(*sums[k], first[k]) for k in parts])
    coarse_image = first_image[0][:, half:]

    second, all_second, t_rows = [], [], []
    for k in parts:
        rows_of_t = sum_of_terms(sums[k][0][:, rows:], 1).sum(axis=0)
        field, copies = precondition(
            first_image[k],
            sent[k],
            beside=None if k else coarse_image,
            below=two_terms(padded(rows_of_t, widths[k] + (0 if k else rank))),
        )
        second.append(field)
        all_second.append(gathered(copies))
        near, far = all_second[k]
        rode = near[:, rows:, : widths[k]].astype(F32) + far[:, rows:, : widths[k]].astype(F32)
        t_rows.append(sum_of_terms(rode, 1).sum(axis=0))
    sums = [
        products(
            all_second[k], widths[k], [t_rows[k], *all_second[0], *all_first[k]], 6 * share, share
        )
        for k in parts
    ]
    second_image, sent = zip(*[image_of(*sums[k], second[k]) for k in parts])

    t0, third, third_image, tables = [], [], [], []
    for k in parts:
        rode = sum_of_terms(sums[k][0][:, rows:], 1)
        t0.append(rode[:, :t_share].reshape(rank, widths[k])[:, :half])
        field, copies = precondition(
            second_image[k], sent[k], below=two_terms(rode[:, t_share:].sum(axis=0))
        )
        third.append(field)
        everyone = gathered(copies)
        arrived, own = products(everyone, widths[k])
        own, *everyone = lax.optimization_barrier((own, *everyone))
        third_image.append(image_of(arrived, own, field, send=False)[0])
        table = sum_of_terms(jnp.stack([array[:, rows:] for array in everyone]), 2)
        table = jnp.where(lax.axis_index("c") == 0, table, table[::-1])
        table = table.reshape(n_columns, 2, share, widths[k]).transpose(1, 0, 2, 3)
        tables.append(table.reshape(2, rank, widths[k]))

    def joined(fields):
        if PARTS == 1:
            return fields[0]
        return jnp.concatenate([fields[0][:, :half], *fields[1:], fields[0][:, half:]], axis=1)

    first, second, third = joined(first), joined(second), joined(third)
    first_image, second_image = joined(first_image), joined(second_image)
    third_image = joined(third_image)
    t0 = jnp.concatenate(t0, axis=1)
    k_first, k_second = (joined([table[i] for table in tables]) for i in range(2))

    k_basis = k_first[:, rhs:]
    s0 = mm(coarse_coupling, t0[:, :rhs])
    s1 = mm(coarse_coupling, k_first[:, :rhs] + mm(k_basis, s0))
    s2 = mm(coarse_coupling, k_second[:, :rhs] + mm(k_second[:, rhs:], s0) + mm(k_basis, s1))
    weights = jnp.concatenate([s0, s1, s2], axis=0)

    none = jnp.zeros_like(coarse_basis)
    coarse_parts = jnp.concatenate(
        [
            jnp.concatenate([coarse_basis, none, none], axis=1),
            jnp.concatenate([second[:, rhs:], coarse_basis, none], axis=1),
            jnp.concatenate([third[:, rhs:], second[:, rhs:], coarse_basis], axis=1),
            jnp.concatenate([coarse_image, none, none], axis=1),
            jnp.concatenate([second_image[:, rhs:], coarse_image, none], axis=1),
        ],
        axis=0,
    )
    coarse_parts = mm3(coarse_parts, weights).reshape(5, rows, rhs)
    v = [field[:, :rhs] + coarse_parts[k] for k, field in enumerate([first, second, third])]
    w = [right_sides]
    w += [field[:, :rhs] + coarse_parts[3 + k] for k, field in enumerate([first_image, second_image])]
    last_parts = [third_image[:, rhs:], second_image[:, rhs:], coarse_image]
    w.append(third_image[:, :rhs] + mm3(jnp.concatenate(last_parts, axis=1), weights))

    moments = jnp.stack([jnp.sum(w[k - k // 2] * v[k // 2], axis=0) for k in range(2 * STEPS)])
    moments = from_everyone(moments, ROWS).sum(axis=0)
    moments = from_everyone(moments, COLUMNS).sum(axis=0)

    m = [moments[k] for k in range(2 * STEPS)]
    one, zero = jnp.ones_like(m[0]), jnp.zeros_like(m[0])
    in_r, kept_r, kept_x, direction, energy = [one], [one], [], [], None
    for step in range(STEPS):
        basis = range(step + 1)
        fresh = sum(in_r[p] * in_r[q] * m[p + q] for p in basis for q in basis)
        before = [fresh / energy * d for d in direction] if step else []
        direction = [r + d for r, d in zip(in_r, before + [zero])]
        energy = fresh
        alpha = energy / sum(direction[p] * direction[q] * m[p + q + 1] for p in basis for q in basis)
        in_r = [a - b for a, b in zip(in_r + [zero], [zero] + [alpha * d for d in direction])]
        active = step < iters_per_column
        kept_r = [jnp.where(active, a, b) for a, b in zip(in_r, kept_r + [zero])]
        kept_x = [jnp.where(active, b + alpha * d, b) for d, b in zip(direction, kept_x + [zero])]

    solution = sum(c * field for c, field in zip(kept_x, v))
    residual = w[0] + sum(c * field for c, field in zip(kept_r[1:], w[1:]))
    return (solution, residual)


def solution(mesh):
    split = Mesh(mesh.devices.reshape(4, 2, 8, 4), HI_LO)
    return jax.shard_map(
        local,
        mesh=split,
        in_specs=(
            P(None, LO, None, HI, None),
            P(HI_LO, None),
            P(HI_LO),
            P(HI_LO, None),
            P(),
            P(),
            P(),
            P(),
        ),
        out_specs=(P(HI_LO, None), P(HI_LO, None)),
        check_vma=False,
    )
```

profile of v0, /device:TPU:1, one launch (start us, length us, event | category | flops | bytes accessed | tf_op | source)
XLA Modules:
  0.0 322.5 jit_solution(8700473003303353411)
XLA Ops:
  0.7 7.2 %by_x.1 = (bf16[8,64,512]{2,1,0:T(8,128)(2,1)}, bf16[8,64,512]{2,1,0:T(8,128)(2,1)}, bf16[8,64,512]{2,1,0:T(8,128)(2,1)}, bf16[8,64,512]{2,1,0:T(8,128)(2,1)}) custom-call(s32[1]{0:T(128)} %bitcast.me_ref, bf16[8,64,2048]{2,1,0:T(8,128)(2,1)} %bitcast.56), custom_call_target="tpu_custom_call" | custom-call | tf_op jit(solution)/shard_map/by_x/pallas_call | solution.py:83
  9.6 2.0 shard_map.95
  11.6 2.1 collective-permute-start
  13.7 2.4 collective-permute-start.1
  16.1 1.6 collective-permute-start.2
  17.7 3.0 collective-permute-start.3
  20.7 4.2 %collective-permute-start.4 = (bf16[64,512]{1,0:T(8,128)(2,1)}, bf16[64,512]{1,0:T(8,128)(2,1)S(1)}, u32[]{:S(2)}, u32[]{:S(2)}) collective-permute-start(bf16[64,512]{1,0:T(8,128)(2,1)} %get-tuple-element.63), channel_id=1, source_target_pairs={{0,16},{4,20},{8,24},{12,28},{16,0},{20,4},{24,8},{28,12},{1,17},{... | collective-permute-start | bytes 196616 | tf_op jit(solution)/shard_map/ppermute | solution.py:48
  29.2 2.2 collective-permute-start.5
  31.4 1.4 collective-permute-start.6
  32.8 2.7 collective-permute-start.7
  36.2 2.7 collective-permute-done.7.refs_7_
  39.6 2.7 shard_map.96
  42.3 3.7 %all-to-all-start = ((bf16[8,64,576]{2,1,0:T(8,128)(2,1)}), bf16[8,64,576]{2,1,0:T(8,128)(2,1)S(1)}, u32[]{:S(2)}, u32[]{:S(2)}) async-start(bf16[8,64,576]{2,1,0:T(8,128)(2,1)} %get-tuple-element.74), calls=%async_computation | async-start | bytes 1310720 | tf_op jit(solution)/shard_map/all_to_all | solution.py:39
  48.7 10.2 %collective-permute-done.10.refs_3_ = bf16[8,64,512]{2,1,0:T(8,128)(2,1)S(1)} collective-permute-done((bf16[8,64,512]{2,1,0:T(8,128)(2,1)}, bf16[8,64,512]{2,1,0:T(8,128)(2,1)S(1)}, u32[]{:S(2)}, u32[]{:S(2)}) %collective-permute-start.10) | collective-permute-done | bytes 524320 | tf_op jit(solution)/shard_map/ppermute | solution.py:44
  58.9 1.9 collective-permute-done.8.refs_1_
  60.7 9.7 %collective-permute-done.9.refs_2_ = bf16[8,64,512]{2,1,0:T(8,128)(2,1)S(1)} collective-permute-done((bf16[8,64,512]{2,1,0:T(8,128)(2,1)}, bf16[8,64,512]{2,1,0:T(8,128)(2,1)S(1)}, u32[]{:S(2)}, u32[]{:S(2)}) %collective-permute-start.9) | collective-permute-done | bytes 524320 | tf_op jit(solution)/shard_map/ppermute | solution.py:44
  71.2 3.0 shard_map.97
  74.3 3.6 %collective-permute-start.11 = (bf16[4,4,64,512]{3,2,1,0:T(8,128)(2,1)}, bf16[4,4,64,512]{3,2,1,0:T(8,128)(2,1)S(1)}, u32[]{:S(2)}, u32[]{:S(2)}) collective-permute-start(bf16[4,4,64,512]{3,2,1,0:T(8,128)(2,1)} %get-tuple-element.73), channel_id=1, source_target_pairs={{0,32},{32,0},{1,33},{33,1},{2,34},{34,2},{3,35},{35,3},{4,36},{36... | collective-permute-start | bytes 3145736 | tf_op jit(solution)/shard_map/ppermute | solution.py:44
  82.1 5.6 %times.3 = (bf16[16,72,576]{2,1,0:T(8,128)(2,1)}, f32[64,576]{1,0:T(8,128)}) custom-call(s32[2]{0:T(128)} %pad_add_fusion.me_ref, bf16[1024,512]{1,0:T(8,128)(2,1)} %bitcast.50, bf16[1024,512]{1,0:T(8,128)(2,1)} %bitcast.53, bf16[8,64,576]{2,1,0:T(8,128)(2,1)} %copy-done.4, bf16[8,64,576]{2,1,0:T(8,128)(2,1)} %copy-done.9, bf16[16,8,576]{2,1,0:T(8,128)(2,1)} %fusion.8.refs_0_), custom_call_target="tpu_custom_call" | custom-call | tf_op jit(solution)/shard_map/times/pallas_call | solution.py:324
  87.7 24.8 %all_to_all.40.arrived_ref = bf16[16,72,576]{2,1,0:T(8,128)(2,1)S(1)} all-to-all(bf16[16,72,576]{2,1,0:T(8,128)(2,1)} %get-tuple-element.75), channel_id=1, replica_groups=mesh['y'=4,'c'=2,'z'=8,'x'=4] {'y','x'}, dimensions={0} | all-to-all | bytes 2654208 | tf_op jit(solution)/shard_map/all_to_all | solution.py:39
  113.7 3.1 shard_map.98
  119.6 2.1 collective-permute-start.16
  121.7 2.4 collective-permute-start.17
  124.1 1.4 slice.137.refs_8_
  125.5 2.9 collective-permute-start.18
  128.8 1.8 collective-permute-start.20
  132.5 2.5 collective-permute-done.20.refs_7_
  135.6 2.9 shard_map.99
  138.6 24.5 %all_to_all.41.near_ref.refs_1_ = bf16[8,72,640]{2,1,0:T(8,128)(2,1)S(1)} all-to-all(bf16[8,72,640]{2,1,0:T(8,128)(2,1)} %get-tuple-element.87), channel_id=1, replica_groups=mesh['y'=4,'c'=2,'z'=8,'x'=4] {'z'}, dimensions={0} | all-to-all | bytes 1474560 | tf_op jit(solution)/shard_map/all_to_all | solution.py:39
  163.1 2.7 collective-permute-start.21
  165.8 1.8 collective-permute-done.21.far_ref.refs_2_
  168.5 7.3 %times.4 = (bf16[16,88,576]{2,1,0:T(8,128)(2,1)}, f32[64,576]{1,0:T(8,128)}) custom-call(s32[2]{0:T(128)} %pad_add_fusion.me_ref, bf16[1024,512]{1,0:T(8,128)(2,1)} %bitcast.51, bf16[1024,512]{1,0:T(8,128)(2,1)} %bitcast.54, bf16[8,72,640]{2,1,0:T(8,128)(2,1)} %copy-done.2, bf16[8,72,640]{2,1,0:T(8,128)(2,1)} %copy-done.7, f32[4,576]{1,0:T(4,128)} %fusion.17.refs_0_, ...), custom_call_target="tpu_custom_call" | custom-call | tf_op jit(solution)/shard_map/times/pallas_call | solution.py:324
  175.9 30.0 %all_to_all.42.arrived_ref = bf16[16,88,576]{2,1,0:T(8,128)(2,1)S(1)} all-to-all(bf16[16,88,576]{2,1,0:T(8,128)(2,1)} %get-tuple-element.88), channel_id=1, replica_groups=mesh['y'=4,'c'=2,'z'=8,'x'=4] {'y','x'}, dimensions={0} | all-to-all | bytes 3244032 | tf_op jit(solution)/shard_map/all_to_all | solution.py:39
  207.2 3.2 %shard_map.100 = (f32[64,576]{1,0:T(8,128)}, bf16[64,576]{1,0:T(8,128)(2,1)}, bf16[64,576]{1,0:T(8,128)(2,1)}, bf16[64,576]{1,0:T(8,128)(2,1)}, bf16[64,576]{1,0...) custom-call(s32[2]{0:T(128)} %pad_add_fusion.me_ref, ...), custom_call_target="tpu_custom_call" | custom-call | tf_op jit(solution)/shard_map/pallas_call | solution.py:236
  212.3 1.8 collective-permute-start.26
  214.1 2.8 collective-permute-start.27
  217.2 1.8 collective-permute-start.29
  220.8 1.9 collective-permute-done.29.refs_7_
  223.3 3.0 shard_map.101
  226.3 28.0 %all_to_all.43.near_ref = bf16[8,80,576]{2,1,0:T(8,128)(2,1)S(1)} all-to-all(bf16[8,80,576]{2,1,0:T(8,128)(2,1)} %get-tuple-element.100), channel_id=1, replica_groups=mesh['y'=4,'c'=2,'z'=8,'x'=4] {'z'}, dimensions={0} | all-to-all | bytes 1474560 | tf_op jit(solution)/shard_map/all_to_all | solution.py:39
  254.3 2.9 collective-permute-start.30
  259.3 5.6 %times.5 = (bf16[16,64,576]{2,1,0:T(8,128)(2,1)}, f32[64,576]{1,0:T(8,128)}) custom-call(s32[2]{0:T(128)} %pad_add_fusion.me_ref, bf16[1024,512]{1,0:T(8,128)(2,1)} %bitcast.52, bf16[1024,512]{1,0:T(8,128)(2,1)} %bitcast.55, bf16[8,80,576]{2,1,0:T(8,128)(2,1)} %copy-done.6, bf16[8,80,576]{2,1,0:T(8,128)(2,1)} %collective-permute-done.30.far_ref), custom_call_target="tpu_custom_call" | custom-call | tf_op jit(solution)/shard_map/times/pallas_call | solution.py:324
  264.9 5.2 %all-to-all-start.5 = ((bf16[16,64,576]{2,1,0:T(8,128)(2,1)}), bf16[16,64,576]{2,1,0:T(8,128)(2,1)S(1)}, u32[]{:S(2)}, u32[]{:S(2)}) async-start(bf16[16,64,576]{2,1,0:T(8,128)(2,1)} %get-tuple-element.104), calls=%async_computation.5 | async-start | bytes 2621440 | tf_op jit(solution)/shard_map/all_to_all | solution.py:39
  273.7 1.4 fusion.7
  275.1 15.0 %all-to-all-done.5.arrived_ref = bf16[16,64,576]{2,1,0:T(8,128)(2,1)S(1)} async-done(((bf16[16,64,576]{2,1,0:T(8,128)(2,1)}), bf16[16,64,576]{2,1,0:T(8,128)(2,1)S(1)}, u32[]{:S(2)}, u32[]{:S(2)}) %all-to-all-start.5) | async-done | bytes 1179680 | tf_op jit(solution)/shard_map/all_to_all | solution.py:39
  291.3 2.6 shard_map.102
  295.9 12.1 %all_to_all.44 = f32[16,6,512]{2,1,0:T(8,128)S(1)} all-to-all(f32[16,6,512]{2,1,0:T(8,128)S(1)} %broadcast_in_dim.49), channel_id=1, replica_groups=mesh['y'=4,'c'=2,'z'=8,'x'=4] {'y','x'}, dimensions={0} | all-to-all | bytes 393216 | tf_op jit(solution)/shard_map/all_to_all | solution.py:35
  308.0 13.5 %all_to_all.45 = f32[16,6,512]{2,1,0:T(8,128)S(1)} all-to-all(f32[16,6,512]{2,1,0:T(8,128)S(1)} %broadcast_in_dim.50), channel_id=1, replica_groups=mesh['y'=4,'c'=2,'z'=8,'x'=4] {'c','z'}, dimensions={0} | all-to-all | bytes 393216 | tf_op jit(solution)/shard_map/all_to_all | solution.py:35
  (221 shorter events, 37.5 us)
Async XLA Ops:
  7.8 17.1 %copy-start.14 = (f32[9,64,64]{2,1,0:T(8,128)S(1)}, f32[9,64,64]{2,1,0:T(8,128)}, u32[]{:S(2)}) copy-start(f32[9,64,64]{2,1,0:T(8,128)} %param.12) | copy-start | bytes 442372
  11.6 17.6 %collective-permute-start = (bf16[64,512]{1,0:T(8,128)(2,1)}, bf16[64,512]{1,0:T(8,128)(2,1)S(1)}, u32[]{:S(2)}, u32[]{:S(2)}) collective-permute-start(bf16[64,512]{1,0:T(8,128)(2,1)} %get-tuple-element.59), channel_id=1, source_target_pairs={{0,1},{1,0},{2,3},{3,2},{4,5},{5,4},{6,7},{7,6},{8,9},{9,8},{10,11... | collective-permute-start | bytes 196616 | tf_op jit(solution)/shard_map/ppermute | solution.py:48
  13.7 17.7 %collective-permute-start.1 = (bf16[64,512]{1,0:T(8,128)(2,1)}, bf16[64,512]{1,0:T(8,128)(2,1)S(1)}, u32[]{:S(2)}, u32[]{:S(2)}) collective-permute-start(bf16[64,512]{1,0:T(8,128)(2,1)} %get-tuple-element.60), channel_id=1, source_target_pairs={{0,2},{1,3},{2,0},{3,1},{4,6},{5,7},{6,4},{7,5},{8,10},{9,11},{10,... | collective-permute-start | bytes 196616 | tf_op jit(solution)/shard_map/ppermute | solution.py:48
  16.1 16.7 %collective-permute-start.2 = (bf16[64,512]{1,0:T(8,128)(2,1)}, bf16[64,512]{1,0:T(8,128)(2,1)S(1)}, u32[]{:S(2)}, u32[]{:S(2)}) collective-permute-start(bf16[64,512]{1,0:T(8,128)(2,1)} %get-tuple-element.61), channel_id=1, source_target_pairs={{0,4},{4,0},{8,12},{12,8},{16,20},{20,16},{24,28},{28,24},{1,5},{5... | collective-permute-start | bytes 196616 | tf_op jit(solution)/shard_map/ppermute | solution.py:48
  17.7 18.4 %collective-permute-start.3 = (bf16[64,512]{1,0:T(8,128)(2,1)}, bf16[64,512]{1,0:T(8,128)(2,1)S(1)}, u32[]{:S(2)}, u32[]{:S(2)}) collective-permute-start(bf16[64,512]{1,0:T(8,128)(2,1)} %get-tuple-element.62), channel_id=1, source_target_pairs={{0,8},{4,12},{8,0},{12,4},{16,24},{20,28},{24,16},{28,20},{1,9},{5... | collective-permute-start | bytes 196616 | tf_op jit(solution)/shard_map/ppermute | solution.py:48
  20.7 15.4 %collective-permute-start.4 = (bf16[64,512]{1,0:T(8,128)(2,1)}, bf16[64,512]{1,0:T(8,128)(2,1)S(1)}, u32[]{:S(2)}, u32[]{:S(2)}) collective-permute-start(bf16[64,512]{1,0:T(8,128)(2,1)} %get-tuple-element.63), channel_id=1, source_target_pairs={{0,16},{4,20},{8,24},{12,28},{16,0},{20,4},{24,8},{28,12},{1,17},{... | collective-permute-start | bytes 196616 | tf_op jit(solution)/shard_map/ppermute | solution.py:48
  29.2 9.7 %copy-start.39 = (bf16[64,512]{1,0:T(8,128)(2,1)}, bf16[64,512]{1,0:T(8,128)(2,1)S(1)}, u32[]{:S(2)}) copy-start(bf16[64,512]{1,0:T(8,128)(2,1)S(1)} %collective-permute-done.refs_0_) | copy-start | bytes 196612
  29.2 6.9 %collective-permute-start.5 = (bf16[64,512]{1,0:T(8,128)(2,1)S(1)}, bf16[64,512]{1,0:T(8,128)(2,1)S(1)}, u32[]{:S(2)}, u32[]{:S(2)}) collective-permute-start(bf16[64,512]{1,0:T(8,128)(2,1)S(1)} %copy-done.50), channel_id=1, source_target_pairs={{0,32},{32,0},{1,33},{33,1},{2,34},{34,2},{3,35},{35,3},{4,36},{36... | collective-permute-start | bytes 196616 | tf_op jit(solution)/shard_map/ppermute | solution.py:48
  31.4 4.8 %collective-permute-start.6 = (bf16[64,512]{1,0:T(8,128)(2,1)S(1)}, bf16[64,512]{1,0:T(8,128)(2,1)S(1)}, u32[]{:S(2)}, u32[]{:S(2)}) collective-permute-start(bf16[64,512]{1,0:T(8,128)(2,1)S(1)} %copy-done.49), channel_id=1, source_target_pairs={{0,64},{64,0},{128,192},{192,128},{1,65},{65,1},{129,193},{193,129... | collective-permute-start | bytes 196616 | tf_op jit(solution)/shard_map/ppermute | solution.py:48
  32.8 6.2 %collective-permute-start.7 = (bf16[64,512]{1,0:T(8,128)(2,1)S(1)}, bf16[64,512]{1,0:T(8,128)(2,1)S(1)}, u32[]{:S(2)}, u32[]{:S(2)}) collective-permute-start(bf16[64,512]{1,0:T(8,128)(2,1)S(1)} %copy-done.48), channel_id=1, source_target_pairs={{0,128},{64,192},{128,0},{192,64},{1,129},{65,193},{129,1},{193,65... | collective-permute-start | bytes 196616 | tf_op jit(solution)/shard_map/ppermute | solution.py:48
  42.3 35.8 %copy-start.8 = (f32[64,512]{1,0:T(8,128)S(1)}, f32[64,512]{1,0:T(8,128)}, u32[]{:S(2)}) copy-start(f32[64,512]{1,0:T(8,128)} %field_ref.1) | copy-start | bytes 393220
  42.3 35.5 %all-to-all-start = ((bf16[8,64,576]{2,1,0:T(8,128)(2,1)}), bf16[8,64,576]{2,1,0:T(8,128)(2,1)S(1)}, u32[]{:S(2)}, u32[]{:S(2)}) async-start(bf16[8,64,576]{2,1,0:T(8,128)(2,1)} %get-tuple-element.74), calls=%async_computation | async-start | bytes 1310720 | tf_op jit(solution)/shard_map/all_to_all | solution.py:39
  46.0 12.9 %collective-permute-start.10 = (bf16[8,64,512]{2,1,0:T(8,128)(2,1)}, bf16[8,64,512]{2,1,0:T(8,128)(2,1)S(1)}, u32[]{:S(2)}, u32[]{:S(2)}) collective-permute-start(bf16[8,64,512]{2,1,0:T(8,128)(2,1)} %get-tuple-element.71), channel_id=1, source_target_pairs={{0,3},{1,0},{2,1},{3,2},{4,7},{5,4},{6,5},{7,6},{8,11},{9,8},{10,9... | collective-permute-start | bytes 1572872 | tf_op jit(solution)/shard_map/ppermute | solution.py:44
  46.2 14.5 %collective-permute-start.8 = (bf16[8,64,512]{2,1,0:T(8,128)(2,1)}, bf16[8,64,512]{2,1,0:T(8,128)(2,1)S(1)}, u32[]{:S(2)}, u32[]{:S(2)}) collective-permute-start(bf16[8,64,512]{2,1,0:T(8,128)(2,1)} %get-tuple-element.69), channel_id=1, source_target_pairs={{0,1},{1,2},{2,3},{3,0},{4,5},{5,6},{6,7},{7,4},{8,9},{9,10},{10,1... | collective-permute-start | bytes 1572872 | tf_op jit(solution)/shard_map/ppermute | solution.py:44
  47.5 22.9 %collective-permute-start.9 = (bf16[8,64,512]{2,1,0:T(8,128)(2,1)}, bf16[8,64,512]{2,1,0:T(8,128)(2,1)S(1)}, u32[]{:S(2)}, u32[]{:S(2)}) collective-permute-start(bf16[8,64,512]{2,1,0:T(8,128)(2,1)} %get-tuple-element.70), channel_id=1, source_target_pairs={{0,2},{1,3},{2,0},{3,1},{4,6},{5,7},{6,4},{7,5},{8,10},{9,11},{10,... | collective-permute-start | bytes 1572872 | tf_op jit(solution)/shard_map/ppermute | solution.py:44
  58.9 11.6 %copy-start.18 = (bf16[8,64,512]{2,1,0:T(8,128)(2,1)}, bf16[8,64,512]{2,1,0:T(8,128)(2,1)S(1)}, u32[]{:S(2)}) copy-start(bf16[8,64,512]{2,1,0:T(8,128)(2,1)S(1)} %collective-permute-done.10.refs_3_) | copy-start | bytes 1572868
  60.7 9.7 %copy-start.19 = (bf16[8,64,512]{2,1,0:T(8,128)(2,1)}, bf16[8,64,512]{2,1,0:T(8,128)(2,1)S(1)}, u32[]{:S(2)}) copy-start(bf16[8,64,512]{2,1,0:T(8,128)(2,1)S(1)} %collective-permute-done.8.refs_1_) | copy-start | bytes 1572868
  74.3 6.1 %collective-permute-start.11 = (bf16[4,4,64,512]{3,2,1,0:T(8,128)(2,1)}, bf16[4,4,64,512]{3,2,1,0:T(8,128)(2,1)S(1)}, u32[]{:S(2)}, u32[]{:S(2)}) collective-permute-start(bf16[4,4,64,512]{3,2,1,0:T(8,128)(2,1)} %get-tuple-element.73), channel_id=1, source_target_pairs={{0,32},{32,0},{1,33},{33,1},{2,34},{34,2},{3,35},{35,3},{4,36},{36... | collective-permute-start | bytes 3145736 | tf_op jit(solution)/shard_map/ppermute | solution.py:44
  77.8 3.4 %collective-permute-start.12 = (bf16[8,64,576]{2,1,0:T(8,128)(2,1)S(1)}, bf16[8,64,576]{2,1,0:T(8,128)(2,1)S(1)}, u32[]{:S(2)}, u32[]{:S(2)}) collective-permute-start(bf16[8,64,576]{2,1,0:T(8,128)(2,1)S(1)} %all-to-all-done.near_ref.refs_3_), channel_id=1, source_target_pairs={{0,32},{32,0},{1,33},{33,1},{2,34},{34,2},{3,35},{35,3},{4,36},{36... | collective-permute-start | bytes 1769480 | tf_op jit(solution)/shard_map/ppermute | solution.py:44
  116.8 8.7 %collective-permute-start.13 = (bf16[64,576]{1,0:T(8,128)(2,1)}, bf16[64,576]{1,0:T(8,128)(2,1)S(1)}, u32[]{:S(2)}, u32[]{:S(2)}) collective-permute-start(bf16[64,576]{1,0:T(8,128)(2,1)} %get-tuple-element.78), channel_id=1, source_target_pairs={{0,1},{1,0},{2,3},{3,2},{4,5},{5,4},{6,7},{7,6},{8,9},{9,8},{10,11... | collective-permute-start | bytes 221192 | tf_op jit(solution)/shard_map/ppermute | solution.py:48
  117.1 11.3 %collective-permute-start.14 = (bf16[64,576]{1,0:T(8,128)(2,1)}, bf16[64,576]{1,0:T(8,128)(2,1)S(1)}, u32[]{:S(2)}, u32[]{:S(2)}) collective-permute-start(bf16[64,576]{1,0:T(8,128)(2,1)} %get-tuple-element.79), channel_id=1, source_target_pairs={{0,2},{1,3},{2,0},{3,1},{4,6},{5,7},{6,4},{7,5},{8,10},{9,11},{10,... | collective-permute-start | bytes 221192 | tf_op jit(solution)/shard_map/ppermute | solution.py:48
  118.3 10.4 %collective-permute-start.15 = (bf16[64,576]{1,0:T(8,128)(2,1)}, bf16[64,576]{1,0:T(8,128)(2,1)S(1)}, u32[]{:S(2)}, u32[]{:S(2)}) collective-permute-start(bf16[64,576]{1,0:T(8,128)(2,1)} %get-tuple-element.80), channel_id=1, source_target_pairs={{0,4},{4,0},{8,12},{12,8},{16,20},{20,16},{24,28},{28,24},{1,5},{5... | collective-permute-start | bytes 221192 | tf_op jit(solution)/shard_map/ppermute | solution.py:48
  119.6 11.6 %collective-permute-start.16 = (bf16[64,576]{1,0:T(8,128)(2,1)}, bf16[64,576]{1,0:T(8,128)(2,1)S(1)}, u32[]{:S(2)}, u32[]{:S(2)}) collective-permute-start(bf16[64,576]{1,0:T(8,128)(2,1)} %get-tuple-element.81), channel_id=1, source_target_pairs={{0,8},{4,12},{8,0},{12,4},{16,24},{20,28},{24,16},{28,20},{1,9},{5... | collective-permute-start | bytes 221192 | tf_op jit(solution)/shard_map/ppermute | solution.py:48
  121.7 9.5 %collective-permute-start.17 = (bf16[64,576]{1,0:T(8,128)(2,1)}, bf16[64,576]{1,0:T(8,128)(2,1)S(1)}, u32[]{:S(2)}, u32[]{:S(2)}) collective-permute-start(bf16[64,576]{1,0:T(8,128)(2,1)} %get-tuple-element.82), channel_id=1, source_target_pairs={{0,16},{4,20},{8,24},{12,28},{16,0},{20,4},{24,8},{28,12},{1,17},{... | collective-permute-start | bytes 221192 | tf_op jit(solution)/shard_map/ppermute | solution.py:48
  125.5 9.4 %copy-start.24 = (bf16[64,576]{1,0:T(8,128)(2,1)}, bf16[64,576]{1,0:T(8,128)(2,1)S(1)}, u32[]{:S(2)}) copy-start(bf16[64,576]{1,0:T(8,128)(2,1)S(1)} %collective-permute-done.13.refs_0_) | copy-start | bytes 221188
  125.5 5.7 %collective-permute-start.18 = (bf16[64,576]{1,0:T(8,128)(2,1)}, bf16[64,576]{1,0:T(8,128)(2,1)S(1)}, u32[]{:S(2)}, u32[]{:S(2)}) collective-permute-start(bf16[64,576]{1,0:T(8,128)(2,1)} %get-tuple-element.83), channel_id=1, source_target_pairs={{0,32},{32,0},{1,33},{33,1},{2,34},{34,2},{3,35},{35,3},{4,36},{36... | collective-permute-start | bytes 221192 | tf_op jit(solution)/shard_map/ppermute | solution.py:48
  128.4 4.1 %collective-permute-start.19 = (bf16[64,576]{1,0:T(8,128)(2,1)}, bf16[64,576]{1,0:T(8,128)(2,1)S(1)}, u32[]{:S(2)}, u32[]{:S(2)}) collective-permute-start(bf16[64,576]{1,0:T(8,128)(2,1)} %get-tuple-element.84), channel_id=1, source_target_pairs={{0,64},{64,0},{128,192},{192,128},{1,65},{65,1},{129,193},{193,129... | collective-permute-start | bytes 221192 | tf_op jit(solution)/shard_map/ppermute | solution.py:48
  128.8 6.2 %collective-permute-start.20 = (bf16[64,576]{1,0:T(8,128)(2,1)}, bf16[64,576]{1,0:T(8,128)(2,1)S(1)}, u32[]{:S(2)}, u32[]{:S(2)}) collective-permute-start(bf16[64,576]{1,0:T(8,128)(2,1)} %get-tuple-element.85), channel_id=1, source_target_pairs={{0,128},{64,192},{128,0},{192,64},{1,129},{65,193},{129,1},{193,65... | collective-permute-start | bytes 221192 | tf_op jit(solution)/shard_map/ppermute | solution.py:48
  163.1 4.6 %collective-permute-start.21 = (bf16[8,72,640]{2,1,0:T(8,128)(2,1)S(1)}, bf16[8,72,640]{2,1,0:T(8,128)(2,1)S(1)}, u32[]{:S(2)}, u32[]{:S(2)}) collective-permute-start(bf16[8,72,640]{2,1,0:T(8,128)(2,1)S(1)} %all_to_all.41.near_ref.refs_1_), channel_id=1, source_target_pairs={{0,32},{32,0},{1,33},{33,1},{2,34},{34,2},{3,35},{35,3},{4,36},{36... | collective-permute-start | bytes 2211848 | tf_op jit(solution)/shard_map/ppermute | solution.py:44
  210.4 46.8 %copy-start.17 = (f32[64,64]{1,0:T(8,128)S(1)}, f32[64,64]{1,0:T(8,128)}, u32[]{:S(2)}) copy-start(f32[64,64]{1,0:T(8,128)} %slice.135.refs_8_) | copy-start | bytes 49156
  210.4 46.8 %copy-start.10 = (f32[64,576]{1,0:T(8,128)S(1)}, f32[64,576]{1,0:T(8,128)}, u32[]{:S(2)}) copy-start(f32[64,576]{1,0:T(8,128)} %get-tuple-element.86.field_ref) | copy-start | bytes 442372
  210.4 3.7 %collective-permute-start.22 = (bf16[64,576]{1,0:T(8,128)(2,1)}, bf16[64,576]{1,0:T(8,128)(2,1)S(1)}, u32[]{:S(2)}, u32[]{:S(2)}) collective-permute-start(bf16[64,576]{1,0:T(8,128)(2,1)} %get-tuple-element.91), channel_id=1, source_target_pairs={{0,1},{1,0},{2,3},{3,2},{4,5},{5,4},{6,7},{7,6},{8,9},{9,8},{10,11... | collective-permute-start | bytes 221192 | tf_op jit(solution)/shard_map/ppermute | solution.py:48
  210.8 6.2 %collective-permute-start.23 = (bf16[64,576]{1,0:T(8,128)(2,1)}, bf16[64,576]{1,0:T(8,128)(2,1)S(1)}, u32[]{:S(2)}, u32[]{:S(2)}) collective-permute-start(bf16[64,576]{1,0:T(8,128)(2,1)} %get-tuple-element.92), channel_id=1, source_target_pairs={{0,2},{1,3},{2,0},{3,1},{4,6},{5,7},{6,4},{7,5},{8,10},{9,11},{10,... | collective-permute-start | bytes 221192 | tf_op jit(solution)/shard_map/ppermute | solution.py:48
  211.9 5.3 %collective-permute-start.24 = (bf16[64,576]{1,0:T(8,128)(2,1)}, bf16[64,576]{1,0:T(8,128)(2,1)S(1)}, u32[]{:S(2)}, u32[]{:S(2)}) collective-permute-start(bf16[64,576]{1,0:T(8,128)(2,1)} %get-tuple-element.93), channel_id=1, source_target_pairs={{0,4},{4,0},{8,12},{12,8},{16,20},{20,16},{24,28},{28,24},{1,5},{5... | collective-permute-start | bytes 221192 | tf_op jit(solution)/shard_map/ppermute | solution.py:48
  212.2 7.4 %collective-permute-start.25 = (bf16[64,576]{1,0:T(8,128)(2,1)}, bf16[64,576]{1,0:T(8,128)(2,1)S(1)}, u32[]{:S(2)}, u32[]{:S(2)}) collective-permute-start(bf16[64,576]{1,0:T(8,128)(2,1)} %get-tuple-element.94), channel_id=1, source_target_pairs={{0,8},{4,12},{8,0},{12,4},{16,24},{20,28},{24,16},{28,20},{1,9},{5... | collective-permute-start | bytes 221192 | tf_op jit(solution)/shard_map/ppermute | solution.py:48
  212.3 7.7 %collective-permute-start.26 = (bf16[64,576]{1,0:T(8,128)(2,1)}, bf16[64,576]{1,0:T(8,128)(2,1)S(1)}, u32[]{:S(2)}, u32[]{:S(2)}) collective-permute-start(bf16[64,576]{1,0:T(8,128)(2,1)} %get-tuple-element.95), channel_id=1, source_target_pairs={{0,16},{4,20},{8,24},{12,28},{16,0},{20,4},{24,8},{28,12},{1,17},{... | collective-permute-start | bytes 221192 | tf_op jit(solution)/shard_map/ppermute | solution.py:48
  214.1 8.5 %copy-start.23 = (bf16[64,576]{1,0:T(8,128)(2,1)}, bf16[64,576]{1,0:T(8,128)(2,1)S(1)}, u32[]{:S(2)}) copy-start(bf16[64,576]{1,0:T(8,128)(2,1)S(1)} %collective-permute-done.22.refs_0_) | copy-start | bytes 221188
  214.1 5.9 %collective-permute-start.27 = (bf16[64,576]{1,0:T(8,128)(2,1)}, bf16[64,576]{1,0:T(8,128)(2,1)S(1)}, u32[]{:S(2)}, u32[]{:S(2)}) collective-permute-start(bf16[64,576]{1,0:T(8,128)(2,1)} %get-tuple-element.96), channel_id=1, source_target_pairs={{0,32},{32,0},{1,33},{33,1},{2,34},{34,2},{3,35},{35,3},{4,36},{36... | collective-permute-start | bytes 221192 | tf_op jit(solution)/shard_map/ppermute | solution.py:48
  217.0 3.8 %collective-permute-start.28 = (bf16[64,576]{1,0:T(8,128)(2,1)}, bf16[64,576]{1,0:T(8,128)(2,1)S(1)}, u32[]{:S(2)}, u32[]{:S(2)}) collective-permute-start(bf16[64,576]{1,0:T(8,128)(2,1)} %get-tuple-element.97), channel_id=1, source_target_pairs={{0,64},{64,0},{128,192},{192,128},{1,65},{65,1},{129,193},{193,129... | collective-permute-start | bytes 221192 | tf_op jit(solution)/shard_map/ppermute | solution.py:48
  217.2 5.5 %collective-permute-start.29 = (bf16[64,576]{1,0:T(8,128)(2,1)}, bf16[64,576]{1,0:T(8,128)(2,1)S(1)}, u32[]{:S(2)}, u32[]{:S(2)}) collective-permute-start(bf16[64,576]{1,0:T(8,128)(2,1)} %get-tuple-element.98), channel_id=1, source_target_pairs={{0,128},{64,192},{128,0},{192,64},{1,129},{65,193},{129,1},{193,65... | collective-permute-start | bytes 221192 | tf_op jit(solution)/shard_map/ppermute | solution.py:48
  223.3 34.1 %copy-start.13 = (f32[64,576]{1,0:T(8,128)S(1)}, f32[64,576]{1,0:T(8,128)}, u32[]{:S(2)}) copy-start(f32[64,576]{1,0:T(8,128)} %get-tuple-element.90.field_ref) | copy-start | bytes 442372
  226.3 32.3 %copy-start.16 = (f32[64,64]{1,0:T(8,128)S(1)}, f32[64,64]{1,0:T(8,128)}, u32[]{:S(2)}) copy-start(f32[64,64]{1,0:T(8,128)} %slice.137.refs_8_) | copy-start | bytes 49156
  254.3 5.0 %collective-permute-start.30 = (bf16[8,80,576]{2,1,0:T(8,128)(2,1)S(1)}, bf16[8,80,576]{2,1,0:T(8,128)(2,1)}, u32[]{:S(2)}, u32[]{:S(2)}) collective-permute-start(bf16[8,80,576]{2,1,0:T(8,128)(2,1)S(1)} %all_to_all.43.near_ref), channel_id=1, source_target_pairs={{0,32},{32,0},{1,33},{33,1},{2,34},{34,2},{3,35},{35,3},{4,36},{36... | collective-permute-start | bytes 2211848 | tf_op jit(solution)/shard_map/ppermute | solution.py:44
  264.9 25.3 %all-to-all-start.5 = ((bf16[16,64,576]{2,1,0:T(8,128)(2,1)}), bf16[16,64,576]{2,1,0:T(8,128)(2,1)S(1)}, u32[]{:S(2)}, u32[]{:S(2)}) async-start(bf16[16,64,576]{2,1,0:T(8,128)(2,1)} %get-tuple-element.104), calls=%async_computation.5 | async-start | bytes 2621440 | tf_op jit(solution)/shard_map/all_to_all | solution.py:39
  273.7 20.9 %copy-start.11 = (f32[64,576]{1,0:T(8,128)S(1)}, f32[64,576]{1,0:T(8,128)}, u32[]{:S(2)}) copy-start(f32[64,576]{1,0:T(8,128)} %get-tuple-element.77.field_ref) | copy-start | bytes 442372
  273.7 20.9 %copy-start.12 = (f32[64,576]{1,0:T(8,128)S(1)}, f32[64,576]{1,0:T(8,128)}, u32[]{:S(2)}) copy-start(f32[64,576]{1,0:T(8,128)} %get-tuple-element.99.field_ref) | copy-start | bytes 442372
  273.7 20.9 %copy-start.15 = (f32[64,576]{1,0:T(8,128)S(1)}, f32[64,576]{1,0:T(8,128)}, u32[]{:S(2)}) copy-start(f32[64,576]{1,0:T(8,128)} %get-tuple-element.67.field_ref) | copy-start | bytes 442372
  295.8 25.7 %copy-start.47 = (s32[512]{0:T(512)S(1)}, s32[512]{0:T(512)}, u32[]{:S(2)}) copy-start(s32[512]{0:T(512)} %param.15) | copy-start | bytes 6148
  (38 other events, 130.5 us)
where the time goes:
time: 324 us; the launch traced here: 323 us
  blocking collectives  133 us (41%)
  starting transfers between devices  60.9 us (19%)
  waiting for transfers between devices  50.2 us (15%)
  Pallas kernels  48.2 us (15%)
  local copies, waits for them, and re-layouts  13.2 us (4%)
  other arithmetic  7.84 us (2%)
  matrix products  7 us (2%)
    all_to_all x4, blocking collectives, exchanged(): return lax.all_to_all(array, axes, split_axis=0, concat_axis=0, tiled=True)  107 us
    ppermute x24, starting transfers between devices, from_partner(): lax.ppermute(value, axis, [(i, i ^ distance) for i in range(lax.axis_size...  40.5 us
    ppermute x7, waiting for transfers between devices, shifted(): lax.ppermute(value, axis, [(i, (i + step) % size) for i in range(size)])  25.6 us
    all_to_all x2, blocking collectives, from_everyone(): return lax.all_to_all(copies, axes, split_axis=0, concat_axis=0, tiled=True)  25.6 us
    pallas_call x8, Pallas kernels, kernel_call(): pl.pallas_call(kernel, out_shape=[jax.ShapeDtypeStruct(shape, dtype) for...  22.6 us
    pallas_call x3, Pallas kernels, products(): pl.pallas_call(functools.partial(times_kernel, rows, width, share, rank),...  18.5 us
    all_to_all x2, waiting for transfers between devices, exchanged(): return lax.all_to_all(array, axes, split_axis=0, concat_axis=0, tiled=True)  15 us
    ppermute x7, starting transfers between devices, shifted(): lax.ppermute(value, axis, [(i, (i + step) % size) for i in range(size)])  11.6 us
  transfers between devices with their start and end apart: 33, of which 14 were waited for; matrix products, arithmetic and copies ran while one was open for 5% of the time, Pallas kernels for 1%

commit v1 on v0

--- a/solution.py
+++ b/solution.py
@@ -19,7 +19,6 @@
 EXACT = lax.Precision.HIGHEST
 STEPS = 3
 INTERPRET = False
-PARTS = 1
 
 
 def mm(left, right):
@@ -55,15 +54,22 @@
 
 def by_x_kernel(n_x, n_z, me_ref, grm_ref, *out_refs):
     rows = grm_ref.shape[1]
-    whole = grm_ref[0]
-    for x in range(n_x):
-        starts = [(z * n_x + x) * rows for z in range(n_z)]
-        columns = jnp.concatenate([whole[:, at : at + rows] for at in starts], axis=1)
+
+    def regroup(block, _):
+        whole = grm_ref[block]
+        columns = []
+        for x in range(n_x):
+            starts = [(z * n_x + x) * rows for z in range(n_z)]
+            columns.append(jnp.concatenate([whole[:, at : at + rows] for at in starts], axis=1))
         for step, out_ref in enumerate(out_refs):
-
-            @pl.when(lax.rem(x - me_ref[0] + n_x, n_x) == step)
-            def _():
-                out_ref[0] = columns
+            wanted = lax.rem(me_ref[0] + step, n_x)
+            chosen = columns[0]
+            for x in range(1, n_x):
+                chosen = jnp.where(wanted == x, columns[x], chosen)
+            out_ref[block] = chosen
+        return 0
+
+    lax.fori_loop(0, grm_ref.shape[0], regroup, 0)
 
 
 def place_kernel(n_x, n_c, me_ref, *refs):
@@ -80,18 +86,12 @@
     rows = grm.shape[2]
     me = lax.axis_index("x").astype(jnp.int32)[None]
     depth = n_z * rows
-    return pl.pallas_call(
+    return kernel_call(
         functools.partial(by_x_kernel, n_x, n_z),
-        grid=(n_y * n_c,),
-        out_shape=[jax.ShapeDtypeStruct((n_y * n_c, rows, depth), grm.dtype)] * n_x,
-        in_specs=[
-            pl.BlockSpec(memory_space=pltpu.SMEM),
-            pl.BlockSpec((1, rows, n_x * depth), lambda i: (i, 0, 0)),
-        ],
-        out_specs=[pl.BlockSpec((1, rows, depth), lambda i: (i, 0, 0))] * n_x,
-        name="by_x",
-        interpret=INTERPRET,
-    )(me, grm.reshape(n_y * n_c, rows, n_x * depth))
+        [((n_y * n_c, rows, depth), grm.dtype)] * n_x,
+        [me, grm.reshape(n_y * n_c, rows, n_x * depth)],
+        1,
+    )
 
 
 def rearranged(blocks):
@@ -183,7 +183,7 @@
     send_coefficients(field_ref[...], basis_ref, sent_refs)
 
 
-def image_kernel(me_ref, variance_ref, arrived_ref, own_ref, field_ref, *refs):
+def image_kernel(with_coarse, me_ref, variance_ref, arrived_ref, own_ref, field_ref, *refs):
     rows = own_ref.shape[0]
 
     def add(d, total):
@@ -194,9 +194,27 @@
     image = variance_ref[0] * total + variance_ref[1] * field_ref[...]
     if len(refs) == 1:
         refs[0][...] = image
-    else:
+        return
+    if not with_coarse:
         refs[1][...] = image
         send_coefficients(image, refs[0], refs[2:])
+        return
+    basis_ref, coupling_ref, image_ref, coarse_ref, s0_ref = refs[:5]
+    rank = coupling_ref.shape[0]
+    rhs = image.shape[1] - rank
+    share = (arrived_ref.shape[1] - rows) // 6
+    pieces = []
+    for d in range(arrived_ref.shape[0]):
+        rode = arrived_ref[d, rows:, :rhs].astype(F32)
+        pieces.append(rode[:share] + rode[3 * share : 4 * share])
+    t0 = jnp.concatenate(pieces, axis=0)
+    s0 = jnp.dot(coupling_ref[...], t0, precision=EXACT, preferred_element_type=F32)
+    coarse = image[:, rhs:]
+    image = image[:, :rhs] + jnp.dot(coarse, s0, precision=EXACT, preferred_element_type=F32)
+    image_ref[...] = image
+    coarse_ref[...] = coarse
+    s0_ref[...] = s0
+    send_coefficients(image, basis_ref, refs[5:])
 
 
 def lift_kernel(levels, cuts, inside, field_ref, own_ref, lift_ref, *refs):
@@ -248,6 +266,7 @@
     levels = couplings.shape[0] - 1
     rank = couplings.shape[1]
     split_at = levels * rank
+    width = rhs + rank
     n_rows, n_columns = lax.axis_size(ROWS), lax.axis_size(COLUMNS)
     me_rows, me_columns = lax.axis_index(ROWS), lax.axis_index(COLUMNS)
 
@@ -344,21 +363,30 @@
         )(places, *g_blocks, *everyone, *riders)
         return exchanged(partial, ROWS), own
 
-    def image_of(arrived, own, field, send=True):
+    def image_of(arrived, own, field):
         width = field.shape[1]
-        shapes = [((rows, width), F32)] + (coefficient_shapes(width) if send else [])
-        operands = [places, variance, arrived, own, field] + ([basis_terms] if send else [])
-        image, *sent = kernel_call(image_kernel, shapes, operands, 2)
+        operands = [places, variance, arrived, own, field, basis_terms]
+        shapes = [((rows, width), F32)] + coefficient_shapes(width)
+        kernel = functools.partial(image_kernel, False)
+        image, *sent = kernel_call(kernel, shapes, operands, 2)
         return image, sent
+
+    def last_image_of(arrived, own, field):
+        operands = [places, variance, arrived, own, field]
+        kernel = functools.partial(image_kernel, False)
+        return kernel_call(kernel, [(field.shape, F32)], operands, 2)[0]
+
+    def image_with_coarse(arrived, own, field):
+        operands = [places, variance, arrived, own, field, basis_terms, coarse_coupling]
+        shapes = [((rows, rhs), F32), ((rows, rank), F32), ((rank, rhs), F32)]
+        kernel = functools.partial(image_kernel, True)
+        shapes = shapes + coefficient_shapes(rhs)
+        image, coarse, s0, *sent = kernel_call(kernel, shapes, operands, 2)
+        return image, coarse, s0, sent
 
     def sum_of_terms(terms, axis):
         top, rest = jnp.split(terms.astype(F32), 2, axis=axis)
         return top + rest
-
-    half = rhs // PARTS
-    cuts = [(k * half, (k + 1) * half) for k in range(PARTS)]
-    widths = [half + (0 if k else rank) for k in range(PARTS)]
-    parts = range(len(cuts))
 
     def padded(array, width):
         more = width - array.shape[-1]
@@ -369,88 +397,64 @@
     t_parts = mm3(coarse_basis.T, right_sides).reshape(n_rows, t_share, rhs)
     t_top = lax.reduce_precision(t_parts, 8, 7)
     t_parts = jnp.concatenate([t_top, t_parts - t_top], axis=1).astype(BF16)
-    t_parts = [padded(t_parts[:, :, slice(*cuts[k])], widths[k]) for k in parts]
-
-    first = precondition(right_sides, sent, cuts, True, beside=coarse_basis)
-    first, copies = first[::2], first[1::2]
-    all_first = [gathered(copies[k]) for k in parts]
-    sums = [products(all_first[k], widths[k], [t_parts[k]], 2 * t_share) for k in parts]
-    first_image, sent = zip(*[image_of(*sums[k], first[k]) for k in parts])
-    coarse_image = first_image[0][:, half:]
-
-    second, all_second, t_rows = [], [], []
-    for k in parts:
-        rows_of_t = sum_of_terms(sums[k][0][:, rows:], 1).sum(axis=0)
-        field, copies = precondition(
-            first_image[k],
-            sent[k],
-            beside=None if k else coarse_image,
-            below=two_terms(padded(rows_of_t, widths[k] + (0 if k else rank))),
-        )
-        second.append(field)
-        all_second.append(gathered(copies))
-        near, far = all_second[k]
-        rode = near[:, rows:, : widths[k]].astype(F32) + far[:, rows:, : widths[k]].astype(F32)
-        t_rows.append(sum_of_terms(rode, 1).sum(axis=0))
-    sums = [
-        products(
-            all_second[k], widths[k], [t_rows[k], *all_second[0], *all_first[k]], 6 * share, share
-        )
-        for k in parts
+    t_parts = padded(t_parts, width)
+
+    cuts = [(0, rhs)]
+    first, copies = precondition(right_sides, sent, cuts, True, beside=coarse_basis)
+    all_first = gathered(copies)
+    arrived, own = products(all_first, width, [t_parts], 2 * t_share)
+    first_image, sent = image_of(arrived, own, first)
+    coarse_image = first_image[:, rhs:]
+
+    t_rows = sum_of_terms(arrived[:, rows:], 1).sum(axis=0)
+    t_rows = two_terms(padded(t_rows, width + rank))
+    second, copies = precondition(first_image, sent, beside=coarse_image, below=t_rows)
+    all_second = gathered(copies)
+    near, far = all_second
+    t_rows = near[:, rows:, :width].astype(F32) + far[:, rows:, :width].astype(F32)
+    t_rows = sum_of_terms(t_rows, 1).sum(axis=0)
+    riders = [t_rows, *all_second, *all_first]
+    arrived, own = products(all_second, width, riders, 6 * share, share)
+    second_image, second_coarse, s0, sent = image_with_coarse(arrived, own, second)
+
+    rode = sum_of_terms(arrived[:, rows:], 1)[:, t_share:].sum(axis=0)
+    below = [rode[:, :rhs], rode[:, rhs:].reshape(-1, rhs)]
+    below = two_terms(jnp.concatenate(below, axis=0))
+    n_below = below.shape[0]
+    below = jnp.pad(below, ((0, -n_below % 8), (0, 0)))
+    third, copies = precondition(second_image, sent, below=below)
+    everyone = gathered(copies)
+    arrived, own = products(everyone, rhs)
+    own, *everyone = lax.optimization_barrier((own, *everyone))
+    third_image = last_image_of(arrived, own, third)
+
+    table = sum_of_terms(jnp.stack([array[:, rows : rows + n_below] for array in everyone]), 2)
+    table = jnp.where(lax.axis_index("c") == 0, table, table[::-1])
+    table = table.reshape(n_columns, n_below // 2, rhs)
+    k_first = table[:, :share].reshape(rank, rhs)
+    k_second = table[:, share : 2 * share].reshape(rank, rhs)
+    k_coarse = table[:, 2 * share :].reshape(n_columns, 2, share, rank).transpose(1, 0, 2, 3)
+    k_basis, k_coarse = k_coarse.reshape(2, rank, rank)
+    s1 = mm(coarse_coupling, k_first + mm(k_basis, s0))
+    s2 = mm(coarse_coupling, k_second + mm(k_coarse, s0) + mm(k_basis, s1))
+    weights = jnp.concatenate([s0, s1, s2], axis=0)
+
+    none = jnp.zeros_like(coarse_basis)
+    second_lift = second[:, rhs:]
+    coarse_parts = [
+        [coarse_basis, none, none],
+        [second_lift, coarse_basis, none],
+        [none, second_lift, coarse_basis],
+        [coarse_image, none, none],
+        [none, coarse_image, none],
+        [none, second_coarse, coarse_image],
     ]
-    second_image, sent = zip(*[image_of(*sums[k], second[k]) for k in parts])
-
-    t0, third, third_image, tables = [], [], [], []
-    for k in parts:
-        rode = sum_of_terms(sums[k][0][:, rows:], 1)
-        t0.append(rode[:, :t_share].reshape(rank, widths[k])[:, :half])
-        field, copies = precondition(
-            second_image[k], sent[k], below=two_terms(rode[:, t_share:].sum(axis=0))
-        )
-        third.append(field)
-        everyone = gathered(copies)
-        arrived, own = products(everyone, widths[k])
-        own, *everyone = lax.optimization_barrier((own, *everyone))
-        third_image.append(image_of(arrived, own, field, send=False)[0])
-        table = sum_of_terms(jnp.stack([array[:, rows:] for array in everyone]), 2)
-        table = jnp.where(lax.axis_index("c") == 0, table, table[::-1])
-        table = table.reshape(n_columns, 2, share, widths[k]).transpose(1, 0, 2, 3)
-        tables.append(table.reshape(2, rank, widths[k]))
-
-    def joined(fields):
-        if PARTS == 1:
-            return fields[0]
-        return jnp.concatenate([fields[0][:, :half], *fields[1:], fields[0][:, half:]], axis=1)
-
-    first, second, third = joined(first), joined(second), joined(third)
-    first_image, second_image = joined(first_image), joined(second_image)
-    third_image = joined(third_image)
-    t0 = jnp.concatenate(t0, axis=1)
-    k_first, k_second = (joined([table[i] for table in tables]) for i in range(2))
-
-    k_basis = k_first[:, rhs:]
-    s0 = mm(coarse_coupling, t0[:, :rhs])
-    s1 = mm(coarse_coupling, k_first[:, :rhs] + mm(k_basis, s0))
-    s2 = mm(coarse_coupling, k_second[:, :rhs] + mm(k_second[:, rhs:], s0) + mm(k_basis, s1))
-    weights = jnp.concatenate([s0, s1, s2], axis=0)
-
-    none = jnp.zeros_like(coarse_basis)
-    coarse_parts = jnp.concatenate(
-        [
-            jnp.concatenate([coarse_basis, none, none], axis=1),
-            jnp.concatenate([second[:, rhs:], coarse_basis, none], axis=1),
-            jnp.concatenate([third[:, rhs:], second[:, rhs:], coarse_basis], axis=1),
-            jnp.concatenate([coarse_image, none, none], axis=1),
-            jnp.concatenate([second_image[:, rhs:], coarse_image, none], axis=1),
-        ],
-        axis=0,
-    )
-    coarse_parts = mm3(coarse_parts, weights).reshape(5, rows, rhs)
-    v = [field[:, :rhs] + coarse_parts[k] for k, field in enumerate([first, second, third])]
-    w = [right_sides]
-    w += [field[:, :rhs] + coarse_parts[3 + k] for k, field in enumerate([first_image, second_image])]
-    last_parts = [third_image[:, rhs:], second_image[:, rhs:], coarse_image]
-    w.append(third_image[:, :rhs] + mm3(jnp.concatenate(last_parts, axis=1), weights))
+    coarse_parts = jnp.concatenate([jnp.concatenate(row, axis=1) for row in coarse_parts], axis=0)
+    coarse_parts = mm3(coarse_parts, weights).reshape(6, rows, rhs)
+    fields = [first[:, :rhs], second[:, :rhs], third]
+    v = [field + part for field, part in zip(fields, coarse_parts[:3])]
+    fields = [first_image[:, :rhs], second_image, third_image]
+    w = [right_sides] + [field + part for field, part in zip(fields, coarse_parts[3:])]
 
     moments = jnp.stack([jnp.sum(w[k - k // 2] * v[k // 2], axis=0) for k in range(2 * STEPS)])
     moments = from_everyone(moments, ROWS).sum(axis=0)

time: 324 us -> 319 us (0.985)
  blocking collectives: 133 us -> 101 us
  waiting for transfers between devices: 50.2 us -> 75.5 us
  starting transfers between devices: 60.9 us -> 65.6 us
  Pallas kernels: 48.2 us -> 44.8 us
    all_to_all x4 -> x3, blocking collectives: 107 us -> 75.4 us  [exchanged(): return lax.all_to_all(array, axes, split_axis=0, concat_axis=0, tiled=True)]
    all_to_all x2 -> x3, waiting for transfers between devices: 15 us -> 40.4 us  [exchanged(): return lax.all_to_all(array, axes, split_axis=0, concat_axis=0, tiled=True)]
    pallas_call x1 -> x0, Pallas kernels: 7.19 us -> none  [cut_by_x(): pl.pallas_call(functools.partial(by_x_kernel, n_x, n_z), grid=(n_y * n_c,...]
    all_to_all x2 -> x3, starting transfers between devices: 8.82 us -> 14.6 us  [exchanged(): return lax.all_to_all(array, axes, split_axis=0, concat_axis=0, tiled=True)]
    pallas_call x8 -> x9, Pallas kernels: 22.6 us -> 26.9 us  [kernel_call(): pl.pallas_call(kernel, out_shape=[jax.ShapeDtypeStruct(shape, dtype) for...]
    unnamed x108 -> x116, local copies, waits for them, and re-layouts: 6.98 us -> 8.48 us
  transfers between devices with their start and end apart: 33 -> 34, of which waited for: 14 -> 15; matrix products, arithmetic and copies ran while one was open for 5% -> 4% of each run, Pallas kernels for 1% -> 1%
where the time goes in v1:
time: 319 us; the launch traced here: 318 us
  blocking collectives  101 us (32%)
  waiting for transfers between devices  75.5 us (24%)
  starting transfers between devices  65.6 us (21%)
  Pallas kernels  44.8 us (14%)
  local copies, waits for them, and re-layouts  14 us (4%)
  other arithmetic  9.19 us (3%)
  matrix products  5.57 us (2%)
    all_to_all x3, blocking collectives, exchanged(): return lax.all_to_all(array, axes, split_axis=0, concat_axis=0, tiled=True)  75.4 us
    all_to_all x3, waiting for transfers between devices, exchanged(): return lax.all_to_all(array, axes, split_axis=0, concat_axis=0, tiled=True)  40.4 us
    ppermute x24, starting transfers between devices, from_partner(): lax.ppermute(value, axis, [(i, i ^ distance) for i in range(lax.axis_size...  39.7 us
    pallas_call x9, Pallas kernels, kernel_call(): pl.pallas_call(kernel, out_shape=[jax.ShapeDtypeStruct(shape, dtype) for...  26.9 us
    all_to_all x2, blocking collectives, from_everyone(): return lax.all_to_all(copies, axes, split_axis=0, concat_axis=0, tiled=True)  25.8 us
    ppermute x7, waiting for transfers between devices, shifted(): lax.ppermute(value, axis, [(i, (i + step) % size) for i in range(size)])  25.8 us
    pallas_call x3, Pallas kernels, products(): pl.pallas_call(functools.partial(times_kernel, rows, width, share, rank),...  17.9 us
    all_to_all x3, starting transfers between devices, exchanged(): return lax.all_to_all(array, axes, split_axis=0, concat_axis=0, tiled=True)  14.6 us
  transfers between devices with their start and end apart: 34, of which 15 were waited for; matrix products, arithmetic and copies ran while one was open for 4% of the time, Pallas kernels for 1%

profile of v1, /device:TPU:1, one launch (start us, length us, event | category | flops | bytes accessed | tf_op | source)
XLA Modules:
  0.0 318.0 jit_solution(11551737625817955465)
XLA Ops:
  0.7 4.3 %shard_map.95 = (bf16[8,64,512]{2,1,0:T(8,128)(2,1)}, bf16[8,64,512]{2,1,0:T(8,128)(2,1)}, bf16[8,64,512]{2,1,0:T(8,128)(2,1)}, bf16[8,64,512]{2,1,0:T(8,128)(2,1)}) custom-call(s32[1]{0:T(128)} %bitcast.me_ref, bf16[8,64,2048]{2,1,0:T(8,128)(2,1)} %bitcast.55), custom_call_target="tpu_custom_call" | custom-call | tf_op jit(solution)/shard_map/pallas_call | solution.py:254
  6.7 2.0 shard_map.96
  8.7 2.0 collective-permute-start
  10.7 2.4 collective-permute-start.1
  13.1 1.6 collective-permute-start.2
  14.8 3.0 collective-permute-start.3
  17.8 4.2 %collective-permute-start.4 = (bf16[64,512]{1,0:T(8,128)(2,1)}, bf16[64,512]{1,0:T(8,128)(2,1)S(1)}, u32[]{:S(2)}, u32[]{:S(2)}) collective-permute-start(bf16[64,512]{1,0:T(8,128)(2,1)} %get-tuple-element.65), channel_id=1, source_target_pairs={{0,16},{4,20},{8,24},{12,28},{16,0},{20,4},{24,8},{28,12},{1,17},{... | collective-permute-start | bytes 196616 | tf_op jit(solution)/shard_map/ppermute | solution.py:47
  26.2 2.2 collective-permute-start.5
  28.4 1.4 collective-permute-start.6
  29.8 2.7 collective-permute-start.7
  33.2 2.7 collective-permute-done.7.refs_7_
  36.6 2.7 shard_map.97
  39.3 3.7 %all-to-all-start = ((bf16[8,64,576]{2,1,0:T(8,128)(2,1)}), bf16[8,64,576]{2,1,0:T(8,128)(2,1)S(1)}, u32[]{:S(2)}, u32[]{:S(2)}) async-start(bf16[8,64,576]{2,1,0:T(8,128)(2,1)} %get-tuple-element.76), calls=%async_computation | async-start | bytes 1310720 | tf_op jit(solution)/shard_map/all_to_all | solution.py:38
  45.7 10.2 %collective-permute-done.10.refs_3_ = bf16[8,64,512]{2,1,0:T(8,128)(2,1)S(1)} collective-permute-done((bf16[8,64,512]{2,1,0:T(8,128)(2,1)}, bf16[8,64,512]{2,1,0:T(8,128)(2,1)S(1)}, u32[]{:S(2)}, u32[]{:S(2)}) %collective-permute-start.10) | collective-permute-done | bytes 524320 | tf_op jit(solution)/shard_map/ppermute | solution.py:43
  55.9 2.0 collective-permute-done.8.refs_1_
  57.9 9.5 %collective-permute-done.9.refs_2_ = bf16[8,64,512]{2,1,0:T(8,128)(2,1)S(1)} collective-permute-done((bf16[8,64,512]{2,1,0:T(8,128)(2,1)}, bf16[8,64,512]{2,1,0:T(8,128)(2,1)S(1)}, u32[]{:S(2)}, u32[]{:S(2)}) %collective-permute-start.9) | collective-permute-done | bytes 524320 | tf_op jit(solution)/shard_map/ppermute | solution.py:43
  68.2 3.0 shard_map.98
  71.2 3.7 %collective-permute-start.11 = (bf16[4,4,64,512]{3,2,1,0:T(8,128)(2,1)}, bf16[4,4,64,512]{3,2,1,0:T(8,128)(2,1)S(1)}, u32[]{:S(2)}, u32[]{:S(2)}) collective-permute-start(bf16[4,4,64,512]{3,2,1,0:T(8,128)(2,1)} %get-tuple-element.75), channel_id=1, source_target_pairs={{0,32},{32,0},{1,33},{33,1},{2,34},{34,2},{3,35},{35,3},{4,36},{36... | collective-permute-start | bytes 3145736 | tf_op jit(solution)/shard_map/ppermute | solution.py:43
  79.2 5.6 %times.3 = (bf16[16,72,576]{2,1,0:T(8,128)(2,1)}, f32[64,576]{1,0:T(8,128)}) custom-call(s32[2]{0:T(128)} %pad_add_fusion.me_ref, bf16[1024,512]{1,0:T(8,128)(2,1)} %bitcast.49, bf16[1024,512]{1,0:T(8,128)(2,1)} %bitcast.52, bf16[8,64,576]{2,1,0:T(8,128)(2,1)} %copy-done.4, bf16[8,64,576]{2,1,0:T(8,128)(2,1)} %copy-done.9, bf16[16,8,576]{2,1,0:T(8,128)(2,1)} %fusion.13.refs_0_), custom_call_target="tpu_custom_call" | custom-call | tf_op jit(solution)/shard_map/times/pallas_call | solution.py:343
  84.7 25.0 %all_to_all.40.arrived_ref = bf16[16,72,576]{2,1,0:T(8,128)(2,1)S(1)} all-to-all(bf16[16,72,576]{2,1,0:T(8,128)(2,1)} %get-tuple-element.77), channel_id=1, replica_groups=mesh['y'=4,'c'=2,'z'=8,'x'=4] {'y','x'}, dimensions={0} | all-to-all | bytes 2654208 | tf_op jit(solution)/shard_map/all_to_all | solution.py:38
  110.9 3.1 shard_map.99
  116.8 2.1 collective-permute-start.16
  118.9 2.4 collective-permute-start.17
  122.7 2.9 collective-permute-start.18
  126.0 1.8 collective-permute-start.20
  129.7 2.5 collective-permute-done.20.refs_7_
  132.9 2.9 shard_map.100
  135.8 24.5 %all_to_all.41.near_ref.refs_1_ = bf16[8,72,640]{2,1,0:T(8,128)(2,1)S(1)} all-to-all(bf16[8,72,640]{2,1,0:T(8,128)(2,1)} %get-tuple-element.89), channel_id=1, replica_groups=mesh['y'=4,'c'=2,'z'=8,'x'=4] {'z'}, dimensions={0} | all-to-all | bytes 1474560 | tf_op jit(solution)/shard_map/all_to_all | solution.py:38
  160.3 2.7 collective-permute-start.21
  163.0 1.8 collective-permute-done.21.far_ref.refs_2_
  165.8 7.3 %times.4 = (bf16[16,88,576]{2,1,0:T(8,128)(2,1)}, f32[64,576]{1,0:T(8,128)}) custom-call(s32[2]{0:T(128)} %pad_add_fusion.me_ref, bf16[1024,512]{1,0:T(8,128)(2,1)} %bitcast.50, bf16[1024,512]{1,0:T(8,128)(2,1)} %bitcast.53, bf16[8,72,640]{2,1,0:T(8,128)(2,1)} %copy-done.2, bf16[8,72,640]{2,1,0:T(8,128)(2,1)} %copy-done.7, f32[4,576]{1,0:T(4,128)} %fusion.20.refs_0_, ...), custom_call_target="tpu_custom_call" | custom-call | tf_op jit(solution)/shard_map/times/pallas_call | solution.py:343
  173.1 5.3 %all-to-all-start.3 = ((bf16[16,88,576]{2,1,0:T(8,128)(2,1)}), bf16[16,88,576]{2,1,0:T(8,128)(2,1)S(1)}, u32[]{:S(2)}, u32[]{:S(2)}) async-start(bf16[16,88,576]{2,1,0:T(8,128)(2,1)} %get-tuple-element.90), calls=%async_computation.3 | async-start | bytes 3604480 | tf_op jit(solution)/shard_map/all_to_all | solution.py:38
  179.0 27.0 %all-to-all-done.3.arrived_ref = bf16[16,88,576]{2,1,0:T(8,128)(2,1)S(1)} async-done(((bf16[16,88,576]{2,1,0:T(8,128)(2,1)}), bf16[16,88,576]{2,1,0:T(8,128)(2,1)S(1)}, u32[]{:S(2)}, u32[]{:S(2)}) %all-to-all-start.3) | async-done | bytes 1622048 | tf_op jit(solution)/shard_map/all_to_all | solution.py:38
  207.4 3.7 %shard_map.101 = (f32[64,512]{1,0:T(8,128)}, f32[64,64]{1,0:T(8,128)}, f32[64,512]{1,0:T(8,128)}, bf16[64,512]{1,0:T(8,128)(2,1)}, bf16[64,512]{1,0:T(8,128)(2,1...) custom-call(s32[2]{0:T(128)} %pad_add_fusion.me_ref, ...), custom_call_target="tpu_custom_call" | custom-call | tf_op jit(solution)/shard_map/pallas_call | solution.py:254
  211.8 1.8 collective-permute-start.26
  214.5 2.6 collective-permute-start.27
  217.5 2.4 collective-permute-start.29
  220.8 1.6 collective-permute-done.29.refs_7_
  223.0 2.7 shard_map.102
  225.8 25.8 %all_to_all.42.near_ref = bf16[8,88,512]{2,1,0:T(8,128)(2,1)S(1)} all-to-all(bf16[8,88,512]{2,1,0:T(8,128)(2,1)} %get-tuple-element.103), channel_id=1, replica_groups=mesh['y'=4,'c'=2,'z'=8,'x'=4] {'z'}, dimensions={0} | all-to-all | bytes 1441792 | tf_op jit(solution)/shard_map/all_to_all | solution.py:38
  251.6 2.7 collective-permute-start.30
  257.0 5.0 %times.5 = (bf16[16,64,512]{2,1,0:T(8,128)(2,1)}, f32[64,512]{1,0:T(8,128)}) custom-call(s32[2]{0:T(128)} %pad_add_fusion.me_ref, bf16[1024,512]{1,0:T(8,128)(2,1)} %bitcast.51, bf16[1024,512]{1,0:T(8,128)(2,1)} %bitcast.54, bf16[8,88,512]{2,1,0:T(8,128)(2,1)} %copy-done.6, bf16[8,88,512]{2,1,0:T(8,128)(2,1)} %copy-done.17), custom_call_target="tpu_custom_call" | custom-call | tf_op jit(solution)/shard_map/times/pallas_call | solution.py:343
  264.5 5.6 %all-to-all-start.5 = ((bf16[16,64,512]{2,1,0:T(8,128)(2,1)}), bf16[16,64,512]{2,1,0:T(8,128)(2,1)S(1)}, u32[]{:S(2)}, u32[]{:S(2)}) async-start(bf16[16,64,512]{2,1,0:T(8,128)(2,1)} %get-tuple-element.108), calls=%async_computation.5 | async-start | bytes 2097152 | tf_op jit(solution)/shard_map/all_to_all | solution.py:38
  271.6 1.5 fusion.4
  273.1 13.4 %all-to-all-done.5.arrived_ref = bf16[16,64,512]{2,1,0:T(8,128)(2,1)S(1)} async-done(((bf16[16,64,512]{2,1,0:T(8,128)(2,1)}), bf16[16,64,512]{2,1,0:T(8,128)(2,1)S(1)}, u32[]{:S(2)}, u32[]{:S(2)}) %all-to-all-start.5) | async-done | bytes 1048608 | tf_op jit(solution)/shard_map/all_to_all | solution.py:38
  287.5 2.4 shard_map.103
  291.1 12.3 %all_to_all.43 = f32[16,6,512]{2,1,0:T(8,128)S(1)} all-to-all(f32[16,6,512]{2,1,0:T(8,128)S(1)} %broadcast_in_dim.49), channel_id=1, replica_groups=mesh['y'=4,'c'=2,'z'=8,'x'=4] {'y','x'}, dimensions={0} | all-to-all | bytes 393216 | tf_op jit(solution)/shard_map/all_to_all | solution.py:34
  303.4 13.5 %all_to_all.44 = f32[16,6,512]{2,1,0:T(8,128)S(1)} all-to-all(f32[16,6,512]{2,1,0:T(8,128)S(1)} %broadcast_in_dim.50), channel_id=1, replica_groups=mesh['y'=4,'c'=2,'z'=8,'x'=4] {'c','z'}, dimensions={0} | all-to-all | bytes 393216 | tf_op jit(solution)/shard_map/all_to_all | solution.py:34
  (231 shorter events, 38.2 us)
Async XLA Ops:
  4.9 17.1 %copy-start.13 = (f32[9,64,64]{2,1,0:T(8,128)S(1)}, f32[9,64,64]{2,1,0:T(8,128)}, u32[]{:S(2)}) copy-start(f32[9,64,64]{2,1,0:T(8,128)} %param.12) | copy-start | bytes 442372
  8.7 17.6 %collective-permute-start = (bf16[64,512]{1,0:T(8,128)(2,1)}, bf16[64,512]{1,0:T(8,128)(2,1)S(1)}, u32[]{:S(2)}, u32[]{:S(2)}) collective-permute-start(bf16[64,512]{1,0:T(8,128)(2,1)} %get-tuple-element.61), channel_id=1, source_target_pairs={{0,1},{1,0},{2,3},{3,2},{4,5},{5,4},{6,7},{7,6},{8,9},{9,8},{10,11... | collective-permute-start | bytes 196616 | tf_op jit(solution)/shard_map/ppermute | solution.py:47
  10.7 17.7 %collective-permute-start.1 = (bf16[64,512]{1,0:T(8,128)(2,1)}, bf16[64,512]{1,0:T(8,128)(2,1)S(1)}, u32[]{:S(2)}, u32[]{:S(2)}) collective-permute-start(bf16[64,512]{1,0:T(8,128)(2,1)} %get-tuple-element.62), channel_id=1, source_target_pairs={{0,2},{1,3},{2,0},{3,1},{4,6},{5,7},{6,4},{7,5},{8,10},{9,11},{10,... | collective-permute-start | bytes 196616 | tf_op jit(solution)/shard_map/ppermute | solution.py:47
  13.1 16.7 %collective-permute-start.2 = (bf16[64,512]{1,0:T(8,128)(2,1)}, bf16[64,512]{1,0:T(8,128)(2,1)S(1)}, u32[]{:S(2)}, u32[]{:S(2)}) collective-permute-start(bf16[64,512]{1,0:T(8,128)(2,1)} %get-tuple-element.63), channel_id=1, source_target_pairs={{0,4},{4,0},{8,12},{12,8},{16,20},{20,16},{24,28},{28,24},{1,5},{5... | collective-permute-start | bytes 196616 | tf_op jit(solution)/shard_map/ppermute | solution.py:47
  14.8 18.4 %collective-permute-start.3 = (bf16[64,512]{1,0:T(8,128)(2,1)}, bf16[64,512]{1,0:T(8,128)(2,1)S(1)}, u32[]{:S(2)}, u32[]{:S(2)}) collective-permute-start(bf16[64,512]{1,0:T(8,128)(2,1)} %get-tuple-element.64), channel_id=1, source_target_pairs={{0,8},{4,12},{8,0},{12,4},{16,24},{20,28},{24,16},{28,20},{1,9},{5... | collective-permute-start | bytes 196616 | tf_op jit(solution)/shard_map/ppermute | solution.py:47
  17.8 15.4 %collective-permute-start.4 = (bf16[64,512]{1,0:T(8,128)(2,1)}, bf16[64,512]{1,0:T(8,128)(2,1)S(1)}, u32[]{:S(2)}, u32[]{:S(2)}) collective-permute-start(bf16[64,512]{1,0:T(8,128)(2,1)} %get-tuple-element.65), channel_id=1, source_target_pairs={{0,16},{4,20},{8,24},{12,28},{16,0},{20,4},{24,8},{28,12},{1,17},{... | collective-permute-start | bytes 196616 | tf_op jit(solution)/shard_map/ppermute | solution.py:47
  26.2 9.7 %copy-start.42 = (bf16[64,512]{1,0:T(8,128)(2,1)}, bf16[64,512]{1,0:T(8,128)(2,1)S(1)}, u32[]{:S(2)}) copy-start(bf16[64,512]{1,0:T(8,128)(2,1)S(1)} %collective-permute-done.refs_0_) | copy-start | bytes 196612
  26.2 6.9 %collective-permute-start.5 = (bf16[64,512]{1,0:T(8,128)(2,1)S(1)}, bf16[64,512]{1,0:T(8,128)(2,1)S(1)}, u32[]{:S(2)}, u32[]{:S(2)}) collective-permute-start(bf16[64,512]{1,0:T(8,128)(2,1)S(1)} %copy-done.54), channel_id=1, source_target_pairs={{0,32},{32,0},{1,33},{33,1},{2,34},{34,2},{3,35},{35,3},{4,36},{36... | collective-permute-start | bytes 196616 | tf_op jit(solution)/shard_map/ppermute | solution.py:47
  28.4 4.8 %collective-permute-start.6 = (bf16[64,512]{1,0:T(8,128)(2,1)S(1)}, bf16[64,512]{1,0:T(8,128)(2,1)S(1)}, u32[]{:S(2)}, u32[]{:S(2)}) collective-permute-start(bf16[64,512]{1,0:T(8,128)(2,1)S(1)} %copy-done.53), channel_id=1, source_target_pairs={{0,64},{64,0},{128,192},{192,128},{1,65},{65,1},{129,193},{193,129... | collective-permute-start | bytes 196616 | tf_op jit(solution)/shard_map/ppermute | solution.py:47
  29.8 6.2 %collective-permute-start.7 = (bf16[64,512]{1,0:T(8,128)(2,1)S(1)}, bf16[64,512]{1,0:T(8,128)(2,1)S(1)}, u32[]{:S(2)}, u32[]{:S(2)}) collective-permute-start(bf16[64,512]{1,0:T(8,128)(2,1)S(1)} %copy-done.52), channel_id=1, source_target_pairs={{0,128},{64,192},{128,0},{192,64},{1,129},{65,193},{129,1},{193,65... | collective-permute-start | bytes 196616 | tf_op jit(solution)/shard_map/ppermute | solution.py:47
  39.3 35.7 %copy-start.8 = (f32[64,512]{1,0:T(8,128)S(1)}, f32[64,512]{1,0:T(8,128)}, u32[]{:S(2)}) copy-start(f32[64,512]{1,0:T(8,128)} %field_ref.1) | copy-start | bytes 393220
  39.3 35.6 %all-to-all-start = ((bf16[8,64,576]{2,1,0:T(8,128)(2,1)}), bf16[8,64,576]{2,1,0:T(8,128)(2,1)S(1)}, u32[]{:S(2)}, u32[]{:S(2)}) async-start(bf16[8,64,576]{2,1,0:T(8,128)(2,1)} %get-tuple-element.76), calls=%async_computation | async-start | bytes 1310720 | tf_op jit(solution)/shard_map/all_to_all | solution.py:38
  43.0 12.9 %collective-permute-start.10 = (bf16[8,64,512]{2,1,0:T(8,128)(2,1)}, bf16[8,64,512]{2,1,0:T(8,128)(2,1)S(1)}, u32[]{:S(2)}, u32[]{:S(2)}) collective-permute-start(bf16[8,64,512]{2,1,0:T(8,128)(2,1)} %get-tuple-element.73), channel_id=1, source_target_pairs={{0,3},{1,0},{2,1},{3,2},{4,7},{5,4},{6,5},{7,6},{8,11},{9,8},{10,9... | collective-permute-start | bytes 1572872 | tf_op jit(solution)/shard_map/ppermute | solution.py:43
  43.3 14.6 %collective-permute-start.8 = (bf16[8,64,512]{2,1,0:T(8,128)(2,1)}, bf16[8,64,512]{2,1,0:T(8,128)(2,1)S(1)}, u32[]{:S(2)}, u32[]{:S(2)}) collective-permute-start(bf16[8,64,512]{2,1,0:T(8,128)(2,1)} %get-tuple-element.71), channel_id=1, source_target_pairs={{0,1},{1,2},{2,3},{3,0},{4,5},{5,6},{6,7},{7,4},{8,9},{9,10},{10,1... | collective-permute-start | bytes 1572872 | tf_op jit(solution)/shard_map/ppermute | solution.py:43
  44.6 22.8 %collective-permute-start.9 = (bf16[8,64,512]{2,1,0:T(8,128)(2,1)}, bf16[8,64,512]{2,1,0:T(8,128)(2,1)S(1)}, u32[]{:S(2)}, u32[]{:S(2)}) collective-permute-start(bf16[8,64,512]{2,1,0:T(8,128)(2,1)} %get-tuple-element.72), channel_id=1, source_target_pairs={{0,2},{1,3},{2,0},{3,1},{4,6},{5,7},{6,4},{7,5},{8,10},{9,11},{10,... | collective-permute-start | bytes 1572872 | tf_op jit(solution)/shard_map/ppermute | solution.py:43
  55.9 11.5 %copy-start.22 = (bf16[8,64,512]{2,1,0:T(8,128)(2,1)}, bf16[8,64,512]{2,1,0:T(8,128)(2,1)S(1)}, u32[]{:S(2)}) copy-start(bf16[8,64,512]{2,1,0:T(8,128)(2,1)S(1)} %collective-permute-done.10.refs_3_) | copy-start | bytes 1572868
  71.2 6.2 %collective-permute-start.11 = (bf16[4,4,64,512]{3,2,1,0:T(8,128)(2,1)}, bf16[4,4,64,512]{3,2,1,0:T(8,128)(2,1)S(1)}, u32[]{:S(2)}, u32[]{:S(2)}) collective-permute-start(bf16[4,4,64,512]{3,2,1,0:T(8,128)(2,1)} %get-tuple-element.75), channel_id=1, source_target_pairs={{0,32},{32,0},{1,33},{33,1},{2,34},{34,2},{3,35},{35,3},{4,36},{36... | collective-permute-start | bytes 3145736 | tf_op jit(solution)/shard_map/ppermute | solution.py:43
  74.9 3.4 %collective-permute-start.12 = (bf16[8,64,576]{2,1,0:T(8,128)(2,1)S(1)}, bf16[8,64,576]{2,1,0:T(8,128)(2,1)S(1)}, u32[]{:S(2)}, u32[]{:S(2)}) collective-permute-start(bf16[8,64,576]{2,1,0:T(8,128)(2,1)S(1)} %all-to-all-done.near_ref.refs_3_), channel_id=1, source_target_pairs={{0,32},{32,0},{1,33},{33,1},{2,34},{34,2},{3,35},{35,3},{4,36},{36... | collective-permute-start | bytes 1769480 | tf_op jit(solution)/shard_map/ppermute | solution.py:43
  114.0 8.7 %collective-permute-start.13 = (bf16[64,576]{1,0:T(8,128)(2,1)}, bf16[64,576]{1,0:T(8,128)(2,1)S(1)}, u32[]{:S(2)}, u32[]{:S(2)}) collective-permute-start(bf16[64,576]{1,0:T(8,128)(2,1)} %get-tuple-element.80), channel_id=1, source_target_pairs={{0,1},{1,0},{2,3},{3,2},{4,5},{5,4},{6,7},{7,6},{8,9},{9,8},{10,11... | collective-permute-start | bytes 221192 | tf_op jit(solution)/shard_map/ppermute | solution.py:47
  114.3 11.3 %collective-permute-start.14 = (bf16[64,576]{1,0:T(8,128)(2,1)}, bf16[64,576]{1,0:T(8,128)(2,1)S(1)}, u32[]{:S(2)}, u32[]{:S(2)}) collective-permute-start(bf16[64,576]{1,0:T(8,128)(2,1)} %get-tuple-element.81), channel_id=1, source_target_pairs={{0,2},{1,3},{2,0},{3,1},{4,6},{5,7},{6,4},{7,5},{8,10},{9,11},{10,... | collective-permute-start | bytes 221192 | tf_op jit(solution)/shard_map/ppermute | solution.py:47
  115.6 10.4 %collective-permute-start.15 = (bf16[64,576]{1,0:T(8,128)(2,1)}, bf16[64,576]{1,0:T(8,128)(2,1)S(1)}, u32[]{:S(2)}, u32[]{:S(2)}) collective-permute-start(bf16[64,576]{1,0:T(8,128)(2,1)} %get-tuple-element.82), channel_id=1, source_target_pairs={{0,4},{4,0},{8,12},{12,8},{16,20},{20,16},{24,28},{28,24},{1,5},{5... | collective-permute-start | bytes 221192 | tf_op jit(solution)/shard_map/ppermute | solution.py:47
  116.8 11.6 %collective-permute-start.16 = (bf16[64,576]{1,0:T(8,128)(2,1)}, bf16[64,576]{1,0:T(8,128)(2,1)S(1)}, u32[]{:S(2)}, u32[]{:S(2)}) collective-permute-start(bf16[64,576]{1,0:T(8,128)(2,1)} %get-tuple-element.83), channel_id=1, source_target_pairs={{0,8},{4,12},{8,0},{12,4},{16,24},{20,28},{24,16},{28,20},{1,9},{5... | collective-permute-start | bytes 221192 | tf_op jit(solution)/shard_map/ppermute | solution.py:47
  118.9 9.5 %collective-permute-start.17 = (bf16[64,576]{1,0:T(8,128)(2,1)}, bf16[64,576]{1,0:T(8,128)(2,1)S(1)}, u32[]{:S(2)}, u32[]{:S(2)}) collective-permute-start(bf16[64,576]{1,0:T(8,128)(2,1)} %get-tuple-element.84), channel_id=1, source_target_pairs={{0,16},{4,20},{8,24},{12,28},{16,0},{20,4},{24,8},{28,12},{1,17},{... | collective-permute-start | bytes 221192 | tf_op jit(solution)/shard_map/ppermute | solution.py:47
  122.7 5.7 %collective-permute-start.18 = (bf16[64,576]{1,0:T(8,128)(2,1)}, bf16[64,576]{1,0:T(8,128)(2,1)S(1)}, u32[]{:S(2)}, u32[]{:S(2)}) collective-permute-start(bf16[64,576]{1,0:T(8,128)(2,1)} %get-tuple-element.85), channel_id=1, source_target_pairs={{0,32},{32,0},{1,33},{33,1},{2,34},{34,2},{3,35},{35,3},{4,36},{36... | collective-permute-start | bytes 221192 | tf_op jit(solution)/shard_map/ppermute | solution.py:47
  125.6 4.1 %collective-permute-start.19 = (bf16[64,576]{1,0:T(8,128)(2,1)}, bf16[64,576]{1,0:T(8,128)(2,1)S(1)}, u32[]{:S(2)}, u32[]{:S(2)}) collective-permute-start(bf16[64,576]{1,0:T(8,128)(2,1)} %get-tuple-element.86), channel_id=1, source_target_pairs={{0,64},{64,0},{128,192},{192,128},{1,65},{65,1},{129,193},{193,129... | collective-permute-start | bytes 221192 | tf_op jit(solution)/shard_map/ppermute | solution.py:47
  126.0 6.2 %collective-permute-start.20 = (bf16[64,576]{1,0:T(8,128)(2,1)}, bf16[64,576]{1,0:T(8,128)(2,1)S(1)}, u32[]{:S(2)}, u32[]{:S(2)}) collective-permute-start(bf16[64,576]{1,0:T(8,128)(2,1)} %get-tuple-element.87), channel_id=1, source_target_pairs={{0,128},{64,192},{128,0},{192,64},{1,129},{65,193},{129,1},{193,65... | collective-permute-start | bytes 221192 | tf_op jit(solution)/shard_map/ppermute | solution.py:47
  160.3 4.6 %collective-permute-start.21 = (bf16[8,72,640]{2,1,0:T(8,128)(2,1)S(1)}, bf16[8,72,640]{2,1,0:T(8,128)(2,1)S(1)}, u32[]{:S(2)}, u32[]{:S(2)}) collective-permute-start(bf16[8,72,640]{2,1,0:T(8,128)(2,1)S(1)} %all_to_all.41.near_ref.refs_1_), channel_id=1, source_target_pairs={{0,32},{32,0},{1,33},{33,1},{2,34},{34,2},{3,35},{35,3},{4,36},{36... | collective-permute-start | bytes 2211848 | tf_op jit(solution)/shard_map/ppermute | solution.py:43
  173.1 32.9 %all-to-all-start.3 = ((bf16[16,88,576]{2,1,0:T(8,128)(2,1)}), bf16[16,88,576]{2,1,0:T(8,128)(2,1)S(1)}, u32[]{:S(2)}, u32[]{:S(2)}) async-start(bf16[16,88,576]{2,1,0:T(8,128)(2,1)} %get-tuple-element.90), calls=%async_computation.3 | async-start | bytes 3604480 | tf_op jit(solution)/shard_map/all_to_all | solution.py:38
  211.1 43.2 %copy-start.20 = (f32[64,64]{1,0:T(8,128)S(1)}, f32[64,64]{1,0:T(8,128)}, u32[]{:S(2)}) copy-start(f32[64,64]{1,0:T(8,128)} %slice.102.refs_8_) | copy-start | bytes 49156
  211.1 43.2 %copy-start.10 = (f32[64,576]{1,0:T(8,128)S(1)}, f32[64,576]{1,0:T(8,128)}, u32[]{:S(2)}) copy-start(f32[64,576]{1,0:T(8,128)} %get-tuple-element.88.field_ref) | copy-start | bytes 442372
  211.1 43.4 %copy-start.19 = (f32[64,64]{1,0:T(8,128)S(1)}, f32[64,64]{1,0:T(8,128)}, u32[]{:S(2)}) copy-start(f32[64,64]{1,0:T(8,128)} %slice.104.refs_8_) | copy-start | bytes 49156
  211.1 43.5 %copy-start.50 = (f32[64,64]{1,0:T(8,128)S(1)}, f32[64,64]{1,0:T(8,128)}, u32[]{:S(2)}) copy-start(f32[64,64]{1,0:T(8,128)} %get-tuple-element.92) | copy-start | bytes 49156
  211.1 3.4 %collective-permute-start.22 = (bf16[64,512]{1,0:T(8,128)(2,1)}, bf16[64,512]{1,0:T(8,128)(2,1)S(1)}, u32[]{:S(2)}, u32[]{:S(2)}) collective-permute-start(bf16[64,512]{1,0:T(8,128)(2,1)} %get-tuple-element.95), channel_id=1, source_target_pairs={{0,1},{1,0},{2,3},{3,2},{4,5},{5,4},{6,7},{7,6},{8,9},{9,8},{10,11... | collective-permute-start | bytes 196616 | tf_op jit(solution)/shard_map/ppermute | solution.py:47
  211.2 5.9 %collective-permute-start.23 = (bf16[64,512]{1,0:T(8,128)(2,1)}, bf16[64,512]{1,0:T(8,128)(2,1)S(1)}, u32[]{:S(2)}, u32[]{:S(2)}) collective-permute-start(bf16[64,512]{1,0:T(8,128)(2,1)} %get-tuple-element.96), channel_id=1, source_target_pairs={{0,2},{1,3},{2,0},{3,1},{4,6},{5,7},{6,4},{7,5},{8,10},{9,11},{10,... | collective-permute-start | bytes 196616 | tf_op jit(solution)/shard_map/ppermute | solution.py:47
  211.4 6.1 %collective-permute-start.24 = (bf16[64,512]{1,0:T(8,128)(2,1)}, bf16[64,512]{1,0:T(8,128)(2,1)S(1)}, u32[]{:S(2)}, u32[]{:S(2)}) collective-permute-start(bf16[64,512]{1,0:T(8,128)(2,1)} %get-tuple-element.97), channel_id=1, source_target_pairs={{0,4},{4,0},{8,12},{12,8},{16,20},{20,16},{24,28},{28,24},{1,5},{5... | collective-permute-start | bytes 196616 | tf_op jit(solution)/shard_map/ppermute | solution.py:47
  211.7 8.8 %collective-permute-start.25 = (bf16[64,512]{1,0:T(8,128)(2,1)}, bf16[64,512]{1,0:T(8,128)(2,1)S(1)}, u32[]{:S(2)}, u32[]{:S(2)}) collective-permute-start(bf16[64,512]{1,0:T(8,128)(2,1)} %get-tuple-element.98), channel_id=1, source_target_pairs={{0,8},{4,12},{8,0},{12,4},{16,24},{20,28},{24,16},{28,20},{1,9},{5... | collective-permute-start | bytes 196616 | tf_op jit(solution)/shard_map/ppermute | solution.py:47
  211.8 8.7 %collective-permute-start.26 = (bf16[64,512]{1,0:T(8,128)(2,1)}, bf16[64,512]{1,0:T(8,128)(2,1)S(1)}, u32[]{:S(2)}, u32[]{:S(2)}) collective-permute-start(bf16[64,512]{1,0:T(8,128)(2,1)} %get-tuple-element.99), channel_id=1, source_target_pairs={{0,16},{4,20},{8,24},{12,28},{16,0},{20,4},{24,8},{28,12},{1,17},{... | collective-permute-start | bytes 196616 | tf_op jit(solution)/shard_map/ppermute | solution.py:47
  214.5 5.9 %collective-permute-start.27 = (bf16[64,512]{1,0:T(8,128)(2,1)}, bf16[64,512]{1,0:T(8,128)(2,1)S(1)}, u32[]{:S(2)}, u32[]{:S(2)}) collective-permute-start(bf16[64,512]{1,0:T(8,128)(2,1)} %get-tuple-element.100), channel_id=1, source_target_pairs={{0,32},{32,0},{1,33},{33,1},{2,34},{34,2},{3,35},{35,3},{4,36},{36... | collective-permute-start | bytes 196616 | tf_op jit(solution)/shard_map/ppermute | solution.py:47
  217.2 3.6 %collective-permute-start.28 = (bf16[64,512]{1,0:T(8,128)(2,1)}, bf16[64,512]{1,0:T(8,128)(2,1)S(1)}, u32[]{:S(2)}, u32[]{:S(2)}) collective-permute-start(bf16[64,512]{1,0:T(8,128)(2,1)} %get-tuple-element.101), channel_id=1, source_target_pairs={{0,64},{64,0},{128,192},{192,128},{1,65},{65,1},{129,193},{193,129... | collective-permute-start | bytes 196616 | tf_op jit(solution)/shard_map/ppermute | solution.py:47
  217.5 4.9 %collective-permute-start.29 = (bf16[64,512]{1,0:T(8,128)(2,1)}, bf16[64,512]{1,0:T(8,128)(2,1)S(1)}, u32[]{:S(2)}, u32[]{:S(2)}) collective-permute-start(bf16[64,512]{1,0:T(8,128)(2,1)} %get-tuple-element.102), channel_id=1, source_target_pairs={{0,128},{64,192},{128,0},{192,64},{1,129},{65,193},{129,1},{193,65... | collective-permute-start | bytes 196616 | tf_op jit(solution)/shard_map/ppermute | solution.py:47
  251.6 4.5 %collective-permute-start.30 = (bf16[8,88,512]{2,1,0:T(8,128)(2,1)S(1)}, bf16[8,88,512]{2,1,0:T(8,128)(2,1)S(1)}, u32[]{:S(2)}, u32[]{:S(2)}) collective-permute-start(bf16[8,88,512]{2,1,0:T(8,128)(2,1)S(1)} %all_to_all.42.near_ref), channel_id=1, source_target_pairs={{0,32},{32,0},{1,33},{33,1},{2,34},{34,2},{3,35},{35,3},{4,36},{36... | collective-permute-start | bytes 2162696 | tf_op jit(solution)/shard_map/ppermute | solution.py:43
  264.5 22.0 %all-to-all-start.5 = ((bf16[16,64,512]{2,1,0:T(8,128)(2,1)}), bf16[16,64,512]{2,1,0:T(8,128)(2,1)S(1)}, u32[]{:S(2)}, u32[]{:S(2)}) async-start(bf16[16,64,512]{2,1,0:T(8,128)(2,1)} %get-tuple-element.108), calls=%async_computation.5 | async-start | bytes 2097152 | tf_op jit(solution)/shard_map/all_to_all | solution.py:38
  271.0 18.8 %copy-start.11 = (f32[64,576]{1,0:T(8,128)S(1)}, f32[64,576]{1,0:T(8,128)}, u32[]{:S(2)}) copy-start(f32[64,576]{1,0:T(8,128)} %get-tuple-element.79.field_ref) | copy-start | bytes 442372
  271.0 18.8 %copy-start.14 = (f32[64,512]{1,0:T(8,128)S(1)}, f32[64,512]{1,0:T(8,128)}, u32[]{:S(2)}) copy-start(f32[64,512]{1,0:T(8,128)} %get-tuple-element.94.field_ref) | copy-start | bytes 393220
  271.0 18.8 %copy-start.15 = (f32[64,512]{1,0:T(8,128)S(1)}, f32[64,512]{1,0:T(8,128)}, u32[]{:S(2)}) copy-start(f32[64,512]{1,0:T(8,128)} %get-tuple-element.107.field_ref) | copy-start | bytes 393220
  271.0 18.8 %copy-start.18 = (f32[64,576]{1,0:T(8,128)S(1)}, f32[64,576]{1,0:T(8,128)}, u32[]{:S(2)}) copy-start(f32[64,576]{1,0:T(8,128)} %get-tuple-element.69.field_ref) | copy-start | bytes 442372
  289.8 27.1 %copy-start.51 = (s32[512]{0:T(512)S(1)}, s32[512]{0:T(512)}, u32[]{:S(2)}) copy-start(s32[512]{0:T(512)} %param.15) | copy-start | bytes 6148
  289.9 27.2 %copy-start.16 = (f32[64,512]{1,0:T(8,128)S(1)}, f32[64,512]{1,0:T(8,128)}, u32[]{:S(2)}) copy-start(f32[64,512]{1,0:T(8,128)} %shard_map.103) | copy-start | bytes 393220
  (43 other events, 150.0 us)

commit v2 on v1

--- a/solution.py
+++ b/solution.py
@@ -94,7 +94,7 @@
     )
 
 
-def rearranged(blocks):
+def rearranged(blocks, ready):
     n_y, n_c, _, n_x = (lax.axis_size(name) for name in HI_LO)
     _, rows, depth = blocks[0].shape
     me = jnp.stack([lax.axis_index("x"), lax.axis_index("c")]).astype(jnp.int32)
@@ -105,7 +105,8 @@
         [me, *arrived],
         1,
     )
-    return kept.reshape(-1, depth), shifted(other, "c", 1).reshape(-1, depth)
+    other, *ready = lax.optimization_barrier((other, *ready))
+    return (kept.reshape(-1, depth), shifted(other, "c", 1).reshape(-1, depth)), ready
 
 
 def times_kernel(rows, width, share, rank, me_ref, g_near_ref, g_far_ref, near_ref, far_ref, *refs):
@@ -300,7 +301,7 @@
 
     def precondition(field, sent, cuts=None, inside=False, beside=None, below=None):
         far = [("x", 1), ("x", 2), ("z", 1), ("z", 2), ("z", 4), ("c", 1), ("y", 1), ("y", 2)]
-        order = [5, 0, 6, 2, 1, 7, 3, 4]
+        order = [4, 3, 7, 1, 2, 6, 0, 5]
         arrived = {bit: from_partner(sent[bit], *far[bit]) for bit in order}
         extra = [array for array in (beside, below) if array is not None]
         more_rows = 0 if below is None else below.shape[0]
@@ -320,7 +321,13 @@
     places = jnp.stack([me_rows, me_columns]).astype(jnp.int32)
     right_sides, *blocks = lax.optimization_barrier((right_sides, *cut_by_x(grm)))
     sent = kernel_call(coefficients_kernel, coefficient_shapes(rhs), [right_sides, basis_terms])
-    g_blocks = rearranged(blocks)
+    share = rank // n_columns
+    t_share = rank // n_rows
+    t_parts = mm3(coarse_basis.T, right_sides).reshape(n_rows, t_share, rhs)
+    t_top = lax.reduce_precision(t_parts, 8, 7)
+    t_parts = jnp.concatenate([t_top, t_parts - t_top], axis=1).astype(BF16)
+    t_parts = jnp.pad(t_parts, ((0, 0), (0, 0), (0, rank)))
+    g_blocks, (t_parts, places) = rearranged(blocks, (t_parts, places))
 
     def gathered(copies):
         near = exchanged(copies, "z")
@@ -328,7 +335,7 @@
 
     def products(everyone, width, riders=(), more_rows=0, share=0):
         depth = lax.axis_size("z") * rows
-        per_step = n_rows // 4
+        per_step = n_rows // 2
         height = rows + more_rows
 
         def whole(array):
@@ -342,7 +349,7 @@
             rider_specs = [some((per_step, *riders[0].shape[1:]))]
         partial, own = pl.pallas_call(
             functools.partial(times_kernel, rows, width, share, rank),
-            grid=(4,),
+            grid=(2,),
             out_shape=[
                 jax.ShapeDtypeStruct((n_rows, height, width), BF16),
                 jax.ShapeDtypeStruct((rows, width), F32),
@@ -392,13 +399,6 @@
         more = width - array.shape[-1]
         return jnp.pad(array, [(0, 0)] * (array.ndim - 1) + [(0, more)])
 
-    share = rank // n_columns
-    t_share = rank // n_rows
-    t_parts = mm3(coarse_basis.T, right_sides).reshape(n_rows, t_share, rhs)
-    t_top = lax.reduce_precision(t_parts, 8, 7)
-    t_parts = jnp.concatenate([t_top, t_parts - t_top], axis=1).astype(BF16)
-    t_parts = padded(t_parts, width)
-
     cuts = [(0, rhs)]
     first, copies = precondition(right_sides, sent, cuts, True, beside=coarse_basis)
     all_first = gathered(copies)

time: 319 us -> 306 us (0.959)
  waiting for transfers between devices: 75.5 us -> 65.8 us
  starting transfers between devices: 65.6 us -> 61.1 us
    ppermute x7, waiting for transfers between devices: 25.8 us -> 18.3 us  [shifted(): lax.ppermute(value, axis, [(i, (i + step) % size) for i in range(size)])]
    ppermute x24, starting transfers between devices: 39.7 us -> 35.5 us  [from_partner(): lax.ppermute(value, axis, [(i, i ^ distance) for i in range(lax.axis_size...]
  transfers between devices with their start and end apart: 34 -> 34, of which waited for: 15 -> 15; matrix products, arithmetic and copies ran while one was open for 4% -> 4% of each run, Pallas kernels for 1% -> 2%
where the time goes in v2:
time: 306 us; the launch traced here: 304 us
  blocking collectives  104 us (34%)
  waiting for transfers between devices  65.8 us (22%)
  starting transfers between devices  61.1 us (20%)
  Pallas kernels  42.8 us (14%)
  local copies, waits for them, and re-layouts  14 us (5%)
  other arithmetic  9.09 us (3%)
  matrix products  5.55 us (2%)
    all_to_all x3, blocking collectives, exchanged(): return lax.all_to_all(array, axes, split_axis=0, concat_axis=0, tiled=True)  78.2 us
    all_to_all x3, waiting for transfers between devices, exchanged(): return lax.all_to_all(array, axes, split_axis=0, concat_axis=0, tiled=True)  40.4 us
    ppermute x24, starting transfers between devices, from_partner(): lax.ppermute(value, axis, [(i, i ^ distance) for i in range(lax.axis_size...  35.5 us
    pallas_call x9, Pallas kernels, kernel_call(): pl.pallas_call(kernel, out_shape=[jax.ShapeDtypeStruct(shape, dtype) for...  26.9 us
    all_to_all x2, blocking collectives, from_everyone(): return lax.all_to_all(copies, axes, split_axis=0, concat_axis=0, tiled=True)  25.8 us
    ppermute x7, waiting for transfers between devices, shifted(): lax.ppermute(value, axis, [(i, (i + step) % size) for i in range(size)])  18.3 us
    pallas_call x3, Pallas kernels, products(): pl.pallas_call(functools.partial(times_kernel, rows, width, share, rank),...  15.9 us
    all_to_all x3, starting transfers between devices, exchanged(): return lax.all_to_all(array, axes, split_axis=0, concat_axis=0, tiled=True)  14.5 us
  transfers between devices with their start and end apart: 34, of which 15 were waited for; matrix products, arithmetic and copies ran while one was open for 4% of the time, Pallas kernels for 2%

profile of v2, /device:TPU:1, one launch (start us, length us, event | category | flops | bytes accessed | tf_op | source)
XLA Modules:
  0.0 304.4 jit_solution(4664346874297495649)
XLA Ops:
  0.7 4.3 %shard_map.95 = (bf16[8,64,512]{2,1,0:T(8,128)(2,1)}, bf16[8,64,512]{2,1,0:T(8,128)(2,1)}, bf16[8,64,512]{2,1,0:T(8,128)(2,1)}, bf16[8,64,512]{2,1,0:T(8,128)(2,1)}) custom-call(s32[1]{0:T(128)} %bitcast.me_ref, bf16[8,64,2048]{2,1,0:T(8,128)(2,1)} %bitcast.55), custom_call_target="tpu_custom_call" | custom-call | tf_op jit(solution)/shard_map/pallas_call | solution.py:255
  6.7 2.0 shard_map.96
  8.7 2.0 collective-permute-start
  10.7 2.4 collective-permute-start.1
  13.1 1.6 collective-permute-start.2
  14.8 3.0 collective-permute-start.3
  17.8 4.2 %collective-permute-start.4 = (bf16[64,512]{1,0:T(8,128)(2,1)}, bf16[64,512]{1,0:T(8,128)(2,1)S(1)}, u32[]{:S(2)}, u32[]{:S(2)}) collective-permute-start(bf16[64,512]{1,0:T(8,128)(2,1)} %get-tuple-element.68), channel_id=1, source_target_pairs={{0,16},{4,20},{8,24},{12,28},{16,0},{20,4},{24,8},{28,12},{1,17},{... | collective-permute-start | bytes 196616 | tf_op jit(solution)/shard_map/ppermute | solution.py:47
  26.2 2.2 collective-permute-start.5
  28.4 1.4 collective-permute-start.6
  29.8 2.7 collective-permute-start.7
  33.4 1.3 collective-permute-start.8
  36.6 2.7 shard_map.97
  39.3 3.5 %all-to-all-start = ((bf16[8,64,576]{2,1,0:T(8,128)(2,1)}), bf16[8,64,576]{2,1,0:T(8,128)(2,1)S(1)}, u32[]{:S(2)}, u32[]{:S(2)}) async-start(bf16[8,64,576]{2,1,0:T(8,128)(2,1)} %get-tuple-element.81), calls=%async_computation | async-start | bytes 1310720 | tf_op jit(solution)/shard_map/all_to_all | solution.py:38
  46.3 2.0 collective-permute-done.8.refs_1_
  48.3 9.5 %collective-permute-done.9.refs_2_ = bf16[8,64,512]{2,1,0:T(8,128)(2,1)S(1)} collective-permute-done((bf16[8,64,512]{2,1,0:T(8,128)(2,1)}, bf16[8,64,512]{2,1,0:T(8,128)(2,1)S(1)}, u32[]{:S(2)}, u32[]{:S(2)}) %collective-permute-start.9) | collective-permute-done | bytes 524320 | tf_op jit(solution)/shard_map/ppermute | solution.py:43
  58.6 3.0 shard_map.98
  61.6 3.4 %collective-permute-start.11 = (bf16[4,4,64,512]{3,2,1,0:T(8,128)(2,1)}, bf16[4,4,64,512]{3,2,1,0:T(8,128)(2,1)S(1)}, u32[]{:S(2)}, u32[]{:S(2)}) collective-permute-start(bf16[4,4,64,512]{3,2,1,0:T(8,128)(2,1)} %get-tuple-element.80), channel_id=1, source_target_pairs={{0,32},{32,0},{1,33},{33,1},{2,34},{34,2},{3,35},{35,3},{4,36},{36... | collective-permute-start | bytes 3145736 | tf_op jit(solution)/shard_map/ppermute | solution.py:43
  65.3 2.2 collective-permute-done.11
  69.3 5.0 %times.3 = (bf16[16,72,576]{2,1,0:T(8,128)(2,1)}, f32[64,576]{1,0:T(8,128)}) custom-call(s32[2]{0:T(128)} %pad_add_fusion.1.me_ref, bf16[1024,512]{1,0:T(8,128)(2,1)} %bitcast.49, bf16[1024,512]{1,0:T(8,128)(2,1)} %bitcast.52, bf16[8,64,576]{2,1,0:T(8,128)(2,1)} %copy-done.4, bf16[8,64,576]{2,1,0:T(8,128)(2,1)} %copy-done.9, bf16[16,8,576]{2,1,0:T(8,128)(2,1)} %fusion.13.refs_0_), custom_call_target="tpu_custom_call" | custom-call | tf_op jit(solution)/shard_map/times/pallas_call | solution.py:350
  74.3 24.9 %all_to_all.40.arrived_ref = bf16[16,72,576]{2,1,0:T(8,128)(2,1)S(1)} all-to-all(bf16[16,72,576]{2,1,0:T(8,128)(2,1)} %get-tuple-element.83), channel_id=1, replica_groups=mesh['y'=4,'c'=2,'z'=8,'x'=4] {'y','x'}, dimensions={0} | all-to-all | bytes 2654208 | tf_op jit(solution)/shard_map/all_to_all | solution.py:38
  100.2 3.1 %shard_map.99 = (f32[64,576]{1,0:T(8,128)}, bf16[64,576]{1,0:T(8,128)(2,1)}, bf16[64,576]{1,0:T(8,128)(2,1)}, bf16[64,576]{1,0:T(8,128)(2,1)}, bf16[64,576]{1,0:...) custom-call(s32[2]{0:T(128)} %pad_add_fusion.1.me_ref, ...), custom_call_target="tpu_custom_call" | custom-call | tf_op jit(solution)/shard_map/pallas_call | solution.py:255
  103.7 1.2 collective-permute-start.14
  106.8 1.4 slice.104.refs_8_
  108.2 2.6 collective-permute-start.18
  111.1 1.8 collective-permute-start.20
  114.6 2.4 collective-permute-done.20.refs_7_
  117.7 2.9 shard_map.100
  120.7 27.5 %all_to_all.41.near_ref.refs_1_ = bf16[8,72,640]{2,1,0:T(8,128)(2,1)S(1)} all-to-all(bf16[8,72,640]{2,1,0:T(8,128)(2,1)} %get-tuple-element.95), channel_id=1, replica_groups=mesh['y'=4,'c'=2,'z'=8,'x'=4] {'z'}, dimensions={0} | all-to-all | bytes 1474560 | tf_op jit(solution)/shard_map/all_to_all | solution.py:38
  148.2 2.7 collective-permute-start.21
  150.9 1.8 collective-permute-done.21.far_ref.refs_2_
  153.6 6.8 %times.4 = (bf16[16,88,576]{2,1,0:T(8,128)(2,1)}, f32[64,576]{1,0:T(8,128)}) custom-call(s32[2]{0:T(128)} %pad_add_fusion.1.me_ref, bf16[1024,512]{1,0:T(8,128)(2,1)} %bitcast.50, bf16[1024,512]{1,0:T(8,128)(2,1)} %bitcast.53, bf16[8,72,640]{2,1,0:T(8,128)(2,1)} %copy-done.2, bf16[8,72,640]{2,1,0:T(8,128)(2,1)} %copy-done.7, f32[4,576]{1,0:T(4,128)} %fusion.20.refs_0_, ...), custom_call_target="tpu_custom_call" | custom-call | tf_op jit(solution)/shard_map/times/pallas_call | solution.py:350
  160.4 5.3 %all-to-all-start.3 = ((bf16[16,88,576]{2,1,0:T(8,128)(2,1)}), bf16[16,88,576]{2,1,0:T(8,128)(2,1)S(1)}, u32[]{:S(2)}, u32[]{:S(2)}) async-start(bf16[16,88,576]{2,1,0:T(8,128)(2,1)} %get-tuple-element.96), calls=%async_computation.3 | async-start | bytes 3604480 | tf_op jit(solution)/shard_map/all_to_all | solution.py:38
  166.3 27.0 %all-to-all-done.3.arrived_ref = bf16[16,88,576]{2,1,0:T(8,128)(2,1)S(1)} async-done(((bf16[16,88,576]{2,1,0:T(8,128)(2,1)}), bf16[16,88,576]{2,1,0:T(8,128)(2,1)S(1)}, u32[]{:S(2)}, u32[]{:S(2)}) %all-to-all-start.3) | async-done | bytes 1622048 | tf_op jit(solution)/shard_map/all_to_all | solution.py:38
  194.7 3.7 %shard_map.101 = (f32[64,512]{1,0:T(8,128)}, f32[64,64]{1,0:T(8,128)}, f32[64,512]{1,0:T(8,128)}, bf16[64,512]{1,0:T(8,128)(2,1)}, bf16[64,512]{1,0:T(8,128)(2,1...) custom-call(s32[2]{0:T(128)} %pad_add_fusion.1.me_ref, ...), custom_call_target="tpu_custom_call" | custom-call | tf_op jit(solution)/shard_map/pallas_call | solution.py:255
  199.1 1.8 collective-permute-start.26
  201.8 2.6 collective-permute-start.27
  204.8 2.4 collective-permute-start.29
  208.1 1.6 collective-permute-done.29.refs_7_
  210.3 2.7 shard_map.102
  213.1 25.8 %all_to_all.42.near_ref = bf16[8,88,512]{2,1,0:T(8,128)(2,1)S(1)} all-to-all(bf16[8,88,512]{2,1,0:T(8,128)(2,1)} %get-tuple-element.109), channel_id=1, replica_groups=mesh['y'=4,'c'=2,'z'=8,'x'=4] {'z'}, dimensions={0} | all-to-all | bytes 1441792 | tf_op jit(solution)/shard_map/all_to_all | solution.py:38
  238.9 2.7 collective-permute-start.30
  244.3 4.1 %times.5 = (bf16[16,64,512]{2,1,0:T(8,128)(2,1)}, f32[64,512]{1,0:T(8,128)}) custom-call(s32[2]{0:T(128)} %pad_add_fusion.1.me_ref, bf16[1024,512]{1,0:T(8,128)(2,1)} %bitcast.51, bf16[1024,512]{1,0:T(8,128)(2,1)} %bitcast.54, bf16[8,88,512]{2,1,0:T(8,128)(2,1)} %copy-done.6, bf16[8,88,512]{2,1,0:T(8,128)(2,1)} %copy-done.17), custom_call_target="tpu_custom_call" | custom-call | tf_op jit(solution)/shard_map/times/pallas_call | solution.py:350
  250.9 5.7 %all-to-all-start.5 = ((bf16[16,64,512]{2,1,0:T(8,128)(2,1)}), bf16[16,64,512]{2,1,0:T(8,128)(2,1)S(1)}, u32[]{:S(2)}, u32[]{:S(2)}) async-start(bf16[16,64,512]{2,1,0:T(8,128)(2,1)} %get-tuple-element.114), calls=%async_computation.5 | async-start | bytes 2097152 | tf_op jit(solution)/shard_map/all_to_all | solution.py:38
  258.0 1.5 fusion.4
  259.5 13.4 %all-to-all-done.5.arrived_ref = bf16[16,64,512]{2,1,0:T(8,128)(2,1)S(1)} async-done(((bf16[16,64,512]{2,1,0:T(8,128)(2,1)}), bf16[16,64,512]{2,1,0:T(8,128)(2,1)S(1)}, u32[]{:S(2)}, u32[]{:S(2)}) %all-to-all-start.5) | async-done | bytes 1048608 | tf_op jit(solution)/shard_map/all_to_all | solution.py:38
  273.9 2.4 shard_map.103
  277.5 12.3 %all_to_all.43 = f32[16,6,512]{2,1,0:T(8,128)S(1)} all-to-all(f32[16,6,512]{2,1,0:T(8,128)S(1)} %broadcast_in_dim.49), channel_id=1, replica_groups=mesh['y'=4,'c'=2,'z'=8,'x'=4] {'y','x'}, dimensions={0} | all-to-all | bytes 393216 | tf_op jit(solution)/shard_map/all_to_all | solution.py:34
  289.9 13.5 %all_to_all.44 = f32[16,6,512]{2,1,0:T(8,128)S(1)} all-to-all(f32[16,6,512]{2,1,0:T(8,128)S(1)} %broadcast_in_dim.50), channel_id=1, replica_groups=mesh['y'=4,'c'=2,'z'=8,'x'=4] {'c','z'}, dimensions={0} | all-to-all | bytes 393216 | tf_op jit(solution)/shard_map/all_to_all | solution.py:34
  (231 shorter events, 36.1 us)
Async XLA Ops:
  4.9 17.1 %copy-start.13 = (f32[9,64,64]{2,1,0:T(8,128)S(1)}, f32[9,64,64]{2,1,0:T(8,128)}, u32[]{:S(2)}) copy-start(f32[9,64,64]{2,1,0:T(8,128)} %param.12) | copy-start | bytes 442372
  8.7 17.6 %collective-permute-start = (bf16[64,512]{1,0:T(8,128)(2,1)}, bf16[64,512]{1,0:T(8,128)(2,1)S(1)}, u32[]{:S(2)}, u32[]{:S(2)}) collective-permute-start(bf16[64,512]{1,0:T(8,128)(2,1)} %get-tuple-element.64), channel_id=1, source_target_pairs={{0,1},{1,0},{2,3},{3,2},{4,5},{5,4},{6,7},{7,6},{8,9},{9,8},{10,11... | collective-permute-start | bytes 196616 | tf_op jit(solution)/shard_map/ppermute | solution.py:47
  10.7 17.7 %collective-permute-start.1 = (bf16[64,512]{1,0:T(8,128)(2,1)}, bf16[64,512]{1,0:T(8,128)(2,1)S(1)}, u32[]{:S(2)}, u32[]{:S(2)}) collective-permute-start(bf16[64,512]{1,0:T(8,128)(2,1)} %get-tuple-element.65), channel_id=1, source_target_pairs={{0,2},{1,3},{2,0},{3,1},{4,6},{5,7},{6,4},{7,5},{8,10},{9,11},{10,... | collective-permute-start | bytes 196616 | tf_op jit(solution)/shard_map/ppermute | solution.py:47
  13.1 16.7 %collective-permute-start.2 = (bf16[64,512]{1,0:T(8,128)(2,1)}, bf16[64,512]{1,0:T(8,128)(2,1)S(1)}, u32[]{:S(2)}, u32[]{:S(2)}) collective-permute-start(bf16[64,512]{1,0:T(8,128)(2,1)} %get-tuple-element.66), channel_id=1, source_target_pairs={{0,4},{4,0},{8,12},{12,8},{16,20},{20,16},{24,28},{28,24},{1,5},{5... | collective-permute-start | bytes 196616 | tf_op jit(solution)/shard_map/ppermute | solution.py:47
  14.8 18.4 %collective-permute-start.3 = (bf16[64,512]{1,0:T(8,128)(2,1)}, bf16[64,512]{1,0:T(8,128)(2,1)S(1)}, u32[]{:S(2)}, u32[]{:S(2)}) collective-permute-start(bf16[64,512]{1,0:T(8,128)(2,1)} %get-tuple-element.67), channel_id=1, source_target_pairs={{0,8},{4,12},{8,0},{12,4},{16,24},{20,28},{24,16},{28,20},{1,9},{5... | collective-permute-start | bytes 196616 | tf_op jit(solution)/shard_map/ppermute | solution.py:47
  17.8 15.6 %collective-permute-start.4 = (bf16[64,512]{1,0:T(8,128)(2,1)}, bf16[64,512]{1,0:T(8,128)(2,1)S(1)}, u32[]{:S(2)}, u32[]{:S(2)}) collective-permute-start(bf16[64,512]{1,0:T(8,128)(2,1)} %get-tuple-element.68), channel_id=1, source_target_pairs={{0,16},{4,20},{8,24},{12,28},{16,0},{20,4},{24,8},{28,12},{1,17},{... | collective-permute-start | bytes 196616 | tf_op jit(solution)/shard_map/ppermute | solution.py:47
  24.4 18.5 %copy-start.8 = (f32[64,512]{1,0:T(8,128)S(1)}, f32[64,512]{1,0:T(8,128)}, u32[]{:S(2)}) copy-start(f32[64,512]{1,0:T(8,128)} %field_ref.1) | copy-start | bytes 393220
  26.2 9.7 %copy-start.42 = (bf16[64,512]{1,0:T(8,128)(2,1)}, bf16[64,512]{1,0:T(8,128)(2,1)S(1)}, u32[]{:S(2)}) copy-start(bf16[64,512]{1,0:T(8,128)(2,1)S(1)} %collective-permute-done.refs_0_) | copy-start | bytes 196612
  26.2 8.4 %collective-permute-start.5 = (bf16[64,512]{1,0:T(8,128)(2,1)S(1)}, bf16[64,512]{1,0:T(8,128)(2,1)S(1)}, u32[]{:S(2)}, u32[]{:S(2)}) collective-permute-start(bf16[64,512]{1,0:T(8,128)(2,1)S(1)} %copy-done.54), channel_id=1, source_target_pairs={{0,32},{32,0},{1,33},{33,1},{2,34},{34,2},{3,35},{35,3},{4,36},{36... | collective-permute-start | bytes 196616 | tf_op jit(solution)/shard_map/ppermute | solution.py:47
  28.4 6.8 %collective-permute-start.6 = (bf16[64,512]{1,0:T(8,128)(2,1)S(1)}, bf16[64,512]{1,0:T(8,128)(2,1)S(1)}, u32[]{:S(2)}, u32[]{:S(2)}) collective-permute-start(bf16[64,512]{1,0:T(8,128)(2,1)S(1)} %copy-done.53), channel_id=1, source_target_pairs={{0,64},{64,0},{128,192},{192,128},{1,65},{65,1},{129,193},{193,129... | collective-permute-start | bytes 196616 | tf_op jit(solution)/shard_map/ppermute | solution.py:47
  29.8 6.2 %collective-permute-start.7 = (bf16[64,512]{1,0:T(8,128)(2,1)S(1)}, bf16[64,512]{1,0:T(8,128)(2,1)S(1)}, u32[]{:S(2)}, u32[]{:S(2)}) collective-permute-start(bf16[64,512]{1,0:T(8,128)(2,1)S(1)} %copy-done.52), channel_id=1, source_target_pairs={{0,128},{64,192},{128,0},{192,64},{1,129},{65,193},{129,1},{193,65... | collective-permute-start | bytes 196616 | tf_op jit(solution)/shard_map/ppermute | solution.py:47
  33.2 13.1 %collective-permute-start.10 = (bf16[8,64,512]{2,1,0:T(8,128)(2,1)}, bf16[8,64,512]{2,1,0:T(8,128)(2,1)S(1)}, u32[]{:S(2)}, u32[]{:S(2)}) collective-permute-start(bf16[8,64,512]{2,1,0:T(8,128)(2,1)} %get-tuple-element.76), channel_id=1, source_target_pairs={{0,3},{1,0},{2,1},{3,2},{4,7},{5,4},{6,5},{7,6},{8,11},{9,8},{10,9... | collective-permute-start | bytes 1572872 | tf_op jit(solution)/shard_map/ppermute | solution.py:43
  33.4 14.9 %collective-permute-start.8 = (bf16[8,64,512]{2,1,0:T(8,128)(2,1)}, bf16[8,64,512]{2,1,0:T(8,128)(2,1)S(1)}, u32[]{:S(2)}, u32[]{:S(2)}) collective-permute-start(bf16[8,64,512]{2,1,0:T(8,128)(2,1)} %get-tuple-element.74), channel_id=1, source_target_pairs={{0,1},{1,2},{2,3},{3,0},{4,5},{5,6},{6,7},{7,4},{8,9},{9,10},{10,1... | collective-permute-start | bytes 1572872 | tf_op jit(solution)/shard_map/ppermute | solution.py:43
  34.6 23.1 %collective-permute-start.9 = (bf16[8,64,512]{2,1,0:T(8,128)(2,1)}, bf16[8,64,512]{2,1,0:T(8,128)(2,1)S(1)}, u32[]{:S(2)}, u32[]{:S(2)}) collective-permute-start(bf16[8,64,512]{2,1,0:T(8,128)(2,1)} %get-tuple-element.75), channel_id=1, source_target_pairs={{0,2},{1,3},{2,0},{3,1},{4,6},{5,7},{6,4},{7,5},{8,10},{9,11},{10,... | collective-permute-start | bytes 1572872 | tf_op jit(solution)/shard_map/ppermute | solution.py:43
  39.3 25.7 %all-to-all-start = ((bf16[8,64,576]{2,1,0:T(8,128)(2,1)}), bf16[8,64,576]{2,1,0:T(8,128)(2,1)S(1)}, u32[]{:S(2)}, u32[]{:S(2)}) async-start(bf16[8,64,576]{2,1,0:T(8,128)(2,1)} %get-tuple-element.81), calls=%async_computation | async-start | bytes 1310720 | tf_op jit(solution)/shard_map/all_to_all | solution.py:38
  46.3 11.5 %copy-start.22 = (bf16[8,64,512]{2,1,0:T(8,128)(2,1)}, bf16[8,64,512]{2,1,0:T(8,128)(2,1)S(1)}, u32[]{:S(2)}) copy-start(bf16[8,64,512]{2,1,0:T(8,128)(2,1)S(1)} %collective-permute-done.10.refs_3_) | copy-start | bytes 1572868
  61.6 5.9 %collective-permute-start.11 = (bf16[4,4,64,512]{3,2,1,0:T(8,128)(2,1)}, bf16[4,4,64,512]{3,2,1,0:T(8,128)(2,1)S(1)}, u32[]{:S(2)}, u32[]{:S(2)}) collective-permute-start(bf16[4,4,64,512]{3,2,1,0:T(8,128)(2,1)} %get-tuple-element.80), channel_id=1, source_target_pairs={{0,32},{32,0},{1,33},{33,1},{2,34},{34,2},{3,35},{35,3},{4,36},{36... | collective-permute-start | bytes 3145736 | tf_op jit(solution)/shard_map/ppermute | solution.py:43
  65.0 3.4 %collective-permute-start.12 = (bf16[8,64,576]{2,1,0:T(8,128)(2,1)S(1)}, bf16[8,64,576]{2,1,0:T(8,128)(2,1)S(1)}, u32[]{:S(2)}, u32[]{:S(2)}) collective-permute-start(bf16[8,64,576]{2,1,0:T(8,128)(2,1)S(1)} %all-to-all-done.near_ref.refs_3_), channel_id=1, source_target_pairs={{0,32},{32,0},{1,33},{33,1},{2,34},{34,2},{3,35},{35,3},{4,36},{36... | collective-permute-start | bytes 1769480 | tf_op jit(solution)/shard_map/ppermute | solution.py:43
  103.4 4.8 %collective-permute-start.13 = (bf16[64,576]{1,0:T(8,128)(2,1)}, bf16[64,576]{1,0:T(8,128)(2,1)S(1)}, u32[]{:S(2)}, u32[]{:S(2)}) collective-permute-start(bf16[64,576]{1,0:T(8,128)(2,1)} %get-tuple-element.86), channel_id=1, source_target_pairs={{0,1},{1,0},{2,3},{3,2},{4,5},{5,4},{6,7},{7,6},{8,9},{9,8},{10,11... | collective-permute-start | bytes 221192 | tf_op jit(solution)/shard_map/ppermute | solution.py:47
  103.7 7.1 %collective-permute-start.14 = (bf16[64,576]{1,0:T(8,128)(2,1)}, bf16[64,576]{1,0:T(8,128)(2,1)S(1)}, u32[]{:S(2)}, u32[]{:S(2)}) collective-permute-start(bf16[64,576]{1,0:T(8,128)(2,1)} %get-tuple-element.87), channel_id=1, source_target_pairs={{0,2},{1,3},{2,0},{3,1},{4,6},{5,7},{6,4},{7,5},{8,10},{9,11},{10,... | collective-permute-start | bytes 221192 | tf_op jit(solution)/shard_map/ppermute | solution.py:47
  104.9 6.3 %collective-permute-start.15 = (bf16[64,576]{1,0:T(8,128)(2,1)}, bf16[64,576]{1,0:T(8,128)(2,1)S(1)}, u32[]{:S(2)}, u32[]{:S(2)}) collective-permute-start(bf16[64,576]{1,0:T(8,128)(2,1)} %get-tuple-element.88), channel_id=1, source_target_pairs={{0,4},{4,0},{8,12},{12,8},{16,20},{20,16},{24,28},{28,24},{1,5},{5... | collective-permute-start | bytes 221192 | tf_op jit(solution)/shard_map/ppermute | solution.py:47
  105.6 8.0 %collective-permute-start.16 = (bf16[64,576]{1,0:T(8,128)(2,1)}, bf16[64,576]{1,0:T(8,128)(2,1)S(1)}, u32[]{:S(2)}, u32[]{:S(2)}) collective-permute-start(bf16[64,576]{1,0:T(8,128)(2,1)} %get-tuple-element.89), channel_id=1, source_target_pairs={{0,8},{4,12},{8,0},{12,4},{16,24},{20,28},{24,16},{28,20},{1,9},{5... | collective-permute-start | bytes 221192 | tf_op jit(solution)/shard_map/ppermute | solution.py:47
  106.8 7.8 %collective-permute-start.17 = (bf16[64,576]{1,0:T(8,128)(2,1)}, bf16[64,576]{1,0:T(8,128)(2,1)S(1)}, u32[]{:S(2)}, u32[]{:S(2)}) collective-permute-start(bf16[64,576]{1,0:T(8,128)(2,1)} %get-tuple-element.90), channel_id=1, source_target_pairs={{0,16},{4,20},{8,24},{12,28},{16,0},{20,4},{24,8},{28,12},{1,17},{... | collective-permute-start | bytes 221192 | tf_op jit(solution)/shard_map/ppermute | solution.py:47
  108.2 6.4 %collective-permute-start.18 = (bf16[64,576]{1,0:T(8,128)(2,1)}, bf16[64,576]{1,0:T(8,128)(2,1)S(1)}, u32[]{:S(2)}, u32[]{:S(2)}) collective-permute-start(bf16[64,576]{1,0:T(8,128)(2,1)} %get-tuple-element.91), channel_id=1, source_target_pairs={{0,32},{32,0},{1,33},{33,1},{2,34},{34,2},{3,35},{35,3},{4,36},{36... | collective-permute-start | bytes 221192 | tf_op jit(solution)/shard_map/ppermute | solution.py:47
  110.8 3.8 %collective-permute-start.19 = (bf16[64,576]{1,0:T(8,128)(2,1)}, bf16[64,576]{1,0:T(8,128)(2,1)S(1)}, u32[]{:S(2)}, u32[]{:S(2)}) collective-permute-start(bf16[64,576]{1,0:T(8,128)(2,1)} %get-tuple-element.92), channel_id=1, source_target_pairs={{0,64},{64,0},{128,192},{192,128},{1,65},{65,1},{129,193},{193,129... | collective-permute-start | bytes 221192 | tf_op jit(solution)/shard_map/ppermute | solution.py:47
  111.1 5.9 %collective-permute-start.20 = (bf16[64,576]{1,0:T(8,128)(2,1)}, bf16[64,576]{1,0:T(8,128)(2,1)S(1)}, u32[]{:S(2)}, u32[]{:S(2)}) collective-permute-start(bf16[64,576]{1,0:T(8,128)(2,1)} %get-tuple-element.93), channel_id=1, source_target_pairs={{0,128},{64,192},{128,0},{192,64},{1,129},{65,193},{129,1},{193,65... | collective-permute-start | bytes 221192 | tf_op jit(solution)/shard_map/ppermute | solution.py:47
  148.2 4.6 %collective-permute-start.21 = (bf16[8,72,640]{2,1,0:T(8,128)(2,1)S(1)}, bf16[8,72,640]{2,1,0:T(8,128)(2,1)S(1)}, u32[]{:S(2)}, u32[]{:S(2)}) collective-permute-start(bf16[8,72,640]{2,1,0:T(8,128)(2,1)S(1)} %all_to_all.41.near_ref.refs_1_), channel_id=1, source_target_pairs={{0,32},{32,0},{1,33},{33,1},{2,34},{34,2},{3,35},{35,3},{4,36},{36... | collective-permute-start | bytes 2211848 | tf_op jit(solution)/shard_map/ppermute | solution.py:43
  160.4 32.9 %all-to-all-start.3 = ((bf16[16,88,576]{2,1,0:T(8,128)(2,1)}), bf16[16,88,576]{2,1,0:T(8,128)(2,1)S(1)}, u32[]{:S(2)}, u32[]{:S(2)}) async-start(bf16[16,88,576]{2,1,0:T(8,128)(2,1)} %get-tuple-element.96), calls=%async_computation.3 | async-start | bytes 3604480 | tf_op jit(solution)/shard_map/all_to_all | solution.py:38
  198.4 43.2 %copy-start.20 = (f32[64,64]{1,0:T(8,128)S(1)}, f32[64,64]{1,0:T(8,128)}, u32[]{:S(2)}) copy-start(f32[64,64]{1,0:T(8,128)} %slice.102.refs_8_) | copy-start | bytes 49156
  198.4 43.2 %copy-start.10 = (f32[64,576]{1,0:T(8,128)S(1)}, f32[64,576]{1,0:T(8,128)}, u32[]{:S(2)}) copy-start(f32[64,576]{1,0:T(8,128)} %get-tuple-element.94.field_ref) | copy-start | bytes 442372
  198.4 43.4 %copy-start.19 = (f32[64,64]{1,0:T(8,128)S(1)}, f32[64,64]{1,0:T(8,128)}, u32[]{:S(2)}) copy-start(f32[64,64]{1,0:T(8,128)} %slice.104.refs_8_) | copy-start | bytes 49156
  198.4 43.5 %copy-start.50 = (f32[64,64]{1,0:T(8,128)S(1)}, f32[64,64]{1,0:T(8,128)}, u32[]{:S(2)}) copy-start(f32[64,64]{1,0:T(8,128)} %get-tuple-element.98) | copy-start | bytes 49156
  198.4 3.4 %collective-permute-start.22 = (bf16[64,512]{1,0:T(8,128)(2,1)}, bf16[64,512]{1,0:T(8,128)(2,1)S(1)}, u32[]{:S(2)}, u32[]{:S(2)}) collective-permute-start(bf16[64,512]{1,0:T(8,128)(2,1)} %get-tuple-element.101), channel_id=1, source_target_pairs={{0,1},{1,0},{2,3},{3,2},{4,5},{5,4},{6,7},{7,6},{8,9},{9,8},{10,11... | collective-permute-start | bytes 196616 | tf_op jit(solution)/shard_map/ppermute | solution.py:47
  198.5 6.0 %collective-permute-start.23 = (bf16[64,512]{1,0:T(8,128)(2,1)}, bf16[64,512]{1,0:T(8,128)(2,1)S(1)}, u32[]{:S(2)}, u32[]{:S(2)}) collective-permute-start(bf16[64,512]{1,0:T(8,128)(2,1)} %get-tuple-element.102), channel_id=1, source_target_pairs={{0,2},{1,3},{2,0},{3,1},{4,6},{5,7},{6,4},{7,5},{8,10},{9,11},{10,... | collective-permute-start | bytes 196616 | tf_op jit(solution)/shard_map/ppermute | solution.py:47
  198.7 6.0 %collective-permute-start.24 = (bf16[64,512]{1,0:T(8,128)(2,1)}, bf16[64,512]{1,0:T(8,128)(2,1)S(1)}, u32[]{:S(2)}, u32[]{:S(2)}) collective-permute-start(bf16[64,512]{1,0:T(8,128)(2,1)} %get-tuple-element.103), channel_id=1, source_target_pairs={{0,4},{4,0},{8,12},{12,8},{16,20},{20,16},{24,28},{28,24},{1,5},{5... | collective-permute-start | bytes 196616 | tf_op jit(solution)/shard_map/ppermute | solution.py:47
  199.0 8.8 %collective-permute-start.25 = (bf16[64,512]{1,0:T(8,128)(2,1)}, bf16[64,512]{1,0:T(8,128)(2,1)S(1)}, u32[]{:S(2)}, u32[]{:S(2)}) collective-permute-start(bf16[64,512]{1,0:T(8,128)(2,1)} %get-tuple-element.104), channel_id=1, source_target_pairs={{0,8},{4,12},{8,0},{12,4},{16,24},{20,28},{24,16},{28,20},{1,9},{5... | collective-permute-start | bytes 196616 | tf_op jit(solution)/shard_map/ppermute | solution.py:47
  199.1 8.6 %collective-permute-start.26 = (bf16[64,512]{1,0:T(8,128)(2,1)}, bf16[64,512]{1,0:T(8,128)(2,1)S(1)}, u32[]{:S(2)}, u32[]{:S(2)}) collective-permute-start(bf16[64,512]{1,0:T(8,128)(2,1)} %get-tuple-element.105), channel_id=1, source_target_pairs={{0,16},{4,20},{8,24},{12,28},{16,0},{20,4},{24,8},{28,12},{1,17},{... | collective-permute-start | bytes 196616 | tf_op jit(solution)/shard_map/ppermute | solution.py:47
  201.8 6.0 %collective-permute-start.27 = (bf16[64,512]{1,0:T(8,128)(2,1)}, bf16[64,512]{1,0:T(8,128)(2,1)S(1)}, u32[]{:S(2)}, u32[]{:S(2)}) collective-permute-start(bf16[64,512]{1,0:T(8,128)(2,1)} %get-tuple-element.106), channel_id=1, source_target_pairs={{0,32},{32,0},{1,33},{33,1},{2,34},{34,2},{3,35},{35,3},{4,36},{36... | collective-permute-start | bytes 196616 | tf_op jit(solution)/shard_map/ppermute | solution.py:47
  204.5 3.6 %collective-permute-start.28 = (bf16[64,512]{1,0:T(8,128)(2,1)}, bf16[64,512]{1,0:T(8,128)(2,1)S(1)}, u32[]{:S(2)}, u32[]{:S(2)}) collective-permute-start(bf16[64,512]{1,0:T(8,128)(2,1)} %get-tuple-element.107), channel_id=1, source_target_pairs={{0,64},{64,0},{128,192},{192,128},{1,65},{65,1},{129,193},{193,129... | collective-permute-start | bytes 196616 | tf_op jit(solution)/shard_map/ppermute | solution.py:47
  204.8 4.9 %collective-permute-start.29 = (bf16[64,512]{1,0:T(8,128)(2,1)}, bf16[64,512]{1,0:T(8,128)(2,1)S(1)}, u32[]{:S(2)}, u32[]{:S(2)}) collective-permute-start(bf16[64,512]{1,0:T(8,128)(2,1)} %get-tuple-element.108), channel_id=1, source_target_pairs={{0,128},{64,192},{128,0},{192,64},{1,129},{65,193},{129,1},{193,65... | collective-permute-start | bytes 196616 | tf_op jit(solution)/shard_map/ppermute | solution.py:47
  238.9 4.5 %collective-permute-start.30 = (bf16[8,88,512]{2,1,0:T(8,128)(2,1)S(1)}, bf16[8,88,512]{2,1,0:T(8,128)(2,1)S(1)}, u32[]{:S(2)}, u32[]{:S(2)}) collective-permute-start(bf16[8,88,512]{2,1,0:T(8,128)(2,1)S(1)} %all_to_all.42.near_ref), channel_id=1, source_target_pairs={{0,32},{32,0},{1,33},{33,1},{2,34},{34,2},{3,35},{35,3},{4,36},{36... | collective-permute-start | bytes 2162696 | tf_op jit(solution)/shard_map/ppermute | solution.py:43
  250.9 22.0 %all-to-all-start.5 = ((bf16[16,64,512]{2,1,0:T(8,128)(2,1)}), bf16[16,64,512]{2,1,0:T(8,128)(2,1)S(1)}, u32[]{:S(2)}, u32[]{:S(2)}) async-start(bf16[16,64,512]{2,1,0:T(8,128)(2,1)} %get-tuple-element.114), calls=%async_computation.5 | async-start | bytes 2097152 | tf_op jit(solution)/shard_map/all_to_all | solution.py:38
  257.4 18.8 %copy-start.11 = (f32[64,576]{1,0:T(8,128)S(1)}, f32[64,576]{1,0:T(8,128)}, u32[]{:S(2)}) copy-start(f32[64,576]{1,0:T(8,128)} %get-tuple-element.85.field_ref) | copy-start | bytes 442372
  257.4 18.8 %copy-start.14 = (f32[64,512]{1,0:T(8,128)S(1)}, f32[64,512]{1,0:T(8,128)}, u32[]{:S(2)}) copy-start(f32[64,512]{1,0:T(8,128)} %get-tuple-element.100.field_ref) | copy-start | bytes 393220
  257.5 18.8 %copy-start.15 = (f32[64,512]{1,0:T(8,128)S(1)}, f32[64,512]{1,0:T(8,128)}, u32[]{:S(2)}) copy-start(f32[64,512]{1,0:T(8,128)} %get-tuple-element.113.field_ref) | copy-start | bytes 393220
  257.5 18.8 %copy-start.18 = (f32[64,576]{1,0:T(8,128)S(1)}, f32[64,576]{1,0:T(8,128)}, u32[]{:S(2)}) copy-start(f32[64,576]{1,0:T(8,128)} %get-tuple-element.72.field_ref) | copy-start | bytes 442372
  276.3 27.1 %copy-start.51 = (s32[512]{0:T(512)S(1)}, s32[512]{0:T(512)}, u32[]{:S(2)}) copy-start(s32[512]{0:T(512)} %param.15) | copy-start | bytes 6148
  276.3 27.2 %copy-start.16 = (f32[64,512]{1,0:T(8,128)S(1)}, f32[64,512]{1,0:T(8,128)}, u32[]{:S(2)}) copy-start(f32[64,512]{1,0:T(8,128)} %shard_map.103) | copy-start | bytes 393220
  (43 other events, 142.2 us)

commit v3 on v2

--- a/solution.py
+++ b/solution.py
@@ -125,7 +125,10 @@
     per_step = out_ref.shape[0]
     for k in range(per_step):
         block = product[k * rows : (k + 1) * rows]
-        out_ref[k, :rows] = block.astype(BF16)
+        sent = block.astype(BF16)
+        if out_ref.shape[2] > width:
+            sent = jnp.concatenate([sent, refs[0][k]], axis=1)
+        out_ref[k, :rows] = sent
 
         @pl.when(me_ref[0] == step * per_step + k)
         def _():
@@ -161,9 +164,6 @@
 
         for k in range(per_step):
             out_ref[k, rows:] = below_ref[...]
-    elif out_ref.shape[1] > rows:
-        for k in range(per_step):
-            out_ref[k, rows:] = refs[0][k]
 
 
 def in_two(values):
@@ -188,7 +188,7 @@
     rows = own_ref.shape[0]
 
     def add(d, total):
-        part = arrived_ref[d, :rows].astype(F32)
+        part = arrived_ref[d, :rows, : own_ref.shape[1]].astype(F32)
         return total + jnp.where(me_ref[0] == d, jnp.zeros_like(part), part)
 
     total = lax.fori_loop(0, arrived_ref.shape[0], add, own_ref[...])
@@ -326,14 +326,16 @@
     t_parts = mm3(coarse_basis.T, right_sides).reshape(n_rows, t_share, rhs)
     t_top = lax.reduce_precision(t_parts, 8, 7)
     t_parts = jnp.concatenate([t_top, t_parts - t_top], axis=1).astype(BF16)
-    t_parts = jnp.pad(t_parts, ((0, 0), (0, 0), (0, rank)))
+    t_parts = t_parts.reshape(n_rows, -1, rank)
+    t_height = t_parts.shape[1]
+    t_parts = jnp.pad(t_parts, ((0, 0), (0, rows - t_height), (0, 0)))
     g_blocks, (t_parts, places) = rearranged(blocks, (t_parts, places))
 
     def gathered(copies):
         near = exchanged(copies, "z")
         return near, shifted(near, "c", 1)
 
-    def products(everyone, width, riders=(), more_rows=0, share=0):
+    def products(everyone, width, riders=(), more_rows=0, share=0, more_columns=0):
         depth = lax.axis_size("z") * rows
         per_step = n_rows // 2
         height = rows + more_rows
@@ -351,7 +353,7 @@
             functools.partial(times_kernel, rows, width, share, rank),
             grid=(2,),
             out_shape=[
-                jax.ShapeDtypeStruct((n_rows, height, width), BF16),
+                jax.ShapeDtypeStruct((n_rows, height, width + more_columns), BF16),
                 jax.ShapeDtypeStruct((rows, width), F32),
             ],
             in_specs=[
@@ -360,7 +362,7 @@
                 *[whole(array) for array in everyone],
                 *rider_specs,
             ],
-            out_specs=[some((per_step, height, width)), pl.BlockSpec((rows, width), lambda i: (0, 0))],
+            out_specs=[some((per_step, height, width + more_columns)), pl.BlockSpec((rows, width), lambda i: (0, 0))],
             scratch_shapes=[
                 *[pltpu.VMEM((depth, width), BF16)] * 2,
                 pltpu.VMEM((more_rows or 8, width), BF16),
@@ -402,11 +404,12 @@
     cuts = [(0, rhs)]
     first, copies = precondition(right_sides, sent, cuts, True, beside=coarse_basis)
     all_first = gathered(copies)
-    arrived, own = products(all_first, width, [t_parts], 2 * t_share)
+    arrived, own = products(all_first, width, [t_parts], more_columns=rank)
     first_image, sent = image_of(arrived, own, first)
     coarse_image = first_image[:, rhs:]
 
-    t_rows = sum_of_terms(arrived[:, rows:], 1).sum(axis=0)
+    t_rows = arrived[:, :t_height, width:].reshape(n_rows, 2 * t_share, rhs)
+    t_rows = sum_of_terms(t_rows, 1).sum(axis=0)
     t_rows = two_terms(padded(t_rows, width + rank))
     second, copies = precondition(first_image, sent, beside=coarse_image, below=t_rows)
     all_second = gathered(copies)

time: 306 us -> 305 us (level)
    unnamed x116 -> x118, local copies, waits for them, and re-layouts: 8.46 us -> 8.16 us
  transfers between devices with their start and end apart: 34 -> 34, of which waited for: 15 -> 16; matrix products, arithmetic and copies ran while one was open for 4% -> 4% of each run, Pallas kernels for 2% -> 2%
where the time goes in v3:
time: 305 us; the launch traced here: 303 us
  blocking collectives  103 us (34%)
  waiting for transfers between devices  65.1 us (21%)
  starting transfers between devices  61.1 us (20%)
  Pallas kernels  43.4 us (14%)
  local copies, waits for them, and re-layouts  14.7 us (5%)
  other arithmetic  8.68 us (3%)
  matrix products  5.56 us (2%)
    all_to_all x3, blocking collectives, exchanged(): return lax.all_to_all(array, axes, split_axis=0, concat_axis=0, tiled=True)  76.7 us
    all_to_all x3, waiting for transfers between devices, exchanged(): return lax.all_to_all(array, axes, split_axis=0, concat_axis=0, tiled=True)  40.4 us
    ppermute x24, starting transfers between devices, from_partner(): lax.ppermute(value, axis, [(i, i ^ distance) for i in range(lax.axis_size...  35.6 us
    pallas_call x9, Pallas kernels, kernel_call(): pl.pallas_call(kernel, out_shape=[jax.ShapeDtypeStruct(shape, dtype) for...  26.7 us
    all_to_all x2, blocking collectives, from_everyone(): return lax.all_to_all(copies, axes, split_axis=0, concat_axis=0, tiled=True)  25.8 us
    ppermute x7, waiting for transfers between devices, shifted(): lax.ppermute(value, axis, [(i, (i + step) % size) for i in range(size)])  17.9 us
    pallas_call x3, Pallas kernels, products(): pl.pallas_call(functools.partial(times_kernel, rows, width, share, rank),...  16.8 us
    all_to_all x3, starting transfers between devices, exchanged(): return lax.all_to_all(array, axes, split_axis=0, concat_axis=0, tiled=True)  14.5 us
  transfers between devices with their start and end apart: 34, of which 16 were waited for; matrix products, arithmetic and copies ran while one was open for 4% of the time, Pallas kernels for 2%

profile of v3, /device:TPU:1, one launch (start us, length us, event | category | flops | bytes accessed | tf_op | source)
XLA Modules:
  0.0 303.4 jit_solution(13749185284688684089)
XLA Ops:
  0.7 4.2 %shard_map.95 = (bf16[8,64,512]{2,1,0:T(8,128)(2,1)}, bf16[8,64,512]{2,1,0:T(8,128)(2,1)}, bf16[8,64,512]{2,1,0:T(8,128)(2,1)}, bf16[8,64,512]{2,1,0:T(8,128)(2,1)}) custom-call(s32[1]{0:T(128)} %bitcast.me_ref, bf16[8,64,2048]{2,1,0:T(8,128)(2,1)} %bitcast.55), custom_call_target="tpu_custom_call" | custom-call | tf_op jit(solution)/shard_map/pallas_call | solution.py:255
  6.6 2.0 shard_map.96
  8.6 2.0 collective-permute-start
  10.6 2.5 collective-permute-start.1
  13.1 1.6 collective-permute-start.2
  14.7 3.0 collective-permute-start.3
  17.7 4.2 %collective-permute-start.4 = (bf16[64,512]{1,0:T(8,128)(2,1)}, bf16[64,512]{1,0:T(8,128)(2,1)S(1)}, u32[]{:S(2)}, u32[]{:S(2)}) collective-permute-start(bf16[64,512]{1,0:T(8,128)(2,1)} %get-tuple-element.68), channel_id=1, source_target_pairs={{0,16},{4,20},{8,24},{12,28},{16,0},{20,4},{24,8},{28,12},{1,17},{... | collective-permute-start | bytes 196616 | tf_op jit(solution)/shard_map/ppermute | solution.py:47
  26.3 2.2 collective-permute-start.5
  28.5 1.4 collective-permute-start.6
  29.9 2.7 collective-permute-start.7
  33.4 1.3 collective-permute-start.8
  36.7 2.7 shard_map.97
  39.4 3.5 %all-to-all-start = ((bf16[8,64,576]{2,1,0:T(8,128)(2,1)}), bf16[8,64,576]{2,1,0:T(8,128)(2,1)S(1)}, u32[]{:S(2)}, u32[]{:S(2)}) async-start(bf16[8,64,576]{2,1,0:T(8,128)(2,1)} %get-tuple-element.81), calls=%async_computation | async-start | bytes 1310720 | tf_op jit(solution)/shard_map/all_to_all | solution.py:38
  46.3 2.0 collective-permute-done.8.refs_1_
  48.3 9.5 %collective-permute-done.9.refs_2_ = bf16[8,64,512]{2,1,0:T(8,128)(2,1)S(1)} collective-permute-done((bf16[8,64,512]{2,1,0:T(8,128)(2,1)S(1)}, bf16[8,64,512]{2,1,0:T(8,128)(2,1)S(1)}, u32[]{:S(2)}, u32[]{:S(2)}) %collective-permute-start.9) | collective-permute-done | bytes 524320 | tf_op jit(solution)/shard_map/ppermute | solution.py:43
  58.7 3.0 shard_map.98
  61.7 3.4 %collective-permute-start.11 = (bf16[4,4,64,512]{3,2,1,0:T(8,128)(2,1)}, bf16[4,4,64,512]{3,2,1,0:T(8,128)(2,1)S(1)}, u32[]{:S(2)}, u32[]{:S(2)}) collective-permute-start(bf16[4,4,64,512]{3,2,1,0:T(8,128)(2,1)} %get-tuple-element.80), channel_id=1, source_target_pairs={{0,32},{32,0},{1,33},{33,1},{2,34},{34,2},{3,35},{35,3},{4,36},{36... | collective-permute-start | bytes 3145736 | tf_op jit(solution)/shard_map/ppermute | solution.py:43
  65.3 2.2 collective-permute-done.11
  69.3 5.8 %times.3 = (bf16[16,64,640]{2,1,0:T(8,128)(2,1)}, f32[64,576]{1,0:T(8,128)}) custom-call(s32[2]{0:T(128)} %pad_add_fusion.1.me_ref, bf16[1024,512]{1,0:T(8,128)(2,1)} %bitcast.49, bf16[1024,512]{1,0:T(8,128)(2,1)} %bitcast.52, bf16[8,64,576]{2,1,0:T(8,128)(2,1)} %copy-done.4, bf16[8,64,576]{2,1,0:T(8,128)(2,1)} %copy-done.9, ...), custom_call_target="tpu_custom_call" | custom-call | tf_op jit(solution)/shard_map/times/pallas_call | solution.py:352
  75.1 23.3 %all_to_all.40.arrived_ref = bf16[16,64,640]{2,1,0:T(8,128)(2,1)S(1)} all-to-all(bf16[16,64,640]{2,1,0:T(8,128)(2,1)} %get-tuple-element.83), channel_id=1, replica_groups=mesh['y'=4,'c'=2,'z'=8,'x'=4] {'y','x'}, dimensions={0} | all-to-all | bytes 2621440 | tf_op jit(solution)/shard_map/all_to_all | solution.py:38
  99.4 3.1 %shard_map.99 = (f32[64,576]{1,0:T(8,128)}, bf16[64,576]{1,0:T(8,128)(2,1)}, bf16[64,576]{1,0:T(8,128)(2,1)}, bf16[64,576]{1,0:T(8,128)(2,1)}, bf16[64,576]{1,0:...) custom-call(s32[2]{0:T(128)} %pad_add_fusion.1.me_ref, ...), custom_call_target="tpu_custom_call" | custom-call | tf_op jit(solution)/shard_map/pallas_call | solution.py:255
  104.4 1.2 collective-permute-start.16
  105.6 1.4 slice.104.refs_8_
  107.0 2.8 collective-permute-start.18
  110.2 1.8 collective-permute-start.20
  113.6 2.4 collective-permute-done.20.refs_7_
  116.7 2.9 shard_map.100
  119.6 27.6 %all_to_all.41.near_ref.refs_1_ = bf16[8,72,640]{2,1,0:T(8,128)(2,1)S(1)} all-to-all(bf16[8,72,640]{2,1,0:T(8,128)(2,1)} %get-tuple-element.95), channel_id=1, replica_groups=mesh['y'=4,'c'=2,'z'=8,'x'=4] {'z'}, dimensions={0} | all-to-all | bytes 1474560 | tf_op jit(solution)/shard_map/all_to_all | solution.py:38
  147.2 2.7 collective-permute-start.21
  149.9 1.8 collective-permute-done.21.far_ref.refs_2_
  152.6 6.8 %times.4 = (bf16[16,88,576]{2,1,0:T(8,128)(2,1)}, f32[64,576]{1,0:T(8,128)}) custom-call(s32[2]{0:T(128)} %pad_add_fusion.1.me_ref, bf16[1024,512]{1,0:T(8,128)(2,1)} %bitcast.50, bf16[1024,512]{1,0:T(8,128)(2,1)} %bitcast.53, bf16[8,72,640]{2,1,0:T(8,128)(2,1)} %copy-done.2, bf16[8,72,640]{2,1,0:T(8,128)(2,1)} %copy-done.7, f32[4,576]{1,0:T(4,128)} %fusion.17.refs_0_, ...), custom_call_target="tpu_custom_call" | custom-call | tf_op jit(solution)/shard_map/times/pallas_call | solution.py:352
  159.4 5.2 %all-to-all-start.3 = ((bf16[16,88,576]{2,1,0:T(8,128)(2,1)}), bf16[16,88,576]{2,1,0:T(8,128)(2,1)S(1)}, u32[]{:S(2)}, u32[]{:S(2)}) async-start(bf16[16,88,576]{2,1,0:T(8,128)(2,1)} %get-tuple-element.96), calls=%async_computation.3 | async-start | bytes 3604480 | tf_op jit(solution)/shard_map/all_to_all | solution.py:38
  165.3 27.0 %all-to-all-done.3.arrived_ref = bf16[16,88,576]{2,1,0:T(8,128)(2,1)S(1)} async-done(((bf16[16,88,576]{2,1,0:T(8,128)(2,1)}), bf16[16,88,576]{2,1,0:T(8,128)(2,1)S(1)}, u32[]{:S(2)}, u32[]{:S(2)}) %all-to-all-start.3) | async-done | bytes 1622048 | tf_op jit(solution)/shard_map/all_to_all | solution.py:38
  193.7 3.7 %shard_map.101 = (f32[64,512]{1,0:T(8,128)}, f32[64,64]{1,0:T(8,128)}, f32[64,512]{1,0:T(8,128)}, bf16[64,512]{1,0:T(8,128)(2,1)}, bf16[64,512]{1,0:T(8,128)(2,1...) custom-call(s32[2]{0:T(128)} %pad_add_fusion.1.me_ref, ...), custom_call_target="tpu_custom_call" | custom-call | tf_op jit(solution)/shard_map/pallas_call | solution.py:255
  198.1 2.0 collective-permute-start.26
  200.8 2.6 collective-permute-start.27
  203.8 2.4 collective-permute-start.29
  207.1 1.6 collective-permute-done.29.refs_7_
  209.3 2.7 shard_map.102
  212.0 25.9 %all_to_all.42.near_ref = bf16[8,88,512]{2,1,0:T(8,128)(2,1)S(1)} all-to-all(bf16[8,88,512]{2,1,0:T(8,128)(2,1)} %get-tuple-element.109), channel_id=1, replica_groups=mesh['y'=4,'c'=2,'z'=8,'x'=4] {'z'}, dimensions={0} | all-to-all | bytes 1441792 | tf_op jit(solution)/shard_map/all_to_all | solution.py:38
  237.9 2.7 collective-permute-start.30
  243.3 4.1 %times.5 = (bf16[16,64,512]{2,1,0:T(8,128)(2,1)}, f32[64,512]{1,0:T(8,128)}) custom-call(s32[2]{0:T(128)} %pad_add_fusion.1.me_ref, bf16[1024,512]{1,0:T(8,128)(2,1)} %bitcast.51, bf16[1024,512]{1,0:T(8,128)(2,1)} %bitcast.54, bf16[8,88,512]{2,1,0:T(8,128)(2,1)} %copy-done.6, bf16[8,88,512]{2,1,0:T(8,128)(2,1)} %copy-done.17), custom_call_target="tpu_custom_call" | custom-call | tf_op jit(solution)/shard_map/times/pallas_call | solution.py:352
  249.8 5.7 %all-to-all-start.5 = ((bf16[16,64,512]{2,1,0:T(8,128)(2,1)}), bf16[16,64,512]{2,1,0:T(8,128)(2,1)S(1)}, u32[]{:S(2)}, u32[]{:S(2)}) async-start(bf16[16,64,512]{2,1,0:T(8,128)(2,1)} %get-tuple-element.114), calls=%async_computation.5 | async-start | bytes 2097152 | tf_op jit(solution)/shard_map/all_to_all | solution.py:38
  257.0 1.5 fusion.4
  258.5 13.4 %all-to-all-done.5.arrived_ref = bf16[16,64,512]{2,1,0:T(8,128)(2,1)S(1)} async-done(((bf16[16,64,512]{2,1,0:T(8,128)(2,1)}), bf16[16,64,512]{2,1,0:T(8,128)(2,1)S(1)}, u32[]{:S(2)}, u32[]{:S(2)}) %all-to-all-start.5) | async-done | bytes 1048608 | tf_op jit(solution)/shard_map/all_to_all | solution.py:38
  272.9 2.4 shard_map.103
  276.5 12.3 %all_to_all.43 = f32[16,6,512]{2,1,0:T(8,128)S(1)} all-to-all(f32[16,6,512]{2,1,0:T(8,128)S(1)} %broadcast_in_dim.49), channel_id=1, replica_groups=mesh['y'=4,'c'=2,'z'=8,'x'=4] {'y','x'}, dimensions={0} | all-to-all | bytes 393216 | tf_op jit(solution)/shard_map/all_to_all | solution.py:34
  288.8 13.5 %all_to_all.44 = f32[16,6,512]{2,1,0:T(8,128)S(1)} all-to-all(f32[16,6,512]{2,1,0:T(8,128)S(1)} %broadcast_in_dim.50), channel_id=1, replica_groups=mesh['y'=4,'c'=2,'z'=8,'x'=4] {'c','z'}, dimensions={0} | all-to-all | bytes 393216 | tf_op jit(solution)/shard_map/all_to_all | solution.py:34
  (235 shorter events, 35.6 us)
Async XLA Ops:
  4.8 17.1 %copy-start.13 = (f32[9,64,64]{2,1,0:T(8,128)S(1)}, f32[9,64,64]{2,1,0:T(8,128)}, u32[]{:S(2)}) copy-start(f32[9,64,64]{2,1,0:T(8,128)} %param.12) | copy-start | bytes 442372
  8.6 17.7 %collective-permute-start = (bf16[64,512]{1,0:T(8,128)(2,1)}, bf16[64,512]{1,0:T(8,128)(2,1)S(1)}, u32[]{:S(2)}, u32[]{:S(2)}) collective-permute-start(bf16[64,512]{1,0:T(8,128)(2,1)} %get-tuple-element.64), channel_id=1, source_target_pairs={{0,1},{1,0},{2,3},{3,2},{4,5},{5,4},{6,7},{7,6},{8,9},{9,8},{10,11... | collective-permute-start | bytes 196616 | tf_op jit(solution)/shard_map/ppermute | solution.py:47
  10.6 17.9 %collective-permute-start.1 = (bf16[64,512]{1,0:T(8,128)(2,1)}, bf16[64,512]{1,0:T(8,128)(2,1)S(1)}, u32[]{:S(2)}, u32[]{:S(2)}) collective-permute-start(bf16[64,512]{1,0:T(8,128)(2,1)} %get-tuple-element.65), channel_id=1, source_target_pairs={{0,2},{1,3},{2,0},{3,1},{4,6},{5,7},{6,4},{7,5},{8,10},{9,11},{10,... | collective-permute-start | bytes 196616 | tf_op jit(solution)/shard_map/ppermute | solution.py:47
  13.1 16.8 %collective-permute-start.2 = (bf16[64,512]{1,0:T(8,128)(2,1)}, bf16[64,512]{1,0:T(8,128)(2,1)S(1)}, u32[]{:S(2)}, u32[]{:S(2)}) collective-permute-start(bf16[64,512]{1,0:T(8,128)(2,1)} %get-tuple-element.66), channel_id=1, source_target_pairs={{0,4},{4,0},{8,12},{12,8},{16,20},{20,16},{24,28},{28,24},{1,5},{5... | collective-permute-start | bytes 196616 | tf_op jit(solution)/shard_map/ppermute | solution.py:47
  14.7 18.5 %collective-permute-start.3 = (bf16[64,512]{1,0:T(8,128)(2,1)}, bf16[64,512]{1,0:T(8,128)(2,1)S(1)}, u32[]{:S(2)}, u32[]{:S(2)}) collective-permute-start(bf16[64,512]{1,0:T(8,128)(2,1)} %get-tuple-element.67), channel_id=1, source_target_pairs={{0,8},{4,12},{8,0},{12,4},{16,24},{20,28},{24,16},{28,20},{1,9},{5... | collective-permute-start | bytes 196616 | tf_op jit(solution)/shard_map/ppermute | solution.py:47
  17.7 15.7 %collective-permute-start.4 = (bf16[64,512]{1,0:T(8,128)(2,1)}, bf16[64,512]{1,0:T(8,128)(2,1)S(1)}, u32[]{:S(2)}, u32[]{:S(2)}) collective-permute-start(bf16[64,512]{1,0:T(8,128)(2,1)} %get-tuple-element.68), channel_id=1, source_target_pairs={{0,16},{4,20},{8,24},{12,28},{16,0},{20,4},{24,8},{28,12},{1,17},{... | collective-permute-start | bytes 196616 | tf_op jit(solution)/shard_map/ppermute | solution.py:47
  23.5 11.2 %copy-start.52 = (bf16[8,64,512]{2,1,0:T(8,128)(2,1)S(1)}, bf16[8,64,512]{2,1,0:T(8,128)(2,1)}, u32[]{:S(2)}) copy-start(bf16[8,64,512]{2,1,0:T(8,128)(2,1)} %get-tuple-element.75) | copy-start | bytes 1572868
  24.4 18.5 %copy-start.8 = (f32[64,512]{1,0:T(8,128)S(1)}, f32[64,512]{1,0:T(8,128)}, u32[]{:S(2)}) copy-start(f32[64,512]{1,0:T(8,128)} %field_ref.1) | copy-start | bytes 393220
  26.3 8.4 %collective-permute-start.5 = (bf16[64,512]{1,0:T(8,128)(2,1)S(1)}, bf16[64,512]{1,0:T(8,128)(2,1)S(1)}, u32[]{:S(2)}, u32[]{:S(2)}) collective-permute-start(bf16[64,512]{1,0:T(8,128)(2,1)S(1)} %copy-done.55), channel_id=1, source_target_pairs={{0,32},{32,0},{1,33},{33,1},{2,34},{34,2},{3,35},{35,3},{4,36},{36... | collective-permute-start | bytes 196616 | tf_op jit(solution)/shard_map/ppermute | solution.py:47
  28.5 6.9 %collective-permute-start.6 = (bf16[64,512]{1,0:T(8,128)(2,1)S(1)}, bf16[64,512]{1,0:T(8,128)(2,1)S(1)}, u32[]{:S(2)}, u32[]{:S(2)}) collective-permute-start(bf16[64,512]{1,0:T(8,128)(2,1)S(1)} %copy-done.54), channel_id=1, source_target_pairs={{0,64},{64,0},{128,192},{192,128},{1,65},{65,1},{129,193},{193,129... | collective-permute-start | bytes 196616 | tf_op jit(solution)/shard_map/ppermute | solution.py:47
  29.9 6.2 %collective-permute-start.7 = (bf16[64,512]{1,0:T(8,128)(2,1)S(1)}, bf16[64,512]{1,0:T(8,128)(2,1)S(1)}, u32[]{:S(2)}, u32[]{:S(2)}) collective-permute-start(bf16[64,512]{1,0:T(8,128)(2,1)S(1)} %copy-done.53), channel_id=1, source_target_pairs={{0,128},{64,192},{128,0},{192,64},{1,129},{65,193},{129,1},{193,65... | collective-permute-start | bytes 196616 | tf_op jit(solution)/shard_map/ppermute | solution.py:47
  33.2 13.1 %collective-permute-start.10 = (bf16[8,64,512]{2,1,0:T(8,128)(2,1)}, bf16[8,64,512]{2,1,0:T(8,128)(2,1)S(1)}, u32[]{:S(2)}, u32[]{:S(2)}) collective-permute-start(bf16[8,64,512]{2,1,0:T(8,128)(2,1)} %get-tuple-element.76), channel_id=1, source_target_pairs={{0,3},{1,0},{2,1},{3,2},{4,7},{5,4},{6,5},{7,6},{8,11},{9,8},{10,9... | collective-permute-start | bytes 1572872 | tf_op jit(solution)/shard_map/ppermute | solution.py:43
  33.4 14.9 %collective-permute-start.8 = (bf16[8,64,512]{2,1,0:T(8,128)(2,1)}, bf16[8,64,512]{2,1,0:T(8,128)(2,1)S(1)}, u32[]{:S(2)}, u32[]{:S(2)}) collective-permute-start(bf16[8,64,512]{2,1,0:T(8,128)(2,1)} %get-tuple-element.74), channel_id=1, source_target_pairs={{0,1},{1,2},{2,3},{3,0},{4,5},{5,6},{6,7},{7,4},{8,9},{9,10},{10,1... | collective-permute-start | bytes 1572872 | tf_op jit(solution)/shard_map/ppermute | solution.py:43
  34.7 23.1 %collective-permute-start.9 = (bf16[8,64,512]{2,1,0:T(8,128)(2,1)S(1)}, bf16[8,64,512]{2,1,0:T(8,128)(2,1)S(1)}, u32[]{:S(2)}, u32[]{:S(2)}) collective-permute-start(bf16[8,64,512]{2,1,0:T(8,128)(2,1)S(1)} %copy-done.52), channel_id=1, source_target_pairs={{0,2},{1,3},{2,0},{3,1},{4,6},{5,7},{6,4},{7,5},{8,10},{9,11},{10,... | collective-permute-start | bytes 1572872 | tf_op jit(solution)/shard_map/ppermute | solution.py:43
  39.4 25.6 %all-to-all-start = ((bf16[8,64,576]{2,1,0:T(8,128)(2,1)}), bf16[8,64,576]{2,1,0:T(8,128)(2,1)S(1)}, u32[]{:S(2)}, u32[]{:S(2)}) async-start(bf16[8,64,576]{2,1,0:T(8,128)(2,1)} %get-tuple-element.81), calls=%async_computation | async-start | bytes 1310720 | tf_op jit(solution)/shard_map/all_to_all | solution.py:38
  46.3 11.5 %copy-start.22 = (bf16[8,64,512]{2,1,0:T(8,128)(2,1)}, bf16[8,64,512]{2,1,0:T(8,128)(2,1)S(1)}, u32[]{:S(2)}) copy-start(bf16[8,64,512]{2,1,0:T(8,128)(2,1)S(1)} %collective-permute-done.10.refs_3_) | copy-start | bytes 1572868
  61.7 5.9 %collective-permute-start.11 = (bf16[4,4,64,512]{3,2,1,0:T(8,128)(2,1)}, bf16[4,4,64,512]{3,2,1,0:T(8,128)(2,1)S(1)}, u32[]{:S(2)}, u32[]{:S(2)}) collective-permute-start(bf16[4,4,64,512]{3,2,1,0:T(8,128)(2,1)} %get-tuple-element.80), channel_id=1, source_target_pairs={{0,32},{32,0},{1,33},{33,1},{2,34},{34,2},{3,35},{35,3},{4,36},{36... | collective-permute-start | bytes 3145736 | tf_op jit(solution)/shard_map/ppermute | solution.py:43
  65.1 3.4 %collective-permute-start.12 = (bf16[8,64,576]{2,1,0:T(8,128)(2,1)S(1)}, bf16[8,64,576]{2,1,0:T(8,128)(2,1)S(1)}, u32[]{:S(2)}, u32[]{:S(2)}) collective-permute-start(bf16[8,64,576]{2,1,0:T(8,128)(2,1)S(1)} %all-to-all-done.near_ref.refs_3_), channel_id=1, source_target_pairs={{0,32},{32,0},{1,33},{33,1},{2,34},{34,2},{3,35},{35,3},{4,36},{36... | collective-permute-start | bytes 1769480 | tf_op jit(solution)/shard_map/ppermute | solution.py:43
  102.5 4.5 %collective-permute-start.13 = (bf16[64,576]{1,0:T(8,128)(2,1)}, bf16[64,576]{1,0:T(8,128)(2,1)S(1)}, u32[]{:S(2)}, u32[]{:S(2)}) collective-permute-start(bf16[64,576]{1,0:T(8,128)(2,1)} %get-tuple-element.86), channel_id=1, source_target_pairs={{0,1},{1,0},{2,3},{3,2},{4,5},{5,4},{6,7},{7,6},{8,9},{9,8},{10,11... | collective-permute-start | bytes 221192 | tf_op jit(solution)/shard_map/ppermute | solution.py:47
  102.6 7.1 %collective-permute-start.14 = (bf16[64,576]{1,0:T(8,128)(2,1)}, bf16[64,576]{1,0:T(8,128)(2,1)S(1)}, u32[]{:S(2)}, u32[]{:S(2)}) collective-permute-start(bf16[64,576]{1,0:T(8,128)(2,1)} %get-tuple-element.87), channel_id=1, source_target_pairs={{0,2},{1,3},{2,0},{3,1},{4,6},{5,7},{6,4},{7,5},{8,10},{9,11},{10,... | collective-permute-start | bytes 221192 | tf_op jit(solution)/shard_map/ppermute | solution.py:47
  103.7 6.5 %collective-permute-start.15 = (bf16[64,576]{1,0:T(8,128)(2,1)}, bf16[64,576]{1,0:T(8,128)(2,1)S(1)}, u32[]{:S(2)}, u32[]{:S(2)}) collective-permute-start(bf16[64,576]{1,0:T(8,128)(2,1)} %get-tuple-element.88), channel_id=1, source_target_pairs={{0,4},{4,0},{8,12},{12,8},{16,20},{20,16},{24,28},{28,24},{1,5},{5... | collective-permute-start | bytes 221192 | tf_op jit(solution)/shard_map/ppermute | solution.py:47
  104.4 8.1 %collective-permute-start.16 = (bf16[64,576]{1,0:T(8,128)(2,1)}, bf16[64,576]{1,0:T(8,128)(2,1)S(1)}, u32[]{:S(2)}, u32[]{:S(2)}) collective-permute-start(bf16[64,576]{1,0:T(8,128)(2,1)} %get-tuple-element.89), channel_id=1, source_target_pairs={{0,8},{4,12},{8,0},{12,4},{16,24},{20,28},{24,16},{28,20},{1,9},{5... | collective-permute-start | bytes 221192 | tf_op jit(solution)/shard_map/ppermute | solution.py:47
  105.6 7.9 %collective-permute-start.17 = (bf16[64,576]{1,0:T(8,128)(2,1)}, bf16[64,576]{1,0:T(8,128)(2,1)S(1)}, u32[]{:S(2)}, u32[]{:S(2)}) collective-permute-start(bf16[64,576]{1,0:T(8,128)(2,1)} %get-tuple-element.90), channel_id=1, source_target_pairs={{0,16},{4,20},{8,24},{12,28},{16,0},{20,4},{24,8},{28,12},{1,17},{... | collective-permute-start | bytes 221192 | tf_op jit(solution)/shard_map/ppermute | solution.py:47
  107.0 6.5 %collective-permute-start.18 = (bf16[64,576]{1,0:T(8,128)(2,1)}, bf16[64,576]{1,0:T(8,128)(2,1)S(1)}, u32[]{:S(2)}, u32[]{:S(2)}) collective-permute-start(bf16[64,576]{1,0:T(8,128)(2,1)} %get-tuple-element.91), channel_id=1, source_target_pairs={{0,32},{32,0},{1,33},{33,1},{2,34},{34,2},{3,35},{35,3},{4,36},{36... | collective-permute-start | bytes 221192 | tf_op jit(solution)/shard_map/ppermute | solution.py:47
  109.8 3.8 %collective-permute-start.19 = (bf16[64,576]{1,0:T(8,128)(2,1)}, bf16[64,576]{1,0:T(8,128)(2,1)S(1)}, u32[]{:S(2)}, u32[]{:S(2)}) collective-permute-start(bf16[64,576]{1,0:T(8,128)(2,1)} %get-tuple-element.92), channel_id=1, source_target_pairs={{0,64},{64,0},{128,192},{192,128},{1,65},{65,1},{129,193},{193,129... | collective-permute-start | bytes 221192 | tf_op jit(solution)/shard_map/ppermute | solution.py:47
  110.2 5.8 %collective-permute-start.20 = (bf16[64,576]{1,0:T(8,128)(2,1)}, bf16[64,576]{1,0:T(8,128)(2,1)S(1)}, u32[]{:S(2)}, u32[]{:S(2)}) collective-permute-start(bf16[64,576]{1,0:T(8,128)(2,1)} %get-tuple-element.93), channel_id=1, source_target_pairs={{0,128},{64,192},{128,0},{192,64},{1,129},{65,193},{129,1},{193,65... | collective-permute-start | bytes 221192 | tf_op jit(solution)/shard_map/ppermute | solution.py:47
  147.2 4.5 %collective-permute-start.21 = (bf16[8,72,640]{2,1,0:T(8,128)(2,1)S(1)}, bf16[8,72,640]{2,1,0:T(8,128)(2,1)S(1)}, u32[]{:S(2)}, u32[]{:S(2)}) collective-permute-start(bf16[8,72,640]{2,1,0:T(8,128)(2,1)S(1)} %all_to_all.41.near_ref.refs_1_), channel_id=1, source_target_pairs={{0,32},{32,0},{1,33},{33,1},{2,34},{34,2},{3,35},{35,3},{4,36},{36... | collective-permute-start | bytes 2211848 | tf_op jit(solution)/shard_map/ppermute | solution.py:43
  159.4 32.9 %all-to-all-start.3 = ((bf16[16,88,576]{2,1,0:T(8,128)(2,1)}), bf16[16,88,576]{2,1,0:T(8,128)(2,1)S(1)}, u32[]{:S(2)}, u32[]{:S(2)}) async-start(bf16[16,88,576]{2,1,0:T(8,128)(2,1)} %get-tuple-element.96), calls=%async_computation.3 | async-start | bytes 3604480 | tf_op jit(solution)/shard_map/all_to_all | solution.py:38
  197.4 43.2 %copy-start.20 = (f32[64,64]{1,0:T(8,128)S(1)}, f32[64,64]{1,0:T(8,128)}, u32[]{:S(2)}) copy-start(f32[64,64]{1,0:T(8,128)} %slice.102.refs_8_) | copy-start | bytes 49156
  197.4 43.2 %copy-start.10 = (f32[64,576]{1,0:T(8,128)S(1)}, f32[64,576]{1,0:T(8,128)}, u32[]{:S(2)}) copy-start(f32[64,576]{1,0:T(8,128)} %get-tuple-element.94.field_ref) | copy-start | bytes 442372
  197.4 43.4 %copy-start.19 = (f32[64,64]{1,0:T(8,128)S(1)}, f32[64,64]{1,0:T(8,128)}, u32[]{:S(2)}) copy-start(f32[64,64]{1,0:T(8,128)} %slice.104.refs_8_) | copy-start | bytes 49156
  197.4 43.5 %copy-start.50 = (f32[64,64]{1,0:T(8,128)S(1)}, f32[64,64]{1,0:T(8,128)}, u32[]{:S(2)}) copy-start(f32[64,64]{1,0:T(8,128)} %get-tuple-element.98) | copy-start | bytes 49156
  197.4 3.4 %collective-permute-start.22 = (bf16[64,512]{1,0:T(8,128)(2,1)}, bf16[64,512]{1,0:T(8,128)(2,1)S(1)}, u32[]{:S(2)}, u32[]{:S(2)}) collective-permute-start(bf16[64,512]{1,0:T(8,128)(2,1)} %get-tuple-element.101), channel_id=1, source_target_pairs={{0,1},{1,0},{2,3},{3,2},{4,5},{5,4},{6,7},{7,6},{8,9},{9,8},{10,11... | collective-permute-start | bytes 196616 | tf_op jit(solution)/shard_map/ppermute | solution.py:47
  197.5 5.9 %collective-permute-start.23 = (bf16[64,512]{1,0:T(8,128)(2,1)}, bf16[64,512]{1,0:T(8,128)(2,1)S(1)}, u32[]{:S(2)}, u32[]{:S(2)}) collective-permute-start(bf16[64,512]{1,0:T(8,128)(2,1)} %get-tuple-element.102), channel_id=1, source_target_pairs={{0,2},{1,3},{2,0},{3,1},{4,6},{5,7},{6,4},{7,5},{8,10},{9,11},{10,... | collective-permute-start | bytes 196616 | tf_op jit(solution)/shard_map/ppermute | solution.py:47
  197.7 6.0 %collective-permute-start.24 = (bf16[64,512]{1,0:T(8,128)(2,1)}, bf16[64,512]{1,0:T(8,128)(2,1)S(1)}, u32[]{:S(2)}, u32[]{:S(2)}) collective-permute-start(bf16[64,512]{1,0:T(8,128)(2,1)} %get-tuple-element.103), channel_id=1, source_target_pairs={{0,4},{4,0},{8,12},{12,8},{16,20},{20,16},{24,28},{28,24},{1,5},{5... | collective-permute-start | bytes 196616 | tf_op jit(solution)/shard_map/ppermute | solution.py:47
  198.0 8.8 %collective-permute-start.25 = (bf16[64,512]{1,0:T(8,128)(2,1)}, bf16[64,512]{1,0:T(8,128)(2,1)S(1)}, u32[]{:S(2)}, u32[]{:S(2)}) collective-permute-start(bf16[64,512]{1,0:T(8,128)(2,1)} %get-tuple-element.104), channel_id=1, source_target_pairs={{0,8},{4,12},{8,0},{12,4},{16,24},{20,28},{24,16},{28,20},{1,9},{5... | collective-permute-start | bytes 196616 | tf_op jit(solution)/shard_map/ppermute | solution.py:47
  198.1 8.7 %collective-permute-start.26 = (bf16[64,512]{1,0:T(8,128)(2,1)}, bf16[64,512]{1,0:T(8,128)(2,1)S(1)}, u32[]{:S(2)}, u32[]{:S(2)}) collective-permute-start(bf16[64,512]{1,0:T(8,128)(2,1)} %get-tuple-element.105), channel_id=1, source_target_pairs={{0,16},{4,20},{8,24},{12,28},{16,0},{20,4},{24,8},{28,12},{1,17},{... | collective-permute-start | bytes 196616 | tf_op jit(solution)/shard_map/ppermute | solution.py:47
  200.8 6.0 %collective-permute-start.27 = (bf16[64,512]{1,0:T(8,128)(2,1)}, bf16[64,512]{1,0:T(8,128)(2,1)S(1)}, u32[]{:S(2)}, u32[]{:S(2)}) collective-permute-start(bf16[64,512]{1,0:T(8,128)(2,1)} %get-tuple-element.106), channel_id=1, source_target_pairs={{0,32},{32,0},{1,33},{33,1},{2,34},{34,2},{3,35},{35,3},{4,36},{36... | collective-permute-start | bytes 196616 | tf_op jit(solution)/shard_map/ppermute | solution.py:47
  203.5 3.6 %collective-permute-start.28 = (bf16[64,512]{1,0:T(8,128)(2,1)}, bf16[64,512]{1,0:T(8,128)(2,1)S(1)}, u32[]{:S(2)}, u32[]{:S(2)}) collective-permute-start(bf16[64,512]{1,0:T(8,128)(2,1)} %get-tuple-element.107), channel_id=1, source_target_pairs={{0,64},{64,0},{128,192},{192,128},{1,65},{65,1},{129,193},{193,129... | collective-permute-start | bytes 196616 | tf_op jit(solution)/shard_map/ppermute | solution.py:47
  203.8 4.9 %collective-permute-start.29 = (bf16[64,512]{1,0:T(8,128)(2,1)}, bf16[64,512]{1,0:T(8,128)(2,1)S(1)}, u32[]{:S(2)}, u32[]{:S(2)}) collective-permute-start(bf16[64,512]{1,0:T(8,128)(2,1)} %get-tuple-element.108), channel_id=1, source_target_pairs={{0,128},{64,192},{128,0},{192,64},{1,129},{65,193},{129,1},{193,65... | collective-permute-start | bytes 196616 | tf_op jit(solution)/shard_map/ppermute | solution.py:47
  237.9 4.5 %collective-permute-start.30 = (bf16[8,88,512]{2,1,0:T(8,128)(2,1)S(1)}, bf16[8,88,512]{2,1,0:T(8,128)(2,1)S(1)}, u32[]{:S(2)}, u32[]{:S(2)}) collective-permute-start(bf16[8,88,512]{2,1,0:T(8,128)(2,1)S(1)} %all_to_all.42.near_ref), channel_id=1, source_target_pairs={{0,32},{32,0},{1,33},{33,1},{2,34},{34,2},{3,35},{35,3},{4,36},{36... | collective-permute-start | bytes 2162696 | tf_op jit(solution)/shard_map/ppermute | solution.py:43
  249.8 22.0 %all-to-all-start.5 = ((bf16[16,64,512]{2,1,0:T(8,128)(2,1)}), bf16[16,64,512]{2,1,0:T(8,128)(2,1)S(1)}, u32[]{:S(2)}, u32[]{:S(2)}) async-start(bf16[16,64,512]{2,1,0:T(8,128)(2,1)} %get-tuple-element.114), calls=%async_computation.5 | async-start | bytes 2097152 | tf_op jit(solution)/shard_map/all_to_all | solution.py:38
  256.4 18.8 %copy-start.11 = (f32[64,576]{1,0:T(8,128)S(1)}, f32[64,576]{1,0:T(8,128)}, u32[]{:S(2)}) copy-start(f32[64,576]{1,0:T(8,128)} %get-tuple-element.85.field_ref) | copy-start | bytes 442372
  256.4 18.8 %copy-start.14 = (f32[64,512]{1,0:T(8,128)S(1)}, f32[64,512]{1,0:T(8,128)}, u32[]{:S(2)}) copy-start(f32[64,512]{1,0:T(8,128)} %get-tuple-element.100.field_ref) | copy-start | bytes 393220
  256.4 18.8 %copy-start.15 = (f32[64,512]{1,0:T(8,128)S(1)}, f32[64,512]{1,0:T(8,128)}, u32[]{:S(2)}) copy-start(f32[64,512]{1,0:T(8,128)} %get-tuple-element.113.field_ref) | copy-start | bytes 393220
  256.4 18.8 %copy-start.18 = (f32[64,576]{1,0:T(8,128)S(1)}, f32[64,576]{1,0:T(8,128)}, u32[]{:S(2)}) copy-start(f32[64,576]{1,0:T(8,128)} %get-tuple-element.72.field_ref) | copy-start | bytes 442372
  275.2 27.1 %copy-start.51 = (s32[512]{0:T(512)S(1)}, s32[512]{0:T(512)}, u32[]{:S(2)}) copy-start(s32[512]{0:T(512)} %param.15) | copy-start | bytes 6148
  275.3 27.2 %copy-start.16 = (f32[64,512]{1,0:T(8,128)S(1)}, f32[64,512]{1,0:T(8,128)}, u32[]{:S(2)}) copy-start(f32[64,512]{1,0:T(8,128)} %shard_map.103) | copy-start | bytes 393220
  (44 other events, 151.8 us)
